TPU v7x, 32 devices: a whole 2x2x4 slice. The times are simulated.
32 devices in a mesh: dp: 4 (over z), seq: 8 (over y, x, core).
Axes of the slice: x: 2, y: 2, z: 4, core: 2. Of those that a mesh axis runs over, the one named last changes fastest.
Arguments:
- tokens: bfloat16 [4, 2048, 1536], P('dp', 'seq'), may hold values from -6 to 6
- cotangent: bfloat16 [4, 2048, 1536], P('dp', 'seq'), may hold values from -6 to 6
- in_weight: bfloat16 [1536, 6448], P(('dp', 'seq')), may hold values from -0.15625 to 0.15625
- out_weight: bfloat16 [3072, 1536], P(('dp', 'seq')), may hold values from -0.109375 to 0.109375
- conv_weight: bfloat16 [3328, 4], P(('dp', 'seq')), may hold values from -3 to 3
- conv_bias: bfloat16 [3328], P(('dp', 'seq')), may hold values from -0.5 to 0.5
- norm_gain: bfloat16 [1536], P(('dp', 'seq')), may hold values from 0.5 to 1.5
- gate_gain: bfloat16 [3072], P(('dp', 'seq')), may hold values from 0.5 to 1.5
- decay_rate: float32 [48], replicated, may hold values from 0.00012207031 to 0.08
- dt_bias: float32 [48], replicated, may hold values from -2 to 0.5
- d_skip: float32 [48], replicated, may hold values from 0.5 to 2
Outputs:
- block_out: bfloat16 [4, 2048, 1536], P('dp', 'seq')
- grad_input: float32 [4, 2048, 1536], P('dp', 'seq')
- grad_inproj: float32 [1536, 6448], P(('dp', 'seq'))
- grad_outproj: float32 [3072, 1536], P(('dp', 'seq'))
- grad_convw: float32 [3328, 4], P(('dp', 'seq'))
- grad_convb: float32 [3328], P(('dp', 'seq'))
- grad_normgain: float32 [1536], P(('dp', 'seq'))
- grad_gategain: float32 [3072], P(('dp', 'seq'))
- grad_rate: float32 [48], replicated
- grad_dtbias: float32 [48], replicated
- grad_skip: float32 [48], replicated
All inputs are finite; a program needn't handle non-finite values.
Results may differ from a plain program's by a relative error of at most 0.0077.
Values may be sent and summed in bfloat16 or wider, within the bound.
A program may use at most 192 MiB of HBM per device.

v0:
```python
from functools import partial

import jax
import jax.numpy as jnp
from jax import lax
from jax.sharding import PartitionSpec as P

DIN = 3072
HDIM = 64
NSTATE = 128
CONVK = 4
BLOCK = 256
HEADS = 48
CONVCH = 3328


epsilon = 1e-05
highest = lax.Precision.HIGHEST


def from_behind(block, axis, distance):
    devices = range(lax.axis_size(axis))
    route = [(i - distance, i) for i in devices if i - distance in devices]
    return lax.ppermute(block, axis, route)


def entering(array, axis, combine, identity):
    devices, position = (lax.axis_size(axis), lax.axis_index(axis))
    everything = jax.tree.map(
        lambda part, kind: lax.all_gather(part.astype(kind), axis),
        array,
        (jnp.bfloat16, jnp.bfloat16),
    )
    start = jax.tree.map(
        lambda part, zero: jnp.broadcast_to(jnp.asarray(zero, part.dtype), part.shape),
        array,
        identity,
    )

    def entering_hop(k, before):
        reached = k < position
        new = combine(
            before, jax.tree.map(lambda part, own: part[k].astype(own.dtype), everything, array)
        )
        return jax.tree.map(lambda a, b: jnp.where(reached, a, b), new, before)

    return lax.fori_loop(0, devices, entering_hop, start)


def carried_in(array, axis, combine, identity):
    devices, position = (lax.axis_size(axis), lax.axis_index(axis))
    everything = jax.tree.map(
        lambda part, kind: lax.all_gather(part.astype(kind), axis),
        array,
        jax.tree.map(lambda a: jnp.bfloat16 if a.dtype == jnp.float32 else a.dtype, array),
    )
    start = jax.tree.map(
        lambda part, zero: jnp.broadcast_to(jnp.asarray(zero, part.dtype), part.shape),
        array,
        identity,
    )

    def carried_hop(k, before):
        at = devices - 1 - k
        reached = at > position
        new = combine(
            before, jax.tree.map(lambda part, own: part[at].astype(own.dtype), everything, array)
        )
        return jax.tree.map(lambda a, b: jnp.where(reached, a, b), new, before)

    return lax.fori_loop(0, devices, carried_hop, start)


def rms_scale(values, gain):
    mean_sq = jnp.mean(values * values, axis=-1, keepdims=True)
    return values * lax.rsqrt(mean_sq + epsilon) * gain


def gate_norm(gate_part, mixed, gain):
    return rms_scale(mixed * jax.nn.silu(gate_part), gain)


def block_step(rate_in, state_now, pieces):
    x_heads, b_proj, c_proj, step_dt = pieces
    width = x_heads.shape[0]
    cumul = jnp.cumsum(step_dt * -rate_in, axis=0)
    cumul_h = cumul.T
    log_gaps = cumul_h[:, :, None] - cumul_h[:, None, :]
    causal = jnp.arange(width)[:, None] >= jnp.arange(width)[None, :]
    decay = jnp.exp(jnp.where(causal[None], log_gaps, -1e30))
    scores = jnp.einsum("tn,sn->ts", c_proj, b_proj, precision=highest)
    weighted = decay * scores[None] * step_dt.T[:, None, :]
    inner_part = jnp.einsum("hts,shp->thp", weighted, x_heads, precision=highest)
    carried = (
        jnp.einsum("hpn,tn->thp", state_now, c_proj, precision=highest) * jnp.exp(cumul)[:, :, None]
    )
    tail_weight = jnp.exp(cumul[-1][None, :] - cumul) * step_dt
    state_new = state_now * jnp.exp(cumul[-1])[:, None, None] + jnp.einsum(
        "shp,sn->hpn", x_heads * tail_weight[:, :, None], b_proj, precision=highest
    )
    return (state_new, inner_part + carried)


def ssd_blocks(x_heads, b_proj, c_proj, step_dt, rate_in, start_state):
    length = x_heads.shape[0]
    blocks = length // BLOCK
    pieces = (
        x_heads.reshape(blocks, BLOCK, HEADS, HDIM),
        b_proj.reshape(blocks, BLOCK, NSTATE),
        c_proj.reshape(blocks, BLOCK, NSTATE),
        step_dt.reshape(blocks, BLOCK, HEADS),
    )
    stepper = jax.checkpoint(partial(block_step, rate_in))
    end_state, results = lax.scan(stepper, start_state, pieces)
    return (results.reshape(length, HEADS, HDIM), end_state)


def prepare(padded, conv_w, conv_b, dt_raw, bias_in):
    length = dt_raw.shape[0]
    filtered = conv_b
    for offset in range(CONVK):
        filtered = filtered + padded[offset : offset + length] * conv_w[:, offset]
    activated = jax.nn.silu(filtered)
    x_heads = activated[:, :DIN].reshape(length, HEADS, HDIM)
    b_proj = activated[:, DIN : DIN + NSTATE]
    c_proj = activated[:, DIN + NSTATE :]
    step_dt = jax.nn.softplus(dt_raw + bias_in)
    return (x_heads, b_proj, c_proj, step_dt)


def mix_heads(padded, conv_w, conv_b, dt_raw, rate_in, bias_in, skip_in, start_state):
    x_heads, b_proj, c_proj, step_dt = prepare(padded, conv_w, conv_b, dt_raw, bias_in)
    results, end_state = ssd_blocks(x_heads, b_proj, c_proj, step_dt, rate_in, start_state)
    mixed = results + skip_in[:, None] * x_heads
    return (mixed.reshape(dt_raw.shape[0], DIN), end_state)


def combine(earlier, later_part):
    return (
        earlier[0] + later_part[0],
        earlier[1] * jnp.exp(later_part[0])[:, None, None] + later_part[1],
    )


def per_device(
    tokens,
    cotangent,
    in_weight,
    out_weight,
    conv_weight,
    conv_bias,
    norm_gain,
    gate_gain,
    decay_rate,
    dt_bias,
    d_skip,
):
    seq_x = tokens[0]
    cot_rows = cotangent[0]
    length = seq_x.shape[0]
    margin = CONVK - 1
    in_full, out_full, convw_full, convb_full, gain_norm, gain_gate = (
        lax.all_gather(in_weight, ("dp", "seq"), axis=0, tiled=True),
        lax.all_gather(out_weight, ("dp", "seq"), axis=0, tiled=True),
        lax.all_gather(conv_weight, ("dp", "seq"), axis=0, tiled=True),
        lax.all_gather(conv_bias, ("dp", "seq"), axis=0, tiled=True),
        lax.all_gather(norm_gain, ("dp", "seq"), axis=0, tiled=True),
        lax.all_gather(gate_gain, ("dp", "seq"), axis=0, tiled=True),
    )
    x_float = seq_x.astype(jnp.float32)
    normed = rms_scale(x_float, gain_norm.astype(jnp.float32)).astype(jnp.bfloat16)
    projected = jnp.dot(normed, in_full, preferred_element_type=jnp.float32).astype(jnp.bfloat16)
    gate_part = projected[:, :DIN].astype(jnp.float32)
    conv_rows = projected[:, DIN : DIN + CONVCH]
    prev_rim = from_behind(conv_rows[length - margin :], "seq", 1)
    padded = jnp.concatenate([prev_rim, conv_rows], axis=0).astype(jnp.float32)
    dt_raw = projected[:, DIN + CONVCH :].astype(jnp.float32)
    x_heads, b_proj, c_proj, step_dt = prepare(
        padded, convw_full.astype(jnp.float32), convb_full.astype(jnp.float32), dt_raw, dt_bias
    )
    zero_state = jnp.zeros((HEADS, HDIM, NSTATE), jnp.float32)
    local_y, local_end = ssd_blocks(x_heads, b_proj, c_proj, step_dt, decay_rate, zero_state)
    log_decay = jnp.cumsum(step_dt * -decay_rate, axis=0)
    decay_total = log_decay[-1]
    identity = (jnp.zeros_like(decay_total), zero_state)
    prefix = entering((decay_total, local_end), "seq", combine, identity)
    start_state = prefix[1]
    carried = (
        jnp.einsum("hpn,tn->thp", start_state, c_proj, precision=highest)
        * jnp.exp(log_decay)[:, :, None]
    )
    mixed = (local_y + carried + d_skip[:, None] * x_heads).reshape(length, DIN)
    gated = gate_norm(gate_part, mixed, gain_gate.astype(jnp.float32)).astype(jnp.bfloat16)
    block_out = (x_float + jnp.dot(gated, out_full, preferred_element_type=jnp.float32)).astype(
        jnp.bfloat16
    )
    in_back, out_back, convw_back, convb_back, norm_back_gain, gate_back_gain = (
        lax.all_gather(in_weight, ("dp", "seq"), axis=0, tiled=True),
        lax.all_gather(out_weight, ("dp", "seq"), axis=0, tiled=True),
        lax.all_gather(conv_weight, ("dp", "seq"), axis=0, tiled=True),
        lax.all_gather(conv_bias, ("dp", "seq"), axis=0, tiled=True),
        lax.all_gather(norm_gain, ("dp", "seq"), axis=0, tiled=True),
        lax.all_gather(gate_gain, ("dp", "seq"), axis=0, tiled=True),
    )
    d_w_out = lax.dot_general(
        gated, cot_rows, (((0,), (0,)), ((), ())), preferred_element_type=jnp.float32
    )
    d_gated = lax.dot_general(
        cot_rows, out_back, (((1,), (1,)), ((), ())), preferred_element_type=jnp.float32
    )
    _, gated_back = jax.vjp(gate_norm, gate_part, mixed, gate_back_gain.astype(jnp.float32))
    d_gate, d_mixed, d_g2 = gated_back(d_gated)
    d_heads = d_mixed.reshape(length, HEADS, HDIM) * jnp.exp(log_decay)[:, :, None]
    local_grad = jnp.einsum("thp,tn->hpn", d_heads, c_proj, precision=highest)
    suffix = carried_in((decay_total, local_grad), "seq", combine, identity)
    end_grad = suffix[1]
    mixer_fn = partial(mix_heads, start_state=start_state)
    _, mixer_back = jax.vjp(
        mixer_fn,
        padded,
        convw_back.astype(jnp.float32),
        convb_back.astype(jnp.float32),
        dt_raw,
        decay_rate,
        dt_bias,
        d_skip,
    )
    d_pad, d_cw, d_cb, d_raw, d_rate, d_bias, d_skp = mixer_back((d_mixed, end_grad))
    back_rim = from_behind(d_pad[:margin].astype(jnp.bfloat16), "seq", -1).astype(jnp.float32)
    d_conv_in = d_pad[margin:].at[length - margin :].add(back_rim)
    d_proj = jnp.concatenate([d_gate, d_conv_in, d_raw], axis=1).astype(jnp.bfloat16)
    d_w_in = lax.dot_general(
        normed, d_proj, (((0,), (0,)), ((), ())), preferred_element_type=jnp.float32
    )
    d_normed = lax.dot_general(
        d_proj, in_back, (((1,), (1,)), ((), ())), preferred_element_type=jnp.float32
    )
    _, norm_back = jax.vjp(rms_scale, x_float, norm_back_gain.astype(jnp.float32))
    d_xn, d_g1 = norm_back(d_normed)
    grad_x = cot_rows.astype(jnp.float32) + d_xn
    sum_inproj, sum_outproj, sum_convw, sum_convb, sum_normgain, sum_gategain = (
        lax.psum_scatter(d_w_in, ("dp", "seq"), scatter_dimension=0, tiled=True),
        lax.psum_scatter(d_w_out, ("dp", "seq"), scatter_dimension=0, tiled=True),
        lax.psum_scatter(d_cw, ("dp", "seq"), scatter_dimension=0, tiled=True),
        lax.psum_scatter(d_cb, ("dp", "seq"), scatter_dimension=0, tiled=True),
        lax.psum_scatter(d_g1, ("dp", "seq"), scatter_dimension=0, tiled=True),
        lax.psum_scatter(d_g2, ("dp", "seq"), scatter_dimension=0, tiled=True),
    )
    head_sums = lax.psum((d_rate, d_bias, d_skp), ("dp", "seq"))
    return (
        block_out[None],
        grad_x[None],
        sum_inproj,
        sum_outproj,
        sum_convw,
        sum_convb,
        sum_normgain,
        sum_gategain,
        head_sums[0],
        head_sums[1],
        head_sums[2],
    )


def solution(mesh):
    return jax.shard_map(
        per_device,
        mesh=mesh,
        in_specs=(
            P("dp", "seq", None),
            P("dp", "seq", None),
            P(("dp", "seq"), None),
            P(("dp", "seq"), None),
            P(("dp", "seq"), None),
            P(("dp", "seq")),
            P(("dp", "seq")),
            P(("dp", "seq")),
            P(),
            P(),
            P(),
        ),
        out_specs=(
            P("dp", "seq", None),
            P("dp", "seq", None),
            P(("dp", "seq"), None),
            P(("dp", "seq"), None),
            P(("dp", "seq"), None),
            P(("dp", "seq")),
            P(("dp", "seq")),
            P(("dp", "seq")),
            P(),
            P(),
            P(),
        ),
        check_vma=False,
    )
```

profile of v0, /device:TPU:0, one launch (start us, length us, event | category | flops | bytes accessed | tf_op | source)
XLA Modules:
  0.0 1281.0 jit_solution(13721000566881739272)
XLA Ops:
  8.0 44.2 %all-gather.2 = bf16[32,104,4]{1,2,0:T(4,128)(2,1)S(1)} all-gather(bf16[1,104,4]{1,2,0:T(4,128)(2,1)} %bitcast.194), channel_id=1, replica_groups=mesh['dp'=4,'seq'=8] {'dp','seq'}, dimensions={0}, use_global_device_ids=true | all-gather | bytes 27456 | tf_op jit(solution)/shard_map/all_gather | solution.py:165
  54.9 39.6 %all-reduce.21 = (bf16[1536]{0:T(1024)(128)(2,1)S(1)}, bf16[3328]{0:T(1024)(128)(2,1)S(1)}, bf16[3072]{0:T(1024)(128)(2,1)}) all-reduce(bf16[1536]{0:T(1024)(128)(2,1)S(1)} %dynamic-update-slice.4, bf16[3328]{0:T(1024)(128)(2,1)S(1)} %dynamic-update-slice.3, ...), channel_id=1, replica_groups=mesh['dp'=4,'seq'=8] {'dp','seq'}, use_global_device_ids=true, to_apply=%add.14 | all-reduce | flops 7936 | bytes 31744
  97.9 47.3 %all-gather.9.cloned.1.call-done = bf16[1536,6448]{1,0:T(8,128)(2,1)} async-done(((bf16[48,6448]{1,0:T(8,128)(2,1)}), bf16[1536,6448]{1,0:T(8,128)(2,1)}) %all-gather.9.cloned.1.call-update) | async-done | bytes 19808272 | tf_op jit(solution)/shard_map/all_gather | solution.py:163
  145.2 12.7 convolution_convert_fusion
  170.9 4.1 fusion.28
  178.7 3.6 copy.168
  182.3 5.4 add_convert_fusion
  190.5 8.7 all-gather.3
  206.6 5.2 fusion.87
  211.9 20.2 %all-gather.13.cloned.1.call-done = bf16[384,64,128]{2,1,0:T(8,128)(2,1)} async-done(((bf16[48,64,128]{2,1,0:T(8,128)(2,1)}), bf16[384,64,128]{2,1,0:T(8,128)(2,1)}) %all-gather.13.cloned.1.call-update) | async-done | bytes 6291472 | tf_op jit(solution)/shard_map/all_gather | solution.py:30
  232.1 33.9 %while.21 = (s32[]{:T(128)}, f32[48,64,128]{2,1,0:T(8,128)}, s32[]{:T(128)}, bf16[8,48]{1,0:T(8,128)(2,1)}, bf16[8,48,64,128]{3,2,1,0:T(8,128)(2,1)}, /*index=5*/s32[]{:T(128)}, s32[]{:T(128)}) while((s32[]{:T(128)}, f32[48,64,128]{2,1,0:T(8,128)}, s32[]{:T(128)}, bf16[8,48]{1,0:T(8,128)(2,1)}, bf16[8,48,64,128]{3,2,1,0:T(8,128)(2,1)}, ...), condition=%wide.region_4.5_spmd.clone, body=%wide.region_3.4_spmd.clone.sunk | while | flops 1966132 | bytes 3932753 | solution.py:47
  237.0 3.1 fusion.147
  241.3 3.2 fusion.147
  245.7 3.1 fusion.147
  266.1 4.3 fusion.101
  270.5 17.0 %fusion.39 = f32[256,48,64]{0,2,1:T(8,128)} fusion(f32[256,48,64]{0,2,1:T(8,128)S(1)} %bitcast.170, f32[256,48,64]{0,2,1:T(8,128)S(1)} %fusion.101, f32[256,48,64]{0,2,1:T(8,128)} %fusion.87, f32[48,256]{1,0:T(8,128)S(1)} %copy-done.45, f32[256,256]{1,0:T(8,128)S(1)} %copy-done.27, f32[48,256]{1,0:T(8,128)S(1)} %copy-done.46, ...), kind=kOutput, calls=%fused_computation.63 | convolution fusion | flops 2433220608 | bytes 13058240 | tf_op jit(solution)/shard_map/while/body/eval_jaxpr/checkpoint/hts,shp->thp/dot_general | solution.py:93
  287.5 3.6 copy.176
  291.1 5.1 multiply_reduce_fusion.11
  297.3 19.2 %all-gather.11.cloned.1.call-done = bf16[3072,1536]{1,0:T(8,128)(2,1)} async-done(((bf16[96,1536]{1,0:T(8,128)(2,1)}), bf16[3072,1536]{1,0:T(8,128)(2,1)}) %all-gather.11.cloned.1.call-update) | async-done | bytes 9437200 | tf_op jit(solution)/shard_map/all_gather | solution.py:164
  316.6 8.4 multiply_reduce_fusion.7
  325.0 5.7 multiply_reduce_fusion.6
  330.7 3.7 copy.178
  334.4 5.4 fusion.71
  347.1 36.8 %all-gather.15.cloned.1.call-done = bf16[384,64,128]{2,1,0:T(8,128)(2,1)} async-done(((bf16[48,64,128]{2,1,0:T(8,128)(2,1)}), bf16[384,64,128]{2,1,0:T(8,128)(2,1)}) %all-gather.15.cloned.1.call-update) | async-done | bytes 6291472 | tf_op jit(solution)/shard_map/all_gather | solution.py:53
  383.9 34.2 %while.22 = (s32[]{:T(128)}, f32[48,64,128]{2,1,0:T(8,128)}, s32[]{:T(128)}, bf16[8,48]{1,0:T(8,128)(2,1)}, bf16[8,48,64,128]{3,2,1,0:T(8,128)(2,1)}, /*index=5*/s32[]{:T(128)}, s32[]{:T(128)}, s32[]{:T(128)}, s32[]{:T(128)}) while((s32[]{:T(128)}, f32[48,64,128]{2,1,0:T(8,128)}, s32[]{:T(128)}, bf16[8,48]{1,0:T(8,128)(2,1)}, ...), condition=%wide.region_8.9_spmd.clone, body=%wide.region_7.8_spmd.clone.sunk | while | flops 1966136 | bytes 3932815 | solution.py:71
  388.9 3.1 fusion.148
  393.3 3.1 fusion.148
  397.6 3.1 fusion.148
  401.9 3.2 fusion.148
  406.3 3.1 fusion.148
  410.7 3.1 fusion.148
  415.0 3.1 fusion.148
  435.7 5.8 multiply_reduce_fusion.8
  442.4 4.9 multiply_reduce_fusion.9
  447.4 19.6 %fusion.13 = (f32[48,256]{1,0:T(8,128)}, f32[48,256]{1,0:T(8,128)}, f32[48,256]{1,0:T(8,128)}, f32[256,256]{1,0:T(8,128)}) fusion(f32[256,256]{1,0:T(8,128)S(1)} %fusion.127, f32[48,256]{1,0:T(8,128)S(1)} %copy-done.41, f32[48,256]{1,0:T(8,128)S(1)} %copy-done.43, pred[256,256]{1,0:T(8,128)(4,1)S(1)} %copy-done.38, f32[256,48,64]{0,2,1:T(8,128)S(1)} %bitcast.172, ...), kind=kOutput, calls=%fused_computation.21 | convolution fusion | flops 2456711168 | bytes 7127040 | tf_op jit(solution)/shard_map/transpose(jvp())/while/body/eval_jaxpr/checkpoint/hts,shp->thp/dot_general | solution.py:93
  478.9 4.0 reduce-window.36
  492.6 8.2 fusion.79
  500.9 13.4 %bitcast_add_fusion = f32[256,48,64]{0,2,1:T(8,128)} fusion(f32[256,48,64]{0,2,1:T(8,128)} %get-tuple-element.467, f32[256,256]{1,0:T(8,128)S(1)} %copy-done.26, f32[48,256]{1,0:T(8,128)S(1)} %copy-done.42, f32[48,256]{1,0:T(8,128)S(1)} %copy-done.44, pred[256,256]{1,0:T(8,128)(4,1)S(1)} %copy-done.39, f32[256,48,64]{0,2,1:T(8,128)S(1)} %bitcast.177, ...), kind=kOutput, calls=%fused_computation.57 | convolution fusion | flops 2430074880 | bytes 9912320 | tf_op jit(solution)/shard_map/transpose(jvp())/while/body/eval_jaxpr/checkpoint/hts,shp->thp/dot_general | solution.py:93
  514.3 3.9 copy.186
  522.5 7.6 fusion.76
  534.0 4.1 multiply_reduce_fusion.5
  545.1 12.4 fusion.59
  557.6 9.0 fusion.83
  566.7 17.9 %fusion.74 = f32[1536,6448]{1,0:T(8,128)} fusion(bf16[256,48]{1,0:T(8,128)(2,1)S(1)} %copy-done.24, bf16[256,3328]{1,0:T(8,128)(2,1)} %copy-done.15, bf16[256,3072]{1,0:T(8,128)(2,1)} %get-tuple-element.448, bf16[1,256,1536]{2,1,0:T(8,128)(2,1)} %param.17, f32[1536]{0:T(1024)S(1)} %convert_element_type.115, f32[256]{0:T(256)S(1)} %fusion.105), kind=kOutput, calls=%fused_computation.109 | convolution fusion | flops 5082390528 | bytes 43711488 | tf_op jit(solution)/shard_map/dot_general | solution.py:232
  584.6 7.6 fusion.49
  593.9 92.3 %all-reduce.24.cloned.1.call-done = (f32[3328,4]{0,1:T(4,128)}, f32[3328]{0:T(1024)}, f32[1536]{0:T(1024)}, f32[3072]{0:T(1024)}, f32[48]{0:T(128)}, /*index=5*/f32[48]{0:T(128)}, f32[48]{0:T(128)}) async-done(((f32[3328,4]{0,1:T(4,128)}, f32[3328]{0:T(1024)}, f32[1536]{0:T(1024)}, f32[3072]{0:T(1024)}, f32[48]{0:T(128)}, /*index=5*/f32[48]{0:T(128)}, f32[48]{0:T(128)}), (f32[3328,4]{0,1:T(4,128)}, ...) | async-done | bytes 85584
  691.3 209.4 %reduce-scatter.6.cloned.1.call-done = f32[96,1536]{1,0:T(8,128)} async-done(((f32[3072,1536]{1,0:T(8,128)}), f32[96,1536]{1,0:T(8,128)}) %reduce-scatter.6.cloned.1.call-update) | async-done | bytes 589840 | tf_op jit(solution)/shard_map/reduce_scatter | solution.py:243
  900.8 369.8 %reduce-scatter.4.cloned.1.call-done = f32[48,6448]{1,0:T(8,128)} async-done(((f32[1536,6448]{1,0:T(8,128)}), f32[48,6448]{1,0:T(8,128)}) %reduce-scatter.4.cloned.1.call-update) | async-done | bytes 1238032 | tf_op jit(solution)/shard_map/reduce_scatter | solution.py:242
  (255 shorter events, 144.3 us)
Async XLA Ops:
  7.2 138.0 %all-gather.9.cloned.1.call-start = ((), (), s32[]{:S(2)}) async-start(), calls=%async_computation.2 | async-start | bytes 20680704 | tf_op jit(solution)/shard_map/all_gather | solution.py:163
  7.9 224.1 %all-gather.13.cloned.1.call-start = ((), (), s32[]{:S(2)}) async-start(), calls=%async_computation.6 | async-start | bytes 7077888 | tf_op jit(solution)/shard_map/all_gather | solution.py:30
  97.9 60.1 %copy-start.49 = (f32[256]{0:T(256)}, f32[256]{0:T(256)S(1)}, u32[]{:S(2)}) copy-start(f32[256]{0:T(256)S(1)} %fusion.62) | copy-start | bytes 3076
  97.9 62.8 %copy-start.53 = (f32[48]{0:T(128)S(1)}, f32[48]{0:T(128)}, u32[]{:S(2)}) copy-start(f32[48]{0:T(128)} %param.26) | copy-start | bytes 580
  157.9 11.1 copy-start.13
  158.0 11.1 collective-permute-start
  187.7 128.9 %all-gather.11.cloned.1.call-start = ((), (), s32[]{:S(2)}) async-start(), calls=%async_computation.3 | async-start | bytes 9732096 | tf_op jit(solution)/shard_map/all_gather | solution.py:164
  188.4 195.5 %all-gather.15.cloned.1.call-start = ((), (), s32[]{:S(2)}) async-start(), calls=%async_computation.7 | async-start | bytes 7077888 | tf_op jit(solution)/shard_map/all_gather | solution.py:53
  266.0 4.4 copy-start.45
  266.0 4.4 copy-start.46
  266.0 4.4 copy-start.56
  316.6 8.4 copy-start.52
  316.6 8.4 copy-start.7
  316.6 8.4 copy-start.8
  316.6 8.4 copy-start.11
  316.6 8.4 copy-start.47
  339.8 346.3 %all-reduce.24.cloned.1.call-start = ((), (), s32[]{:S(2)}) async-start(), calls=%async_computation.8 | async-start | bytes 183296
  434.1 7.3 copy-start
  434.1 7.3 copy-start.1
  435.6 11.7 copy-start.25
  435.6 6.8 copy-start.3
  435.6 6.8 copy-start.17
  442.4 4.9 copy-start.4
  442.4 4.9 copy-start.38
  442.4 4.9 copy-start.41
  442.4 4.9 copy-start.43
  492.6 8.3 copy-start.5
  492.6 8.3 copy-start.26
  492.6 8.3 copy-start.29
  492.6 8.3 copy-start.39
  492.6 8.3 copy-start.42
  492.6 8.3 copy-start.44
  522.4 7.6 copy-start.19
  522.4 7.6 copy-start.22
  522.4 7.6 copy-start.23
  522.4 8.2 copy-start.18
  522.4 8.6 copy-start.10
  522.5 8.6 copy-start.40
  540.2 4.8 copy-start.24
  540.3 3.1 collective-permute-start.1
  545.1 12.5 copy-start.9
  545.1 12.5 copy-start.48
  557.5 343.3 %reduce-scatter.6.cloned.1.call-start = ((), (), s32[]{:S(2)}) async-start(), calls=%async_computation.5 | async-start | bytes 19464192 | tf_op jit(solution)/shard_map/reduce_scatter | solution.py:243
  566.6 703.9 %reduce-scatter.4.cloned.1.call-start = ((), (), s32[]{:S(2)}) async-start(), calls=%async_computation.4 | async-start | bytes 41361408 | tf_op jit(solution)/shard_map/reduce_scatter | solution.py:242
  584.6 7.6 copy-start.50
  584.6 7.6 copy-start.14
  584.6 7.6 copy-start.16
  584.6 7.6 copy-start.20
  (18 other events, 55.6 us)
Sparse Core Ops, SparseCore 0:
  10.9 134.2 all-gather.8
  187.8 44.1 all-gather.12
  235.0 81.5 all-gather.10
  340.0 43.9 all-gather.14
  557.6 128.4 all-reduce.23
  693.0 207.7 reduce-scatter.5
  907.8 362.7 reduce-scatter.3
where the time goes:
time: 1290 us; the launch traced here: 1280 us
  waiting for transfers between devices  797 us (62%)
  matrix products  169 us (13%)
  other arithmetic  128 us (10%)
  blocking collectives  92.5 us (7%)
  local copies, waits for them, and re-layouts  75 us (6%)
  between operations  15.1 us (1%)
    reduce_scatter x1, waiting for transfers between devices, per_device(): lax.psum_scatter(d_w_in, ('dp', 'seq'), scatter_dimension=0, tiled=True)  370 us
    reduce_scatter x1, waiting for transfers between devices, per_device(): lax.psum_scatter(d_w_out, ('dp', 'seq'), scatter_dimension=0, tiled=True)  209 us
    unnamed x8, waiting for transfers between devices  93.7 us
    dot_general x3, matrix products, block_step(): jnp.einsum('hts,shp->thp', weighted, x_heads, precision=highest)  50 us
    all_gather x1, waiting for transfers between devices, per_device(): lax.all_gather(in_weight, ('dp', 'seq'), axis=0, tiled=True)  47.3 us
    all_gather x1, blocking collectives, per_device(): lax.all_gather(conv_weight, ('dp', 'seq'), axis=0, tiled=True)  44.2 us
    unnamed x1, blocking collectives  39.6 us
    all_gather x1, waiting for transfers between devices, carried_in(): lax.all_gather(part.astype(kind), axis)  36.8 us
  transfers between devices with their start and end apart: 9, of which 8 were waited for; matrix products, arithmetic and copies ran while one was open for 11% of the time, Pallas kernels for 0%

commit v1 on v0

v1 whole, which is shorter than its diff:
```python
from functools import partial

import jax
import jax.numpy as jnp
from jax import lax
from jax.experimental import pallas as pl
from jax.experimental.pallas import tpu as pltpu
from jax.sharding import PartitionSpec as P

HDIM = 64
NSTATE = 128
CONVK = 4
LANES = 128
SUB = 128
TOKENS = 256
EDGE = 8

epsilon = 1e-05
highest = lax.Precision.HIGHEST
bf16 = jnp.bfloat16
f32 = jnp.float32


def dot(a, b, dims, precision=None):
    return lax.dot_general(
        a, b, (dims, ((), ())), preferred_element_type=f32, precision=precision
    )


NN, NT, TN = ((1,), (0,)), ((1,), (1,)), ((0,), (0,))


def sigmoid(a):
    return 0.5 * jnp.tanh(0.5 * a) + 0.5


def iota(shape, axis):
    return lax.broadcasted_iota(jnp.int32, shape, axis)


def steps_of(raw, bias):
    shifted = raw + bias
    return jnp.maximum(shifted, 0.0) + jnp.log1p(jnp.exp(-jnp.abs(shifted)))


def convolve(pad, conv_ref, tile, count):
    total = conv_ref[CONVK : CONVK + 1, tile]
    for k in range(CONVK):
        total = total + pad[EDGE - CONVK + 1 + k : EDGE - CONVK + 1 + k + count, tile] * conv_ref[k : k + 1, tile]
    return total


class Chunk:
    def __init__(self, step, rate):
        n = SUB
        upper = jnp.where(iota((n, n), 0) <= iota((n, n), 1), 1.0, 0.0)
        self.step = step
        self.rows = dot(step * -rate, upper, NN, highest)
        self.cols = self.rows.T
        self.step_cols = step.T

    def col(self, h):
        return jnp.broadcast_to(self.cols[:, h : h + 1], (SUB, SUB))

    def decay(self, h, col, hide):
        return jnp.exp(col - self.rows[h : h + 1, :] + hide)

    def step_col(self, h):
        return jnp.broadcast_to(self.step_cols[:, h : h + 1], (SUB, SUB))


def fwd_kernel(
    proj_ref, raw_ref, cot_ref, wout_ref, conv_ref, lane_ref, head_ref,
    y_ref, dg_ref, out_ref, state_ref, sum_ref,
    pad, act, carry, gated,
):
    block = proj_ref.shape[0]
    din = y_ref.shape[1]
    conv = conv_ref.shape[1]

    @pl.when(pl.program_id(0) == 0)
    def _():
        carry[...] = jnp.zeros_like(carry)
        pad[0:EDGE, :] = jnp.zeros((EDGE, conv), f32)

    @pl.when(pl.program_id(0) > 0)
    def _():
        pad[0:EDGE, :] = pad[block : block + EDGE, :]

    for j in range(conv // LANES):
        tile = slice(j * LANES, (j + 1) * LANES)
        pad[EDGE:, tile] = proj_ref[:, din + j * LANES : din + (j + 1) * LANES].astype(f32)
        filtered = convolve(pad, conv_ref, tile, block)
        act[:, tile] = filtered * sigmoid(filtered)
    dg_ref[...] = dot(cot_ref[...], wout_ref[...], NT)

    low = iota((SUB, LANES), 1) < HDIM
    hide = jnp.where(iota((SUB, SUB), 0) >= iota((SUB, SUB), 1), 0.0, -1e30)
    for i in range(block // SUB):
        rows = slice(i * SUB, (i + 1) * SUB)
        b = act[rows, din : din + NSTATE].astype(bf16)
        c = act[rows, din + NSTATE :].astype(bf16)
        chunk = Chunk(steps_of(raw_ref[:, rows], head_ref[1]), head_ref[0])
        scores = dot(c, b, NT)
        sq = jnp.zeros((SUB, LANES), f32)
        cross = jnp.zeros((SUB, LANES), f32)
        for j in range(din // LANES):
            tile = slice(j * LANES, (j + 1) * LANES)
            x = act[rows, tile]
            col0, col1 = chunk.col(2 * j), chunk.col(2 * j + 1)
            m0 = (chunk.decay(2 * j, col0, hide) * scores).astype(bf16)
            m1 = (chunk.decay(2 * j + 1, col1, hide) * scores).astype(bf16)
            cexp = jnp.where(low, col0, col1)
            xs = x * jnp.where(low, chunk.step_col(2 * j), chunk.step_col(2 * j + 1))
            zero = jnp.zeros_like(xs)
            split = jnp.concatenate(
                [jnp.where(low, xs, zero).astype(bf16), jnp.where(low, zero, xs).astype(bf16)], axis=0
            )
            before = carry[:, tile]
            state_ref[i, :, tile] = before.astype(bf16)
            y = dot(jnp.concatenate([m0, m1], axis=1), split, NN)
            y = y + dot(c, before.astype(bf16), NN) * jnp.exp(cexp)
            y_ref[rows, tile] = y
            last = cexp[SUB - 1 :, :]
            weighted = (xs * jnp.exp(last - cexp)).astype(bf16)
            carry[:, tile] = before * jnp.exp(last) + dot(b, weighted, TN)
            z = proj_ref[rows, tile].astype(f32)
            v = (y + lane_ref[0:1, tile] * x) * (z * sigmoid(z))
            scaled = v * lane_ref[1:2, tile]
            gated[rows, tile] = scaled.astype(bf16)
            sq = sq + v * v
            cross = cross + scaled * dg_ref[rows, tile]
        ones = jnp.ones((4, LANES), f32)
        sum_ref[0:4, rows] = dot(ones, sq, NT, highest)
        sum_ref[4:8, rows] = dot(ones, cross, NT, highest)
    out_ref[...] = dot(gated[...], wout_ref[...], NN).astype(bf16)


def bwd_kernel(
    total_din,
    proj_ref, rim_ref, raw_ref, y_ref, dg_ref, sum_ref, state_ref, cot_ref, conv_ref, lane_ref, head_ref,
    dproj_ref, draw_ref, dwout_ref, dconv_ref, dlane_ref, dhead_ref,
    pad, act, slope, dpad, carry, edge, gated, dact,
):
    block = proj_ref.shape[0]
    din = y_ref.shape[1]
    conv = conv_ref.shape[1]
    step_id = pl.program_id(0)
    first = step_id == pl.num_programs(0) - 1

    @pl.when(step_id == 0)
    def _():
        carry[...] = jnp.zeros_like(carry)
        edge[...] = jnp.zeros_like(edge)
        dpad[0:EDGE, :] = jnp.zeros((EDGE, conv), f32)
        dwout_ref[...] = jnp.zeros_like(dwout_ref)
        dconv_ref[...] = jnp.zeros_like(dconv_ref)
        dlane_ref[...] = jnp.zeros_like(dlane_ref)
        dhead_ref[...] = jnp.zeros_like(dhead_ref)

    dpad[block : block + EDGE, :] = dpad[0:EDGE, :]
    keep = jnp.where(first, 0.0, 1.0)
    for j in range(conv // LANES):
        tile = slice(j * LANES, (j + 1) * LANES)
        src = slice(din + j * LANES, din + (j + 1) * LANES)
        pad[0:EDGE, tile] = rim_ref[rim_ref.shape[0] - EDGE :, src].astype(f32) * keep
        pad[EDGE:, tile] = proj_ref[:, src].astype(f32)
        filtered = convolve(pad, conv_ref, tile, block)
        s = sigmoid(filtered)
        act[:, tile] = filtered * s
        slope[:, tile] = s * (1.0 + filtered * (1.0 - s))

    low = iota((SUB, LANES), 1) < HDIM
    hide = jnp.where(iota((SUB, SUB), 0) >= iota((SUB, SUB), 1), 0.0, -1e30)
    lower = jnp.where(iota((SUB, SUB), 0) >= iota((SUB, SUB), 1), 1.0, 0.0)
    heads = draw_ref.shape[0]
    dgain = [jnp.zeros((1, LANES), f32) for _ in range(din // LANES)]
    dskip = [jnp.zeros((1, LANES), f32) for _ in range(din // LANES)]
    for i in reversed(range(block // SUB)):
        rows = slice(i * SUB, (i + 1) * SUB)
        b = act[rows, din : din + NSTATE].astype(bf16)
        c = act[rows, din + NSTATE :].astype(bf16)
        chunk = Chunk(steps_of(raw_ref[:, rows], head_ref[1]), head_ref[0])
        scores = dot(c, b, NT)
        sums = sum_ref[:, rows].T
        scale = lax.rsqrt(jnp.broadcast_to(sums[:, 0:1], (SUB, LANES)) * (1.0 / total_din) + epsilon)
        mean = jnp.broadcast_to(sums[:, 4:5], (SUB, LANES)) * (1.0 / total_din) * (scale * scale * scale)
        dscores = jnp.zeros((SUB, SUB), f32)
        d_b = jnp.zeros((SUB, NSTATE), f32)
        d_c = jnp.zeros((SUB, NSTATE), f32)
        d_cum = jnp.zeros((heads, SUB), f32)
        d_step = jnp.zeros((heads, SUB), f32)
        reach = jnp.zeros((heads, 8), f32)
        for j in range(din // LANES):
            tile = slice(j * LANES, (j + 1) * LANES)
            x = act[rows, tile]
            y = y_ref[rows, tile]
            skip, gain = lane_ref[0:1, tile], lane_ref[1:2, tile]
            z = proj_ref[rows, tile].astype(f32)
            sz = sigmoid(z)
            mixed = y + skip * x
            silu = z * sz
            v = mixed * silu
            dg = dg_ref[rows, tile]
            vs = v * scale
            dgain[j] = dgain[j] + jnp.sum(dg * vs, axis=0, keepdims=True)
            gated[rows, tile] = (vs * gain).astype(bf16)
            dv = scale * (gain * dg) - v * mean
            dy = dv * silu
            dproj_ref[rows, tile] = (dv * mixed * (sz * (1.0 + z * (1.0 - sz)))).astype(bf16)
            dskip[j] = dskip[j] + jnp.sum(dy * x, axis=0, keepdims=True)

            col0, col1 = chunk.col(2 * j), chunk.col(2 * j + 1)
            l0, l1 = chunk.decay(2 * j, col0, hide), chunk.decay(2 * j + 1, col1, hide)
            m = jnp.concatenate([(l0 * scores).astype(bf16), (l1 * scores).astype(bf16)], axis=0)
            cexp = jnp.where(low, col0, col1)
            step = jnp.where(low, chunk.step_col(2 * j), chunk.step_col(2 * j + 1))
            last = cexp[SUB - 1 :, :]
            grow, tail = jnp.exp(cexp), jnp.exp(last - cexp)
            xs = x * step
            zero = jnp.zeros_like(dy)
            dsplit = jnp.concatenate(
                [jnp.where(low, dy, zero).astype(bf16), jnp.where(low, zero, dy).astype(bf16)], axis=0
            )
            xs16 = xs.astype(bf16)
            dm = dot(dsplit, xs16, NT)
            dscores = dscores + dm[:SUB] * l0 + dm[SUB:] * l1
            dend = carry[:, tile]
            dend16 = dend.astype(bf16)
            before = state_ref[i, :, tile]
            dxs = dot(m, dsplit, TN) + dot(b, dend16, NN) * tail
            grown = (dy * grow).astype(bf16)
            d_c = d_c + dot(grown, before, NT)
            d_b = d_b + dot((xs * tail).astype(bf16), dend16, NT)
            dprev = dend * jnp.exp(last) + dot(c, grown, TN)
            carry[:, tile] = dprev
            pick = jnp.where(lax.shift_right_logical(iota((heads, LANES), 1), 6) + 2 * j == iota((heads, LANES), 0), 1.0, 0.0)
            balance = dy.astype(bf16).astype(f32) * y - xs16.astype(f32) * dxs
            d_cum = d_cum + dot(pick, balance, NT, highest)
            d_step = d_step + dot(pick, x * dxs, NT, highest)
            crossing = jnp.sum(dprev * before.astype(f32), axis=0, keepdims=True)
            reach = reach + dot(pick, jnp.broadcast_to(crossing, (8, LANES)), NT, highest)
            dact[rows, tile] = dxs * step + skip * dy
        ds16 = dscores.astype(bf16)
        dact[rows, din : din + NSTATE] = d_b + dot(ds16, c, TN)
        dact[rows, din + NSTATE :] = d_c + dot(ds16, b, NN)
        d_log = dot(d_cum, lower, NN, highest) + edge[...]
        edge[...] = jnp.broadcast_to(reach[:, 0:1], edge.shape)
        raw = raw_ref[:, rows] + head_ref[1]
        draw = (d_step - head_ref[0] * d_log) * sigmoid(raw)
        draw_ref[:, rows] = draw
        dhead_ref[0] += -chunk.step * d_log
        dhead_ref[1] += draw
    for j in range(din // LANES):
        tile = slice(j * LANES, (j + 1) * LANES)
        dlane_ref[0:1, tile] += dskip[j]
        dlane_ref[1:2, tile] += dgain[j]
    dwout_ref[...] += dot(gated[...], cot_ref[...], TN)
    for j in range(conv // LANES):
        tile = slice(j * LANES, (j + 1) * LANES)
        df = dact[:, tile] * slope[:, tile]
        dpad[0:block, tile] = df
        dconv_ref[CONVK : CONVK + 1, tile] += jnp.sum(df, axis=0, keepdims=True)
        back = jnp.zeros((block, LANES), f32)
        for k in range(CONVK):
            shift = CONVK - 1 - k
            dconv_ref[k : k + 1, tile] += jnp.sum(
                df * pad[EDGE - shift : EDGE - shift + block, tile], axis=0, keepdims=True
            )
            back = back + conv_ref[k : k + 1, tile] * dpad[shift : shift + block, tile]
        dproj_ref[:, din + j * LANES : din + (j + 1) * LANES] = back.astype(bf16)


def rows_spec(block, width):
    return pl.BlockSpec((block, width), lambda t: (t, 0))


def whole(shape):
    return pl.BlockSpec(shape, lambda t: (0,) * len(shape))


def mixer_forward(proj, raw, cot, w_out, conv, lanes, heads):
    length, width = proj.shape
    din, d = w_out.shape
    cc = conv.shape[1]
    block = min(TOKENS, length)
    n = block // SUB
    cols = pl.BlockSpec((8, block), lambda t: (0, t))
    return pl.pallas_call(
        fwd_kernel,
        grid=(length // block,),
        in_specs=[
            rows_spec(block, width), cols, rows_spec(block, d), whole(w_out.shape),
            whole(conv.shape), whole(lanes.shape), whole(heads.shape),
        ],
        out_specs=[
            rows_spec(block, din), rows_spec(block, din), rows_spec(block, d),
            pl.BlockSpec((n, NSTATE, din), lambda t: (t, 0, 0)), cols,
        ],
        out_shape=[
            jax.ShapeDtypeStruct((length, din), f32),
            jax.ShapeDtypeStruct((length, din), f32),
            jax.ShapeDtypeStruct((length, d), bf16),
            jax.ShapeDtypeStruct((length // SUB, NSTATE, din), bf16),
            jax.ShapeDtypeStruct((8, length), f32),
        ],
        scratch_shapes=[
            pltpu.VMEM((block + EDGE, cc), f32),
            pltpu.VMEM((block, cc), f32),
            pltpu.VMEM((NSTATE, din), f32),
            pltpu.VMEM((block, din), bf16),
        ],
        name="mix_forward",
    )(proj, raw, cot, w_out, conv, lanes, heads)


def mixer_backward(total_din, proj, raw, y, dg, sums, states, cot, conv, lanes, heads):
    length, width = proj.shape
    din, d = y.shape[1], cot.shape[1]
    cc = conv.shape[1]
    block = min(TOKENS, length)
    n = block // SUB
    last = length // block - 1
    rim = 16

    def back(block, width):
        return pl.BlockSpec((block, width), lambda t: (last - t, 0))

    cols = pl.BlockSpec((8, block), lambda t: (0, last - t))
    return pl.pallas_call(
        partial(bwd_kernel, total_din),
        grid=(length // block,),
        in_specs=[
            back(block, width),
            pl.BlockSpec((rim, width), lambda t: (jnp.maximum((last - t) * (block // rim) - 1, 0), 0)),
            cols, back(block, din), back(block, din), cols,
            pl.BlockSpec((n, NSTATE, din), lambda t: (last - t, 0, 0)),
            back(block, d), whole(conv.shape), whole(lanes.shape), whole(heads.shape),
        ],
        out_specs=[
            back(block, width), cols, whole((din, d)), whole((8, cc)), whole((8, din)), whole((2, 8, SUB)),
        ],
        out_shape=[
            jax.ShapeDtypeStruct((length, width), bf16),
            jax.ShapeDtypeStruct((8, length), f32),
            jax.ShapeDtypeStruct((din, d), f32),
            jax.ShapeDtypeStruct((8, cc), f32),
            jax.ShapeDtypeStruct((8, din), f32),
            jax.ShapeDtypeStruct((2, 8, SUB), f32),
        ],
        scratch_shapes=[
            pltpu.VMEM((block + EDGE, cc), f32),
            pltpu.VMEM((block, cc), f32),
            pltpu.VMEM((block, cc), f32),
            pltpu.VMEM((block + EDGE, cc), f32),
            pltpu.VMEM((NSTATE, din), f32),
            pltpu.VMEM((8, SUB), f32),
            pltpu.VMEM((block, din), bf16),
            pltpu.VMEM((block, cc), f32),
        ],
        name="mix_backward",
    )(proj, proj, raw, y, dg, sums, states, cot, conv, lanes, heads)


def rms_scale(values, gain):
    mean_sq = jnp.mean(values * values, axis=-1, keepdims=True)
    return values * lax.rsqrt(mean_sq + epsilon) * gain


def widen(array, size, axis):
    pads = [(0, 0)] * array.ndim
    pads[axis] = (0, size - array.shape[axis])
    return jnp.pad(array, pads)


def per_device(
    tokens,
    cotangent,
    in_weight,
    out_weight,
    conv_weight,
    conv_bias,
    norm_gain,
    gate_gain,
    decay_rate,
    dt_bias,
    d_skip,
):
    ranks = lax.axis_size("seq")
    me = lax.axis_index("seq")
    both = ("dp", "seq")
    heads = decay_rate.shape[0] // ranks
    din = heads * HDIM
    padded = -(-din // LANES) * LANES
    din_all = din * ranks
    rows, width = in_weight.shape
    conv_all = din_all + 2 * NSTATE
    main = 2 * padded + 2 * NSTATE

    def mine(array, size, axis=0):
        return lax.dynamic_slice_in_dim(array, me * size, size, axis)

    x_own = tokens[0].astype(f32)
    tok = lax.all_gather(tokens[0], "seq", axis=0, tiled=True)
    cot = lax.all_gather(cotangent[0], "seq", axis=0, tiled=True)
    send = jnp.concatenate(
        [
            widen(in_weight[:, :din_all].reshape(rows, ranks, din), padded, 2),
            widen(in_weight[:, din_all : 2 * din_all].reshape(rows, ranks, din), padded, 2),
            jnp.broadcast_to(
                in_weight[:, None, 2 * din_all : 2 * din_all + 2 * NSTATE], (rows, ranks, 2 * NSTATE)
            ),
            widen(in_weight[:, din_all + conv_all :].reshape(rows, ranks, heads), 8, 2),
        ],
        axis=2,
    ).transpose(1, 0, 2)
    cols = send.shape[2]
    got = lax.all_to_all(send, "seq", 0, 0)
    w_all = lax.all_gather(got.reshape(ranks * rows, cols), "dp", axis=0, tiled=True)
    w_in, w_dt = w_all[:, :main], w_all[:, main:].T
    w_out = widen(mine(lax.all_gather(out_weight, both, axis=0, tiled=True), din), padded, 0)
    conv_w, conv_b, gain_norm, gain_gate = (
        lax.all_gather(a, both, axis=0, tiled=True).astype(f32)
        for a in (conv_weight, conv_bias, norm_gain, gate_gain)
    )
    taps = jnp.concatenate([conv_w.T, conv_b[None], jnp.zeros((8 - CONVK - 1, conv_all), f32)], axis=0)
    conv = jnp.concatenate([widen(mine(taps, din, 1), padded, 1), taps[:, din_all:]], axis=1)
    rate, bias, skip = (mine(a, heads) for a in (decay_rate, dt_bias, d_skip))
    lanes = jnp.stack([jnp.repeat(skip, HDIM), mine(gain_gate, din)])
    lanes = widen(widen(lanes, padded, 1), 8, 0)
    head_rows = jnp.broadcast_to(widen(jnp.stack([rate, bias]), 8, 1)[:, :, None], (2, 8, SUB))

    normed = rms_scale(tok.astype(f32), gain_norm).astype(bf16)
    proj = dot(normed, w_in, NN).astype(bf16)
    raw = dot(w_dt, normed, NT).astype(bf16).astype(f32)
    y, dg, out_part, states, sums = mixer_forward(proj, raw, cot, w_out, conv, lanes, head_rows)
    sums = lax.psum(sums, "seq")
    out_sum = lax.psum_scatter(out_part, "seq", scatter_dimension=0, tiled=True)
    d_proj, d_raw, d_w_out, d_conv, d_lane, d_head = mixer_backward(
        din_all, proj, raw, y, dg, sums, states, cot, conv, lanes, head_rows
    )
    own = mine(sums[0], x_own.shape[0])[:, None]
    block_out = (x_own + lax.rsqrt(own / din_all + epsilon) * out_sum.astype(f32)).astype(bf16)
    d_raw16 = d_raw.astype(bf16)
    d_normed_part = (dot(d_proj, w_in, NT) + dot(d_raw16, w_dt, TN)).astype(bf16)
    d_normed = lax.psum_scatter(d_normed_part, "seq", scatter_dimension=0, tiled=True).astype(f32)
    d_w_in = jnp.concatenate([dot(normed, d_proj, TN), dot(normed, d_raw16, ((0,), (1,)))], axis=1).astype(bf16)

    _, norm_back = jax.vjp(rms_scale, x_own, gain_norm)
    d_xn, d_g1 = norm_back(d_normed)
    grad_x = cotangent[0].astype(f32) + d_xn

    d_w_in = lax.psum_scatter(d_w_in, "dp", scatter_dimension=0, tiled=True)
    d_w_in = lax.all_to_all(d_w_in.reshape(ranks, rows, cols), "seq", 0, 0).astype(f32)
    spread = d_w_in.transpose(1, 0, 2)
    grad_in = jnp.concatenate(
        [
            spread[:, :, :din].reshape(rows, din_all),
            spread[:, :, padded : padded + din].reshape(rows, din_all),
            jnp.sum(spread[:, :, 2 * padded : main], axis=1),
            spread[:, :, main : main + heads].reshape(rows, heads * ranks),
        ],
        axis=1,
    )
    full_out = lax.dynamic_update_slice_in_dim(
        jnp.zeros((din_all, w_out.shape[1]), bf16), d_w_out[:din].astype(bf16), me * din, 0
    )
    grad_out = lax.psum_scatter(full_out, both, scatter_dimension=0, tiled=True).astype(f32)

    def place(own, size):
        return lax.dynamic_update_slice_in_dim(
            jnp.zeros((size * ranks,) + own.shape[1:], f32), own, me * size, 0
        )

    d_cw, d_cb = d_conv[:CONVK].T, d_conv[CONVK]
    full_cw = jnp.concatenate([place(d_cw[:din], din), d_cw[padded:]], axis=0)
    full_cb = jnp.concatenate([place(d_cb[:din], din), d_cb[padded:]], axis=0)
    d_skp = jnp.sum(d_lane[0, :din].reshape(heads, HDIM), axis=1)
    d_rate, d_bias = jnp.sum(d_head, axis=2)[:, :heads]
    g_cw, g_cb, g_gain, g_gate = (
        lax.psum_scatter(a, both, scatter_dimension=0, tiled=True)
        for a in (full_cw, full_cb, d_g1, place(d_lane[1, :din], din))
    )
    head_sums = lax.psum([place(a, heads) for a in (d_rate, d_bias, d_skp)], both)
    return (
        block_out[None],
        grad_x[None],
        grad_in,
        grad_out,
        g_cw,
        g_cb,
        g_gain,
        g_gate,
        head_sums[0],
        head_sums[1],
        head_sums[2],
    )


def solution(mesh):
    rows = P(("dp", "seq"), None)
    flat = P(("dp", "seq"))
    act = P("dp", "seq", None)
    return jax.shard_map(
        per_device,
        mesh=mesh,
        in_specs=(act, act, rows, rows, rows, flat, flat, flat, P(), P(), P()),
        out_specs=(act, act, rows, rows, rows, flat, flat, flat, P(), P(), P()),
        check_vma=False,
    )
```

time: 1290 us -> 885 us (0.69)
  waiting for transfers between devices: 797 us -> 600 us
  matrix products: 169 us -> 46.1 us
  other arithmetic: 128 us -> 17.6 us
  Pallas kernels: 0 us -> 66.9 us
  local copies, waits for them, and re-layouts: 75 us -> 26.6 us
  blocking collectives: 92.5 us -> 108 us
    reduce_scatter x2 -> x4, waiting for transfers between devices: 579 us -> 283 us  [the longest x1 138 us: per_device(): lax.psum_scatter(full_out, both, scatter_dimension=0, tiled=True)]
    dot_general x21 -> x6, matrix products: 169 us -> 46.1 us  [dot(): lax.dot_general(a, b, (dims, ((), ())), preferred_element_type=f32, preci...]
    pallas_call x0 -> x2, Pallas kernels: none -> 66.9 us  [the longest x1 41.1 us: mixer_backward(): pl.pallas_call(partial(bwd_kernel, total_din), grid=(length // block,), i...]
    psum x0 -> x1, waiting for transfers between devices: none -> 53.1 us  [per_device(): sums = lax.psum(sums, 'seq')]
    select_n x17 -> x0, other arithmetic: 49.7 us -> none  [the longest x8 24.6 us: carried_hop(): return jax.tree.map(lambda a, b: jnp.where(reached, a, b), new, before)]
    unnamed x8 -> x11, waiting for transfers between devices: 93.7 us -> 132 us
    all_to_all x0 -> x1, blocking collectives: none -> 25 us  [per_device(): got = lax.all_to_all(send, 'seq', 0, 0)]
    exp x17 -> x0, other arithmetic: 20 us -> none  [the longest x16 19.2 us: combine(): jnp.exp(later_part[0])[:, None, None]]
  transfers between devices with their start and end apart: 9 -> 11, of which waited for: 8 -> 10; matrix products, arithmetic and copies ran while one was open for 11% -> 8% of each run, Pallas kernels for 0% -> 0%
where the time goes in v1:
time: 885 us; the launch traced here: 884 us
  waiting for transfers between devices  600 us (68%)
  blocking collectives  108 us (12%)
  Pallas kernels  66.9 us (8%)
  matrix products  46.1 us (5%)
  local copies, waits for them, and re-layouts  26.6 us (3%)
  other arithmetic  17.6 us (2%)
  between operations  14.6 us (2%)
    reduce_scatter x1, waiting for transfers between devices, per_device(): lax.psum_scatter(full_out, both, scatter_dimension=0, tiled=True)  138 us
    unnamed x11, waiting for transfers between devices  132 us
    all_gather x1, waiting for transfers between devices, per_device(): lax.all_gather(out_weight, both, axis=0, tiled=True)  66 us
    reduce_scatter x1, waiting for transfers between devices, per_device(): d_w_in = lax.psum_scatter(d_w_in, 'dp', scatter_dimension=0, tiled=True)  61 us
    psum x1, waiting for transfers between devices, per_device(): sums = lax.psum(sums, 'seq')  53.1 us
    reduce_scatter x1, waiting for transfers between devices, per_device(): out_sum = lax.psum_scatter(out_part, 'seq', scatter_dimension=0, tiled=True)  46.3 us
    dot_general x6, matrix products, dot(): lax.dot_general(a, b, (dims, ((), ())), preferred_element_type=f32, preci...  46.1 us
    all_gather x1, waiting for transfers between devices, per_device(): cot = lax.all_gather(cotangent[0], 'seq', axis=0, tiled=True)  43.3 us
  transfers between devices with their start and end apart: 11, of which 10 were waited for; matrix products, arithmetic and copies ran while one was open for 8% of the time, Pallas kernels for 0%

profile of v1, /device:TPU:0, one launch (start us, length us, event | category | flops | bytes accessed | tf_op | source)
XLA Modules:
  0.0 884.2 jit_solution(16502960852825074291)
XLA Ops:
  7.2 0.7 all-gather.12.cloned.1.call-update
  8.0 0.7 slice.72
  8.7 0.7 slice.71
  9.7 1.1 fusion.30
  11.0 25.0 %all_to_all.10 = bf16[8,48,1032]{2,1,0:T(8,128)(2,1)} all-to-all(bf16[8,48,1032]{2,1,0:T(8,128)(2,1)S(1)} %fusion.16), channel_id=1, replica_groups=mesh['dp'=4,'seq'=8] {'seq'}, dimensions={0} | all-to-all | bytes 1585152 | tf_op jit(solution)/shard_map/all_to_all | solution.py:418
  36.1 0.7 all-gather.10.cloned.1.call-update
  38.2 40.6 %all-reduce.11 = (bf16[1536]{0:T(1024)(128)(2,1)S(1)}, bf16[3328]{0:T(1024)(128)(2,1)S(1)}, bf16[3072]{0:T(1024)(128)(2,1)S(1)}) all-reduce(bf16[1536]{0:T(1024)(128)(2,1)S(1)} %dynamic-update-slice, bf16[3328]{0:T(1024)(128)(2,1)S(1)} %dynamic-update-slice.1, ...), channel_id=1, replica_groups=mesh['dp'=4,'seq'=8] {'dp','seq'}, use_global_device_ids=true, to_apply=%add.3 | all-reduce | flops 7936 | bytes 31744
  78.9 42.4 %all-gather.2 = bf16[32,104,4]{1,2,0:T(4,128)(2,1)S(1)} all-gather(bf16[1,104,4]{1,2,0:T(4,128)(2,1)S(1)} %bitcast.77), channel_id=1, replica_groups=mesh['dp'=4,'seq'=8] {'dp','seq'}, dimensions={0}, use_global_device_ids=true | all-gather | bytes 27456 | tf_op jit(solution)/shard_map/all_gather | solution.py:423
  122.6 0.6 pad_maximum_fusion.3.conv_ref
  123.2 4.1 fusion
  127.3 8.5 all-gather.8.cloned.1.call-done
  135.8 5.7 fusion.6.raw_ref
  141.5 11.4 %convolution_convert_fusion.1.proj_ref.rim_ref = bf16[2048,1024]{1,0:T(8,128)(2,1)} fusion(bf16[1536,1032]{1,0:T(8,128)(2,1)S(1)} %copy-done.5, bf16[1,2048,1536]{2,1,0:T(8,128)(2,1)} %all-gather.12.cloned.1.call-done, f32[1536]{0:T(1024)S(1)} %convert_element_type.60, f32[2048]{0:T(1024)S(1)} %add_rsqrt_fusion), kind=kOutput, calls=%fused_computation.7 | convolution fusion | flops 6457131008 | bytes 13647872 | tf_op jit(solution)/shard_map/dot_general | solution.py:25
  152.9 66.0 %all-gather.10.cloned.1.call-done = bf16[3072,1536]{1,0:T(8,128)(2,1)} async-done(((bf16[96,1536]{1,0:T(8,128)(2,1)}), bf16[3072,1536]{1,0:T(8,128)(2,1)}) %all-gather.10.cloned.1.call-update) | async-done | bytes 9437200 | tf_op jit(solution)/shard_map/all_gather | solution.py:421
  218.8 2.4 constant_dynamic-slice_fusion.2.wout_ref
  221.2 43.3 %all-gather.14.cloned.1.call-done = bf16[1,2048,1536]{2,1,0:T(8,128)(2,1)} async-done(((bf16[1,256,1536]{2,1,0:T(8,128)(2,1)}), bf16[1,2048,1536]{2,1,0:T(8,128)(2,1)}) %all-gather.14.cloned.1.call-update) | async-done | bytes 6291472 | tf_op jit(solution)/shard_map/all_gather | solution.py:405
  264.5 0.7 broadcast_in_dim.49.head_ref
  265.2 25.8 %mix_forward.1 = (f32[2048,384]{1,0:T(8,128)}, f32[2048,384]{1,0:T(8,128)}, bf16[2048,1536]{1,0:T(8,128)(2,1)}, bf16[16,128,384]{2,1,0:T(8,128)(2,1)}, f32[8,2048]{1,0:T(8,128)}) custom-call(bf16[2048,1024]{1,0:T(8,128)(2,1)} %convolution_convert_fusion.1.proj_ref.rim_ref, f32[8,2048]{1,0:T(8,128)} %fusion.6.raw_ref, bf16[2048,1536]{1,0:T(8,128)(2,1)} %bitcast.66, ...), custom_call_target="tpu_custom_call" | custom-call | tf_op jit(solution)/shard_map/mix_forward/pallas_call | solution.py:289
  291.3 53.1 %all-reduce.15.cloned.1.call-done.sum_ref = f32[8,2048]{1,0:T(8,128)} async-done(((f32[8,2048]{1,0:T(8,128)}), f32[8,2048]{1,0:T(8,128)}) %all-reduce.15.cloned.1.call-update) | async-done | bytes 65552 | tf_op jit(solution)/shard_map/psum | solution.py:437
  344.3 41.1 %mix_backward.1 = (bf16[2048,1024]{1,0:T(8,128)(2,1)}, f32[8,2048]{1,0:T(8,128)}, f32[384,1536]{1,0:T(8,128)}, f32[8,640]{1,0:T(8,128)}, f32[8,384]{1,0:T(8,128)}, /*index=5*/f32[2,8,128]{2,1,0:T(8,128)}) custom-call(bf16[2048,1024]{1,0:T(8,128)(2,1)} %convolution_convert_fusion.1.proj_ref.rim_ref, ...), custom_call_target="tpu_custom_call" | custom-call | tf_op jit(solution)/shard_map/mix_backward/pallas_call | solution.py:330
  385.5 9.5 %fusion.3 = f32[2048,1536]{1,0:T(8,128)S(1)} fusion(bf16[2048,1024]{1,0:T(8,128)(2,1)} %get-tuple-element.27, bf16[1536,1032]{1,0:T(8,128)(2,1)} %all-gather.8.cloned.1.call-done), kind=kOutput, calls=%fused_computation.14 | convolution fusion | flops 6442450944 | bytes 19922944 | tf_op jit(solution)/shard_map/dot_general | solution.py:25
  395.0 5.4 add_convert_fusion
  400.8 4.5 convolution_convert_fusion.3
  405.3 9.6 %convolution_convert_fusion = bf16[1536,1024]{0,1:T(8,128)(2,1)S(1)} fusion(bf16[2048,1024]{1,0:T(8,128)(2,1)S(1)} %copy-done.14, bf16[1,2048,1536]{2,1,0:T(8,128)(2,1)} %all-gather.12.cloned.1.call-done, f32[1536]{0:T(1024)S(1)} %convert_element_type.60, f32[2048]{0:T(1024)S(1)} %add_rsqrt_fusion), kind=kOutput, calls=%fused_computation.6 | convolution fusion | flops 6456606720 | bytes 13645824 | tf_op jit(solution)/shard_map/dot_general | solution.py:25
  415.1 3.9 copy.64
  419.1 0.7 reduce-scatter.8.cloned.1.call-update
  420.5 0.8 slice_reduce_fusion.1
  423.2 0.6 pad_maximum_fusion.2
  423.8 37.9 %reduce-scatter.10.cloned.1.call-done = bf16[256,1536]{1,0:T(8,128)(2,1)} async-done(((bf16[2048,1536]{1,0:T(8,128)(2,1)}), bf16[256,1536]{1,0:T(8,128)(2,1)}) %reduce-scatter.10.cloned.1.call-update) | async-done | bytes 786448 | tf_op jit(solution)/shard_map/reduce_scatter | solution.py:446
  461.8 2.4 fusion.9
  464.3 4.2 broadcast_in_dim.53
  468.4 1.1 convert_dynamic-update-slice_fusion
  469.6 61.0 %reduce-scatter.14.cloned.1.call-done = bf16[384,1032]{1,0:T(8,128)(2,1)} async-done(((bf16[1536,1032]{1,0:T(8,128)(2,1)}), bf16[384,1032]{1,0:T(8,128)(2,1)}) %reduce-scatter.14.cloned.1.call-update) | async-done | bytes 792592 | tf_op jit(solution)/shard_map/reduce_scatter | solution.py:453
  530.6 3.6 all-to-all-start.1
  534.3 13.6 %all-to-all-done.1 = bf16[8,48,1032]{2,1,0:T(8,128)(2,1)S(1)} async-done(((bf16[8,48,1032]{2,1,0:T(8,128)(2,1)}), bf16[8,48,1032]{2,1,0:T(8,128)(2,1)S(1)}, u32[]{:S(2)}, u32[]{:S(2)}) %all-to-all-start.1) | async-done | bytes 792608 | tf_op jit(solution)/shard_map/all_to_all | solution.py:454
  548.5 1.1 pad_maximum_fusion.1
  549.6 46.3 %reduce-scatter.8.cloned.1.call-done = bf16[256,1536]{1,0:T(8,128)(2,1)} async-done(((bf16[2048,1536]{1,0:T(8,128)(2,1)}), bf16[256,1536]{1,0:T(8,128)(2,1)}) %reduce-scatter.8.cloned.1.call-update) | async-done | bytes 786448 | tf_op jit(solution)/shard_map/reduce_scatter | solution.py:438
  595.9 3.5 fusion.11
  599.5 129.8 %all-reduce.17.cloned.1.call-done = (f32[3328,4]{0,1:T(4,128)}, f32[3328]{0:T(1024)}, f32[1536]{0:T(1024)}, f32[3072]{0:T(1024)}, f32[48]{0:T(128)}, /*index=5*/f32[48]{0:T(128)}, f32[48]{0:T(128)}) async-done(((f32[3328,4]{0,1:T(4,128)}, f32[3328]{0:T(1024)}, f32[1536]{0:T(1024)}, f32[3072]{0:T(1024)}, f32[48]{0:T(128)}, /*index=5*/f32[48]{0:T(128)}, f32[48]{0:T(128)}), (f32[3328,4]{0,1:T(4,128)}, ...) | async-done | bytes 85584
  729.2 1.3 dynamic-slice.2
  730.5 1.3 dynamic-slice.3
  731.8 1.3 dynamic-slice.4
  733.0 1.3 constant_dynamic-slice_fusion.3
  734.4 137.7 %reduce-scatter.12.cloned.1.call-done = bf16[96,1536]{1,0:T(8,128)(2,1)} async-done(((bf16[3072,1536]{1,0:T(8,128)(2,1)}), bf16[96,1536]{1,0:T(8,128)(2,1)}) %reduce-scatter.12.cloned.1.call-update) | async-done | bytes 294928 | tf_op jit(solution)/shard_map/reduce_scatter | solution.py:468
  872.1 1.8 convert_element_type.73
  873.9 1.2 copy.96
  875.1 1.1 copy.97
  876.2 1.1 copy.98
  (122 shorter events, 7.3 us)
Async XLA Ops:
  7.2 116.1 %all-gather.12.cloned.1.call-start = ((), (), s32[]{:S(2)}) async-start(), calls=%async_computation.12 | async-start | bytes 7077888 | tf_op jit(solution)/shard_map/all_gather | solution.py:404
  7.9 127.9 %all-gather.8.cloned.1.call-start = ((), (), s32[]{:S(2)}) async-start(), calls=%async_computation.6 | async-start | bytes 4423680 | tf_op jit(solution)/shard_map/all_gather | solution.py:419
  10.8 26.7 %copy-start.15 = (bf16[48]{0:T(256)(128)(2,1)S(1)}, bf16[48]{0:T(256)(128)(2,1)}, u32[]{:S(2)}) copy-start(bf16[48]{0:T(256)(128)(2,1)} %param.17) | copy-start | bytes 292
  10.8 26.9 %copy-start.16 = (bf16[104]{0:T(256)(128)(2,1)S(1)}, bf16[104]{0:T(256)(128)(2,1)}, u32[]{:S(2)}) copy-start(bf16[104]{0:T(256)(128)(2,1)} %param.16) | copy-start | bytes 628
  10.8 27.2 %copy-start.17 = (bf16[96]{0:T(256)(128)(2,1)S(1)}, bf16[96]{0:T(256)(128)(2,1)}, u32[]{:S(2)}) copy-start(bf16[96]{0:T(256)(128)(2,1)} %param.18) | copy-start | bytes 580
  10.8 68.1 %copy-start.8 = (bf16[104,4]{0,1:T(4,128)(2,1)S(1)}, bf16[104,4]{0,1:T(4,128)(2,1)}, u32[]{:S(2)}) copy-start(bf16[104,4]{0,1:T(4,128)(2,1)} %param.15) | copy-start | bytes 2500
  10.8 110.8 %copy-start.18 = (f32[48]{0:T(128)S(1)}, f32[48]{0:T(128)}, u32[]{:S(2)}) copy-start(f32[48]{0:T(128)} %param.21) | copy-start | bytes 580
  10.8 111.1 %copy-start.12 = (f32[48]{0:T(128)S(1)}, f32[48]{0:T(128)}, u32[]{:S(2)}) copy-start(f32[48]{0:T(128)} %param.20) | copy-start | bytes 580
  10.8 111.1 %copy-start.13 = (f32[48]{0:T(128)S(1)}, f32[48]{0:T(128)}, u32[]{:S(2)}) copy-start(f32[48]{0:T(128)} %param.19) | copy-start | bytes 580
  36.1 182.8 %all-gather.10.cloned.1.call-start = ((), (), s32[]{:S(2)}) async-start(), calls=%async_computation.7 | async-start | bytes 9732096 | tf_op jit(solution)/shard_map/all_gather | solution.py:421
  36.8 227.7 %all-gather.14.cloned.1.call-start = ((), (), s32[]{:S(2)}) async-start(), calls=%async_computation.13 | async-start | bytes 7077888 | tf_op jit(solution)/shard_map/all_gather | solution.py:405
  37.4 307.0 %all-reduce.15.cloned.1.call-start = ((), (), s32[]{:S(2)}) async-start(), calls=%async_computation.8 | async-start | bytes 131072 | tf_op jit(solution)/shard_map/psum | solution.py:437
  135.8 5.7 copy-start.5
  291.0 170.7 %reduce-scatter.10.cloned.1.call-start = ((), (), s32[]{:S(2)}) async-start(), calls=%async_computation.10 | async-start | bytes 7077888 | tf_op jit(solution)/shard_map/reduce_scatter | solution.py:446
  385.5 9.5 %copy-start.3 = (f32[8,2048]{1,0:T(8,128)S(1)}, f32[8,2048]{1,0:T(8,128)}, u32[]{:S(2)}) copy-start(f32[8,2048]{1,0:T(8,128)} %get-tuple-element.28) | copy-start | bytes 196612
  400.5 130.2 %reduce-scatter.14.cloned.1.call-start = ((), (), s32[]{:S(2)}) async-start(), calls=%async_computation.14 | async-start | bytes 4423680 | tf_op jit(solution)/shard_map/reduce_scatter | solution.py:453
  400.8 4.5 copy-start.14
  419.0 1.1 copy-start
  419.1 176.9 %reduce-scatter.8.cloned.1.call-start = ((), (), s32[]{:S(2)}) async-start(), calls=%async_computation.9 | async-start | bytes 7077888 | tf_op jit(solution)/shard_map/reduce_scatter | solution.py:438
  419.1 1.3 copy-start.7
  419.1 2.8 copy-start.6
  419.8 309.4 %all-reduce.17.cloned.1.call-start = ((), (), s32[]{:S(2)}) async-start(), calls=%async_computation.15 | async-start | bytes 183296
  421.9 42.3 %copy-start.4 = (f32[3072]{0:T(1024)}, f32[3072]{0:T(1024)S(1)}, u32[]{:S(2)}) copy-start(f32[3072]{0:T(1024)S(1)} %dynamic_update_slice.24) | copy-start | bytes 36868
  422.4 41.8 %copy-start.10 = (f32[48]{0:T(128)}, f32[48]{0:T(128)S(1)}, u32[]{:S(2)}) copy-start(f32[48]{0:T(128)S(1)} %dynamic_update_slice.27) | copy-start | bytes 580
  423.1 41.1 %copy-start.11 = (f32[48]{0:T(128)}, f32[48]{0:T(128)S(1)}, u32[]{:S(2)}) copy-start(f32[48]{0:T(128)S(1)} %bitcast_dynamic-update-slice_fusion.1) | copy-start | bytes 580
  423.2 41.0 %copy-start.9 = (f32[48]{0:T(128)}, f32[48]{0:T(128)S(1)}, u32[]{:S(2)}) copy-start(f32[48]{0:T(128)S(1)} %bitcast_dynamic-update-slice_fusion) | copy-start | bytes 580
  464.2 407.9 %reduce-scatter.12.cloned.1.call-start = ((), (), s32[]{:S(2)}) async-start(), calls=%async_computation.11 | async-start | bytes 9732096 | tf_op jit(solution)/shard_map/reduce_scatter | solution.py:468
  464.3 4.2 copy-start.2
  469.6 64.7 %slice-start = ((f32[8,2048]{1,0:T(8,128)}), f32[1,2048]{1,0:T(1,128)S(1)}, s32[]{:S(2)}) async-start(f32[8,2048]{1,0:T(8,128)} %all-reduce.15.cloned.1.call-done.sum_ref), calls=%async_computation.16 | async-start | bytes 16384 | tf_op jit(solution)/shard_map/slice | solution.py:442
  530.6 17.3 %all-to-all-start.1 = ((bf16[8,48,1032]{2,1,0:T(8,128)(2,1)}), bf16[8,48,1032]{2,1,0:T(8,128)(2,1)S(1)}, u32[]{:S(2)}, u32[]{:S(2)}) async-start(bf16[8,48,1032]{2,1,0:T(8,128)(2,1)} %bitcast.73), calls=%async_computation.3 | async-start | bytes 1769472 | tf_op jit(solution)/shard_map/all_to_all | solution.py:454
  548.2 47.7 %copy-start.1 = (bf16[1,256,1536]{2,1,0:T(8,128)(2,1)S(1)}, bf16[1,256,1536]{2,1,0:T(8,128)(2,1)}, u32[]{:S(2)}) copy-start(bf16[1,256,1536]{2,1,0:T(8,128)(2,1)} %param.12) | copy-start | bytes 2359300
Sparse Core Ops, SparseCore 0:
  9.9 54.3 all-gather.11
  65.9 69.8 all-gather.7
  138.7 80.1 all-gather.9
  220.6 43.9 all-gather.13
  291.1 53.1 all-reduce.14
  400.6 61.1 reduce-scatter.9
  464.1 66.5 reduce-scatter.13
  534.0 61.8 reduce-scatter.7
  603.5 125.6 all-reduce.16
  735.0 137.0 reduce-scatter.11

commit v2 on v1

--- a/solution.py
+++ b/solution.py
@@ -36,6 +36,17 @@
 
 def iota(shape, axis):
     return lax.broadcasted_iota(jnp.int32, shape, axis)
+
+
+def parts(a):
+    high = a.astype(bf16)
+    return high, (a - high.astype(f32)).astype(bf16)
+
+
+def fine(a, b, dims):
+    left = jnp.concatenate([a[0], a[0], a[1]], axis=dims[0][0])
+    right = jnp.concatenate([b[0], b[1], b[0]], axis=dims[1][0])
+    return dot(left, right, dims)
 
 
 def steps_of(raw, bias):
@@ -98,32 +109,28 @@
     hide = jnp.where(iota((SUB, SUB), 0) >= iota((SUB, SUB), 1), 0.0, -1e30)
     for i in range(block // SUB):
         rows = slice(i * SUB, (i + 1) * SUB)
-        b = act[rows, din : din + NSTATE].astype(bf16)
-        c = act[rows, din + NSTATE :].astype(bf16)
+        b, c = parts(act[rows, din : din + NSTATE]), parts(act[rows, din + NSTATE :])
         chunk = Chunk(steps_of(raw_ref[:, rows], head_ref[1]), head_ref[0])
-        scores = dot(c, b, NT)
+        scores = fine(c, b, NT)
         sq = jnp.zeros((SUB, LANES), f32)
         cross = jnp.zeros((SUB, LANES), f32)
         for j in range(din // LANES):
             tile = slice(j * LANES, (j + 1) * LANES)
             x = act[rows, tile]
             col0, col1 = chunk.col(2 * j), chunk.col(2 * j + 1)
-            m0 = (chunk.decay(2 * j, col0, hide) * scores).astype(bf16)
-            m1 = (chunk.decay(2 * j + 1, col1, hide) * scores).astype(bf16)
+            m0 = chunk.decay(2 * j, col0, hide) * scores
+            m1 = chunk.decay(2 * j + 1, col1, hide) * scores
             cexp = jnp.where(low, col0, col1)
             xs = x * jnp.where(low, chunk.step_col(2 * j), chunk.step_col(2 * j + 1))
             zero = jnp.zeros_like(xs)
-            split = jnp.concatenate(
-                [jnp.where(low, xs, zero).astype(bf16), jnp.where(low, zero, xs).astype(bf16)], axis=0
-            )
+            split = jnp.concatenate([jnp.where(low, xs, zero), jnp.where(low, zero, xs)], axis=0)
             before = carry[:, tile]
-            state_ref[i, :, tile] = before.astype(bf16)
-            y = dot(jnp.concatenate([m0, m1], axis=1), split, NN)
-            y = y + dot(c, before.astype(bf16), NN) * jnp.exp(cexp)
+            state_ref[i, :, tile] = before
+            y = fine(parts(jnp.concatenate([m0, m1], axis=1)), parts(split), NN)
+            y = y + fine(c, parts(before), NN) * jnp.exp(cexp)
             y_ref[rows, tile] = y
             last = cexp[SUB - 1 :, :]
-            weighted = (xs * jnp.exp(last - cexp)).astype(bf16)
-            carry[:, tile] = before * jnp.exp(last) + dot(b, weighted, TN)
+            carry[:, tile] = before * jnp.exp(last) + fine(b, parts(xs * jnp.exp(last - cexp)), TN)
             z = proj_ref[rows, tile].astype(f32)
             v = (y + lane_ref[0:1, tile] * x) * (z * sigmoid(z))
             scaled = v * lane_ref[1:2, tile]
@@ -178,10 +185,9 @@
     dskip = [jnp.zeros((1, LANES), f32) for _ in range(din // LANES)]
     for i in reversed(range(block // SUB)):
         rows = slice(i * SUB, (i + 1) * SUB)
-        b = act[rows, din : din + NSTATE].astype(bf16)
-        c = act[rows, din + NSTATE :].astype(bf16)
+        b_parts, c_parts = parts(act[rows, din : din + NSTATE]), parts(act[rows, din + NSTATE :])
         chunk = Chunk(steps_of(raw_ref[:, rows], head_ref[1]), head_ref[0])
-        scores = dot(c, b, NT)
+        scores = fine(c_parts, b_parts, NT)
         sums = sum_ref[:, rows].T
         scale = lax.rsqrt(jnp.broadcast_to(sums[:, 0:1], (SUB, LANES)) * (1.0 / total_din) + epsilon)
         mean = jnp.broadcast_to(sums[:, 4:5], (SUB, LANES)) * (1.0 / total_din) * (scale * scale * scale)
@@ -212,38 +218,36 @@
 
             col0, col1 = chunk.col(2 * j), chunk.col(2 * j + 1)
             l0, l1 = chunk.decay(2 * j, col0, hide), chunk.decay(2 * j + 1, col1, hide)
-            m = jnp.concatenate([(l0 * scores).astype(bf16), (l1 * scores).astype(bf16)], axis=0)
+            m = parts(jnp.concatenate([l0 * scores, l1 * scores], axis=0))
             cexp = jnp.where(low, col0, col1)
             step = jnp.where(low, chunk.step_col(2 * j), chunk.step_col(2 * j + 1))
             last = cexp[SUB - 1 :, :]
             grow, tail = jnp.exp(cexp), jnp.exp(last - cexp)
             xs = x * step
             zero = jnp.zeros_like(dy)
-            dsplit = jnp.concatenate(
-                [jnp.where(low, dy, zero).astype(bf16), jnp.where(low, zero, dy).astype(bf16)], axis=0
-            )
-            xs16 = xs.astype(bf16)
-            dm = dot(dsplit, xs16, NT)
+            dsplit = parts(jnp.concatenate([jnp.where(low, dy, zero), jnp.where(low, zero, dy)], axis=0))
+            xs_parts = parts(xs)
+            dm = fine(dsplit, xs_parts, NT)
             dscores = dscores + dm[:SUB] * l0 + dm[SUB:] * l1
             dend = carry[:, tile]
-            dend16 = dend.astype(bf16)
+            dend_parts = parts(dend)
             before = state_ref[i, :, tile]
-            dxs = dot(m, dsplit, TN) + dot(b, dend16, NN) * tail
-            grown = (dy * grow).astype(bf16)
-            d_c = d_c + dot(grown, before, NT)
-            d_b = d_b + dot((xs * tail).astype(bf16), dend16, NT)
-            dprev = dend * jnp.exp(last) + dot(c, grown, TN)
+            dxs = fine(m, dsplit, TN) + fine(b_parts, dend_parts, NN) * tail
+            grown = parts(dy * grow)
+            d_c = d_c + fine(grown, parts(before), NT)
+            d_b = d_b + fine(parts(xs * tail), dend_parts, NT)
+            dprev = dend * jnp.exp(last) + fine(c_parts, grown, TN)
             carry[:, tile] = dprev
             pick = jnp.where(lax.shift_right_logical(iota((heads, LANES), 1), 6) + 2 * j == iota((heads, LANES), 0), 1.0, 0.0)
-            balance = dy.astype(bf16).astype(f32) * y - xs16.astype(f32) * dxs
+            balance = dy * y - xs * dxs
             d_cum = d_cum + dot(pick, balance, NT, highest)
             d_step = d_step + dot(pick, x * dxs, NT, highest)
-            crossing = jnp.sum(dprev * before.astype(f32), axis=0, keepdims=True)
+            crossing = jnp.sum(dprev * before, axis=0, keepdims=True)
             reach = reach + dot(pick, jnp.broadcast_to(crossing, (8, LANES)), NT, highest)
             dact[rows, tile] = dxs * step + skip * dy
-        ds16 = dscores.astype(bf16)
-        dact[rows, din : din + NSTATE] = d_b + dot(ds16, c, TN)
-        dact[rows, din + NSTATE :] = d_c + dot(ds16, b, NN)
+        ds_parts = parts(dscores)
+        dact[rows, din : din + NSTATE] = d_b + fine(ds_parts, c_parts, TN)
+        dact[rows, din + NSTATE :] = d_c + fine(ds_parts, b_parts, NN)
         d_log = dot(d_cum, lower, NN, highest) + edge[...]
         edge[...] = jnp.broadcast_to(reach[:, 0:1], edge.shape)
         raw = raw_ref[:, rows] + head_ref[1]
@@ -301,7 +305,7 @@
             jax.ShapeDtypeStruct((length, din), f32),
             jax.ShapeDtypeStruct((length, din), f32),
             jax.ShapeDtypeStruct((length, d), bf16),
-            jax.ShapeDtypeStruct((length // SUB, NSTATE, din), bf16),
+            jax.ShapeDtypeStruct((length // SUB, NSTATE, din), f32),
             jax.ShapeDtypeStruct((8, length), f32),
         ],
         scratch_shapes=[
@@ -362,6 +366,577 @@
     )(proj, proj, raw, y, dg, sums, states, cot, conv, lanes, heads)
 
 
+MESH = pl.DeviceIdType.MESH
+
+
+def flip(index, bit):
+    return index + bit * (1 - 2 * (lax.div(index, bit) % 2))
+
+
+def flip_mask(index, mask, bits):
+    for bit in bits:
+        if mask & bit:
+            index = flip(index, bit)
+    return index
+
+
+def bits_of(size):
+    return [1 << k for k in range(size.bit_length() - 1)]
+
+
+def both_orders(size):
+    bits = bits_of(size)
+    slow = bits[1:]
+    return [slow + bits[:1], slow[::-1] + bits[:1]]
+
+
+def remote(src, dst, send, recv, to):
+    return pltpu.make_async_remote_copy(
+        src_ref=src, dst_ref=dst, send_sem=send, recv_sem=recv, device_id=to, device_id_type=MESH
+    )
+
+
+class Spread:
+    def __init__(self, buf, send, recv, own=None):
+        self.size = buf.shape[0]
+        self.bits = bits_of(self.size)
+        self.orders = both_orders(self.size)
+        self.buf, self.send, self.recv = buf, send, recv
+        self.me, self.dp = lax.axis_index("seq"), lax.axis_index("dp")
+        self.own = own
+
+    def masks(self, half):
+        order = self.orders[half]
+        got = [0]
+        for bit in order:
+            got = got + [m | bit for m in got]
+        return got
+
+    def copy(self, half, mask, bit):
+        origin = flip_mask(self.me, mask, self.bits)
+        dst = self.buf.at[origin, half]
+        src = self.own.at[half] if (mask == 0 and self.own is not None) else dst
+        slot = half * self.size + (mask | bit)
+        return remote(src, dst, self.send.at[slot], self.recv.at[slot], (self.dp, flip(self.me, bit)))
+
+    def start(self, half, mask):
+        order = self.orders[half]
+        after = max((order.index(b) for b in self.bits if mask & b), default=-1) + 1
+        for bit in order[after:]:
+            self.copy(half, mask, bit).start()
+
+    def arrive(self, half, mask):
+        order = self.orders[half]
+        top = order[max(order.index(b) for b in self.bits if mask & b)]
+        self.copy(half, mask & ~top, top).wait_recv()
+
+    def forward(self, group):
+        for k in range(1 << group, 2 << group):
+            for half in range(2):
+                mask = self.masks(half)[k]
+                self.arrive(half, mask)
+                self.start(half, mask)
+
+    def finish(self):
+        for half in range(2):
+            for mask in range(1, self.size):
+                order = self.orders[half]
+                top = order[max(order.index(b) for b in self.bits if mask & b)]
+                self.copy(half, mask & ~top, top).wait_send()
+
+    @property
+    def groups(self):
+        return len(self.bits)
+
+
+class Line:
+    def __init__(self, at, size, send, recv):
+        self.at, self.size, self.send, self.recv = at, size, send, recv
+        self.me, self.seq = lax.axis_index("dp"), lax.axis_index("seq")
+
+    def copy(self, way, hop):
+        block = self.me - way * (hop - 1)
+        slot = (self.size if way > 0 else 0) + hop
+        ref = self.at(block)
+        return remote(ref, ref, self.send.at[slot], self.recv.at[slot], (self.me + way, self.seq))
+
+    def sends(self, way, hop):
+        block = self.me - way * (hop - 1)
+        to = self.me + way
+        return (block >= 0) & (block < self.size) & (to >= 0) & (to < self.size)
+
+    def start(self, hop):
+        for way in (1, -1):
+            @pl.when(self.sends(way, hop))
+            def _():
+                self.copy(way, hop).start()
+
+    def arrive(self, hop):
+        for way in (1, -1):
+            source = self.me - way * hop
+            @pl.when((source >= 0) & (source < self.size))
+            def _():
+                ref = self.at(source)
+                slot = (self.size if way > 0 else 0) + hop
+                pltpu.make_async_copy(ref, ref, self.recv.at[slot]).wait()
+
+    def forward(self, hop):
+        self.arrive(hop)
+        if hop + 1 < self.size:
+            self.start(hop + 1)
+
+    def finish(self):
+        for hop in range(1, self.size):
+            for way in (1, -1):
+                @pl.when(self.sends(way, hop))
+                def _():
+                    self.copy(way, hop).wait_send()
+
+
+def greet(ranks, planes):
+    me, dp = lax.axis_index("seq"), lax.axis_index("dp")
+    barrier = pltpu.get_barrier_semaphore()
+    for mask in range(1, ranks):
+        pl.semaphore_signal(
+            barrier, inc=1, device_id=(dp, flip_mask(me, mask, bits_of(ranks))), device_id_type=MESH
+        )
+    for way in (1, -1):
+        @pl.when((dp + way >= 0) & (dp + way < planes))
+        def _():
+            pl.semaphore_signal(barrier, inc=1, device_id=(dp + way, me), device_id_type=MESH)
+    near = jnp.where(dp > 0, 1, 0) + jnp.where(dp < planes - 1, 1, 0)
+    pl.semaphore_wait(barrier, ranks - 1 + near)
+
+
+def gather_kernel(
+    tok_in, cot_in, w_in, wout_in, common_in,
+    tok, cot, w, wout, common,
+    stage, tok_s, tok_r, cot_s, cot_r, com_s, com_r, wz_s, wz_r, oz_s, oz_r, cz_s, cz_r,
+    a2a_s, a2a_r, mix_s, mix_r, local,
+):
+    ranks, planes = tok.shape[0], w.shape[0]
+    me, dp = lax.axis_index("seq"), lax.axis_index("dp")
+    bits = bits_of(ranks)
+    greet(ranks, planes)
+    half = planes // 2
+    tokens = Spread(tok, tok_s, tok_r, tok_in)
+    cots = Spread(cot, cot_s, cot_r, cot_in)
+    commons = Spread(common, com_s, com_r)
+    w_line = Line(lambda d: w.at[d], planes, wz_s, wz_r)
+    o_line = Line(lambda d: stage.at[d], planes, oz_s, oz_r)
+    c_line = Line(lambda d: common.at[me, lax.div(d, half), d % half], planes, cz_s, cz_r)
+
+    def exchange(mask):
+        peer = flip_mask(me, mask, bits)
+        return remote(w_in.at[peer], w.at[dp, me], a2a_s.at[mask], a2a_r.at[mask], (dp, peer))
+
+    def arrived(mask):
+        ref = w.at[dp, flip_mask(me, mask, bits)]
+        return pltpu.make_async_copy(ref, ref, a2a_r.at[mask])
+
+    for mask in range(1, ranks):
+        exchange(mask).start()
+    places = [
+        pltpu.make_async_copy(w_in.at[me], w.at[dp, me], local.at[0]),
+        pltpu.make_async_copy(common_in, common.at[me, lax.div(dp, half), dp % half], local.at[1]),
+        pltpu.make_async_copy(wout_in, stage.at[dp], local.at[2]),
+        pltpu.make_async_copy(tok_in, tok.at[me], local.at[3]),
+        pltpu.make_async_copy(cot_in, cot.at[me], local.at[4]),
+    ]
+    for place in places:
+        place.start()
+    for h in range(2):
+        tokens.start(h, 0)
+    for place in places:
+        place.wait()
+    c_line.start(1)
+    o_line.start(1)
+    for mask in range(1, ranks):
+        arrived(mask).wait()
+    w_line.start(1)
+    for hop in range(1, planes):
+        c_line.forward(hop)
+    tokens.forward(0)
+    for h in range(2):
+        commons.start(h, 0)
+    w_line.forward(1)
+    for group in range(1, tokens.groups - 1):
+        tokens.forward(group)
+    for hop in range(2, planes - 1):
+        w_line.forward(hop)
+    commons.forward(0)
+    for h in range(2):
+        cots.start(h, 0)
+    tokens.forward(tokens.groups - 1)
+    for group in range(1, commons.groups):
+        commons.forward(group)
+    o_line.forward(1)
+    w_line.forward(planes - 1)
+    cots.forward(0)
+    for hop in range(2, planes):
+        o_line.forward(hop)
+
+    def moved(d):
+        index = d * ranks + me
+        return lax.div(index, planes), index % planes
+
+    for d in range(planes):
+        to, place = moved(d)
+
+        @pl.when(to == me)
+        def _():
+            pltpu.make_async_copy(stage.at[d], wout.at[place], mix_r.at[place]).start()
+
+        @pl.when(to != me)
+        def _():
+            remote(stage.at[d], wout.at[place], mix_s.at[d], mix_r.at[place], (dp, to)).start()
+
+    for group in range(1, cots.groups):
+        cots.forward(group)
+    for place in range(planes):
+        pltpu.make_async_copy(wout.at[place], wout.at[place], mix_r.at[place]).wait()
+    for d in range(planes):
+        to, place = moved(d)
+
+        @pl.when(to != me)
+        def _():
+            remote(stage.at[d], wout.at[place], mix_s.at[d], mix_r.at[place], (dp, to)).wait_send()
+
+    for mask in range(1, ranks):
+        exchange(mask).wait_send()
+    for ring in (tokens, cots, commons, w_line, o_line, c_line):
+        ring.finish()
+
+
+def gather_all(ranks, planes, tok, cot, w, w_out, common):
+    length, d = tok.shape
+    halves = (2, length // 2, d)
+    dma = pltpu.SemaphoreType.DMA
+    vmem = pl.BlockSpec(memory_space=pltpu.VMEM)
+    ring, line = 2 * ranks, 2 * planes
+    out = [
+        (ranks,) + halves, (ranks,) + halves, (planes,) + w.shape, (planes,) + w_out.shape,
+        (ranks, 2, planes // 2) + common.shape,
+    ]
+    tok_all, cot_all, w_all, out_all, common_all = pl.pallas_call(
+        gather_kernel,
+        in_specs=[pl.BlockSpec(memory_space=pl.ANY)] * 5,
+        out_specs=[vmem] * 5,
+        out_shape=[jax.ShapeDtypeStruct(s, bf16) for s in out],
+        scratch_shapes=[pltpu.VMEM((planes,) + w_out.shape, bf16)]
+        + [dma((ring,))] * 6
+        + [dma((line,))] * 6
+        + [dma((ranks,)), dma((ranks,)), dma((planes,)), dma((planes,)), dma((5,))],
+        compiler_params=pltpu.CompilerParams(collective_id=0, has_side_effects=True),
+        name="gather_all",
+    )(tok.reshape(halves), cot.reshape(halves), w, w_out, common)
+    rows = common.shape[0]
+    return (
+        tok_all.reshape(ranks * length, d),
+        cot_all.reshape(ranks * length, d),
+        w_all.reshape(planes * ranks * w.shape[1], w.shape[2]),
+        out_all.reshape(planes * w_out.shape[0], d),
+        common_all.reshape(ranks, planes, rows, common.shape[1]).transpose(1, 0, 2, 3),
+    )
+
+
+def add_into(dst, pieces, rows):
+    count = dst.shape[-2]
+
+    def body(i, _):
+        at = pl.ds(pl.multiple_of(i * rows, rows), rows)
+        total = pieces[0][at, :].astype(f32)
+        for piece in pieces[1:]:
+            total = total + piece[at, :].astype(f32)
+        dst[at, :] = total.astype(dst.dtype)
+        return 0
+
+    lax.fori_loop(0, count // rows, body, 0)
+
+
+def flat_views(ref):
+    if len(ref.shape) == 2:
+        return [ref]
+    return [view for k in range(ref.shape[0]) for view in flat_views(ref.at[k])]
+
+
+def add_all(dst, pieces, rows):
+    for views in zip(flat_views(dst), *(flat_views(p) for p in pieces)):
+        add_into(views[0], views[1:], rows)
+
+
+class Collect:
+    def __init__(self, acc, land, send, recv, rows):
+        self.size = acc.shape[0]
+        self.bits = bits_of(self.size)
+        self.orders = both_orders(self.size)
+        self.acc, self.land, self.send, self.recv, self.rows = acc, land, send, recv, rows
+        self.me, self.dp = lax.axis_index("seq"), lax.axis_index("dp")
+
+    def copy(self, half, mask, bit):
+        slot = half * (self.size - 1) + (mask | bit) - 1
+        owner = flip_mask(self.me, mask | bit, self.bits)
+        return remote(
+            self.acc.at[owner, half], self.land.at[slot], self.send.at[slot], self.recv.at[slot],
+            (self.dp, flip(self.me, bit)),
+        )
+
+    def subsets(self, bits):
+        got = [0]
+        for bit in bits:
+            got = got + [m | bit for m in got]
+        return got
+
+    def arrivals(self, half, mask, after):
+        pieces = []
+        for bit in self.orders[half][after:]:
+            slot = half * (self.size - 1) + (mask | bit) - 1
+            pltpu.make_async_copy(self.land.at[slot], self.land.at[slot], self.recv.at[slot]).wait()
+            pieces.append(self.land.at[slot])
+        return pieces
+
+    def push(self, k):
+        for half in range(2):
+            order = self.orders[half]
+            for mask in self.subsets(order[:k]):
+                full = mask | order[k]
+                pieces = self.arrivals(half, full, k + 1)
+                if pieces:
+                    ref = self.acc.at[flip_mask(self.me, full, self.bits), half]
+                    add_all(ref, [ref] + pieces, self.rows)
+                self.copy(half, mask, order[k]).start()
+
+    def total(self, dst):
+        for half in range(2):
+            pieces = self.arrivals(half, 0, 0)
+            add_all(dst.at[half], [self.acc.at[self.me, half]] + pieces, self.rows)
+
+    def finish(self):
+        for half in range(2):
+            order = self.orders[half]
+            for k in range(len(order)):
+                for mask in self.subsets(order[:k]):
+                    self.copy(half, mask, order[k]).wait_send()
+
+
+class Fold:
+    def __init__(self, at, land, size, send, recv, rows):
+        self.at, self.land, self.size, self.send, self.recv, self.rows = at, land, size, send, recv, rows
+        self.me, self.seq = lax.axis_index("dp"), lax.axis_index("seq")
+
+    def copy(self, way, block):
+        slot = (self.size if way > 0 else 0) + block
+        return remote(
+            self.at(block), self.land.at[slot], self.send.at[slot], self.recv.at[slot], (self.me + way, self.seq)
+        )
+
+    def landed(self, way, block):
+        slot = (self.size if way > 0 else 0) + block
+        ref = self.land.at[slot]
+        pltpu.make_async_copy(ref, ref, self.recv.at[slot]).wait()
+        return ref
+
+    def sends(self, way, block):
+        return block > self.me if way > 0 else block < self.me
+
+    def push(self, t):
+        for way, block in ((1, self.size - 1 - t), (-1, t)):
+            @pl.when(self.sends(way, block))
+            def _():
+                behind = self.me - way
+
+                @pl.when((behind >= 0) & (behind < self.size))
+                def _():
+                    add_all(self.at(block), [self.at(block), self.landed(way, block)], self.rows)
+
+                self.copy(way, block).start()
+
+    def total(self, dst):
+        me = self.me
+        add_all(dst, [self.at(me)], self.rows)
+        for way in (1, -1):
+            behind = me - way
+
+            @pl.when((behind >= 0) & (behind < self.size))
+            def _():
+                add_all(dst, [dst, self.landed(way, me)], self.rows)
+
+    def finish(self):
+        for t in range(self.size):
+            for way in (1, -1):
+                @pl.when(self.sends(way, t))
+                def _():
+                    self.copy(way, t).wait_send()
+
+
+def reduce_kernel(
+    out_in, dn_in, w_in, o_in, c_in, s_in,
+    out_sum, dn_sum, w_sum, o_sum, c_sum, s_sum,
+    out_acc, dn_acc, w_acc, c_acc, s_acc, stage, own,
+    out_land, dn_land, w_land, o_land, c_land, s_land, cz_land, sz_land,
+    out_s, out_r, dn_s, dn_r, cr_s, cr_r, sr_s, sr_r,
+    wz_s, wz_r, oz_s, oz_r, cz_s, cz_r, sz_s, sz_r,
+    a2a_s, a2a_r, mix_s, mix_r, local,
+):
+    ranks, planes = out_in.shape[0], w_in.shape[0]
+    me, dp = lax.axis_index("seq"), lax.axis_index("dp")
+    bits = bits_of(ranks)
+    half = planes // 2
+    greet(ranks, planes)
+    loads = [
+        pltpu.make_async_copy(src, dst, local.at[k])
+        for k, (src, dst) in enumerate(
+            [(w_in, w_acc), (out_in, out_acc), (c_in, c_acc), (s_in, s_acc), (dn_in, dn_acc)]
+        )
+    ]
+    for load in loads:
+        load.start()
+    outs = Collect(out_acc, out_land, out_s, out_r, 16)
+    dns = Collect(dn_acc, dn_land, dn_s, dn_r, 16)
+    cs = Collect(c_acc, c_land, cr_s, cr_r, c_acc.shape[-2])
+    ss = Collect(s_acc, s_land, sr_s, sr_r, 8)
+    w_fold = Fold(lambda d: w_acc.at[d], w_land, planes, wz_s, wz_r, w_acc.shape[-2])
+    o_fold = Fold(lambda d: stage.at[d], o_land, planes, oz_s, oz_r, o_in.shape[1])
+    c_fold = Fold(lambda d: own_c(d), cz_land, planes, cz_s, cz_r, c_acc.shape[-2])
+    s_fold = Fold(lambda d: own_s(d), sz_land, planes, sz_s, sz_r, 8)
+
+    def own_c(d):
+        return c_acc.at[me, lax.div(d, half), d % half]
+
+    def own_s(d):
+        return s_acc.at[me, lax.div(d, half), d % half]
+
+    def moved(k):
+        index = me * planes + k
+        return lax.div(index, ranks), index % ranks
+
+    loads[0].wait()
+    w_fold.push(0)
+    for load in loads[1:]:
+        load.wait()
+    top = len(bits) - 1
+    outs.push(top)
+    dns.push(top)
+    cs.push(top)
+    ss.push(top)
+    for k in range(planes):
+        to_plane, to = moved(k)
+
+        @pl.when(to == me)
+        def _():
+            pltpu.make_async_copy(o_in.at[k], stage.at[to_plane], mix_r.at[to_plane]).start()
+
+        @pl.when(to != me)
+        def _():
+            remote(o_in.at[k], stage.at[to_plane], mix_s.at[k], mix_r.at[to_plane], (dp, to)).start()
+
+    for k in reversed(range(top)):
+        cs.push(k)
+        ss.push(k)
+    for k in reversed(range(1, top)):
+        dns.push(k)
+    c_rows = [c_acc.at[me, k] for k in range(2)]
+    for h in range(2):
+        for ring in (cs, ss):
+            pieces = ring.arrivals(h, 0, 0)
+            ref = ring.acc.at[me, h]
+            add_all(ref, [ref] + pieces, ring.rows)
+    for t in range(planes - 1):
+        c_fold.push(t)
+        s_fold.push(t)
+    dns.push(0)
+    for k in reversed(range(1, top)):
+        outs.push(k)
+    w_fold.push(1)
+    for d in range(planes):
+        pltpu.make_async_copy(stage.at[d], stage.at[d], mix_r.at[d]).wait()
+    o_fold.push(0)
+    for t in range(2, planes - 1):
+        w_fold.push(t)
+    outs.push(0)
+    for t in range(1, planes - 1):
+        o_fold.push(t)
+    w_fold.total(own)
+
+    def exchange(mask):
+        peer = flip_mask(me, mask, bits)
+        return remote(own.at[peer], w_sum.at[me], a2a_s.at[mask], a2a_r.at[mask], (dp, peer))
+
+    for mask in range(1, ranks):
+        exchange(mask).start()
+    keep = pltpu.make_async_copy(own.at[me], w_sum.at[me], local.at[0])
+    keep.start()
+    dns.total(dn_sum)
+    c_fold.total(c_sum)
+    s_fold.total(s_sum)
+    outs.total(out_sum)
+    o_fold.total(o_sum)
+    keep.wait()
+    for mask in range(1, ranks):
+        ref = w_sum.at[flip_mask(me, mask, bits)]
+        pltpu.make_async_copy(ref, ref, a2a_r.at[mask]).wait()
+    for mask in range(1, ranks):
+        exchange(mask).wait_send()
+    for k in range(planes):
+        to_plane, to = moved(k)
+
+        @pl.when(to != me)
+        def _():
+            remote(o_in.at[k], stage.at[to_plane], mix_s.at[k], mix_r.at[to_plane], (dp, to)).wait_send()
+
+    for ring in (outs, dns, cs, ss, w_fold, o_fold, c_fold, s_fold):
+        ring.finish()
+
+
+def reduce_all(ranks, planes, out_part, dn_part, w, w_out, common, small):
+    length, d = out_part.shape[0] // ranks, out_part.shape[1]
+    part = (2, length // 2, d)
+    rows, cols = w.shape[2:]
+    dma = pltpu.SemaphoreType.DMA
+    vmem = pl.BlockSpec(memory_space=pltpu.VMEM)
+    cpart, spart = common.shape[1:], small.shape[1:]
+    ring, line = 2 * (ranks - 1), 2 * planes
+    results = pl.pallas_call(
+        reduce_kernel,
+        in_specs=[pl.BlockSpec(memory_space=pl.ANY)] * 6,
+        out_specs=[vmem] * 6,
+        out_shape=[
+            jax.ShapeDtypeStruct(part, f32),
+            jax.ShapeDtypeStruct(part, f32),
+            jax.ShapeDtypeStruct((ranks, rows, cols), bf16),
+            jax.ShapeDtypeStruct(w_out.shape[1:], f32),
+            jax.ShapeDtypeStruct(cpart[2:], f32),
+            jax.ShapeDtypeStruct(spart[2:], f32),
+        ],
+        scratch_shapes=[
+            pltpu.VMEM((ranks,) + part, bf16),
+            pltpu.VMEM((ranks,) + part, bf16),
+            pltpu.VMEM(w.shape, bf16),
+            pltpu.VMEM(common.shape, bf16),
+            pltpu.VMEM(small.shape, f32),
+            pltpu.VMEM(w_out.shape, bf16),
+            pltpu.VMEM(w.shape[1:], bf16),
+            pltpu.VMEM((ring,) + part[1:], bf16),
+            pltpu.VMEM((ring,) + part[1:], bf16),
+            pltpu.VMEM((line,) + w.shape[1:], bf16),
+            pltpu.VMEM((line,) + w_out.shape[1:], bf16),
+            pltpu.VMEM((ring,) + cpart[1:], bf16),
+            pltpu.VMEM((ring,) + spart[1:], f32),
+            pltpu.VMEM((line,) + cpart[2:], bf16),
+            pltpu.VMEM((line,) + spart[2:], f32),
+        ]
+        + [dma((ring,))] * 8
+        + [dma((line,))] * 8
+        + [dma((ranks,)), dma((ranks,)), dma((planes,)), dma((planes,)), dma((5,))],
+        compiler_params=pltpu.CompilerParams(
+            collective_id=1, has_side_effects=True, vmem_limit_bytes=67043328
+        ),
+        name="reduce_all",
+    )(out_part.reshape((ranks,) + part), dn_part.reshape((ranks,) + part), w, w_out, common, small)
+    out_sum, dn_sum, w_sum, o_sum, c_sum, s_sum = results
+    return out_sum.reshape(length, d), dn_sum.reshape(length, d), w_sum, o_sum, c_sum, s_sum
+
+
 def rms_scale(values, gain):
     mean_sq = jnp.mean(values * values, axis=-1, keepdims=True)
     return values * lax.rsqrt(mean_sq + epsilon) * gain
@@ -400,29 +975,33 @@
     def mine(array, size, axis=0):
         return lax.dynamic_slice_in_dim(array, me * size, size, axis)
 
+    planes = lax.axis_size("dp")
     x_own = tokens[0].astype(f32)
-    tok = lax.all_gather(tokens[0], "seq", axis=0, tiled=True)
-    cot = lax.all_gather(cotangent[0], "seq", axis=0, tiled=True)
     send = jnp.concatenate(
         [
             widen(in_weight[:, :din_all].reshape(rows, ranks, din), padded, 2),
             widen(in_weight[:, din_all : 2 * din_all].reshape(rows, ranks, din), padded, 2),
-            jnp.broadcast_to(
-                in_weight[:, None, 2 * din_all : 2 * din_all + 2 * NSTATE], (rows, ranks, 2 * NSTATE)
-            ),
             widen(in_weight[:, din_all + conv_all :].reshape(rows, ranks, heads), 8, 2),
         ],
         axis=2,
     ).transpose(1, 0, 2)
-    cols = send.shape[2]
-    got = lax.all_to_all(send, "seq", 0, 0)
-    w_all = lax.all_gather(got.reshape(ranks * rows, cols), "dp", axis=0, tiled=True)
-    w_in, w_dt = w_all[:, :main], w_all[:, main:].T
-    w_out = widen(mine(lax.all_gather(out_weight, both, axis=0, tiled=True), din), padded, 0)
-    conv_w, conv_b, gain_norm, gain_gate = (
-        lax.all_gather(a, both, axis=0, tiled=True).astype(f32)
-        for a in (conv_weight, conv_bias, norm_gain, gate_gain)
+    small = [norm_gain, gate_gain, conv_weight.reshape(-1), conv_bias]
+    sizes = [a.shape[0] for a in small]
+    packed = widen(jnp.concatenate(small), rows * LANES, 0).reshape(rows, LANES)
+    shared = in_weight[:, 2 * din_all : 2 * din_all + 2 * NSTATE]
+    common = jnp.concatenate([shared, packed], axis=1)
+    tok, cot, w_all, w_out, common = gather_all(
+        ranks, planes, tokens[0], cotangent[0], send, out_weight, common
     )
+    shared = common[..., : 2 * NSTATE].reshape(-1, 2 * NSTATE)
+    w_in = jnp.concatenate([w_all[:, : 2 * padded], shared], axis=1)
+    w_dt = w_all[:, 2 * padded :].T
+    w_out = widen(w_out, padded, 0)
+    packed = common[..., 2 * NSTATE :].reshape(ranks * planes, rows * LANES).astype(f32)
+    gain_norm, gain_gate, conv_w, conv_b = (
+        packed[:, sum(sizes[:k]) : sum(sizes[: k + 1])].reshape(-1) for k in range(4)
+    )
+    conv_w = conv_w.reshape(-1, CONVK)
     taps = jnp.concatenate([conv_w.T, conv_b[None], jnp.zeros((8 - CONVK - 1, conv_all), f32)], axis=0)
     conv = jnp.concatenate([widen(mine(taps, din, 1), padded, 1), taps[:, din_all:]], axis=1)
     rate, bias, skip = (mine(a, heads) for a in (decay_rate, dt_bias, d_skip))
@@ -435,53 +1014,66 @@
     raw = dot(w_dt, normed, NT).astype(bf16).astype(f32)
     y, dg, out_part, states, sums = mixer_forward(proj, raw, cot, w_out, conv, lanes, head_rows)
     sums = lax.psum(sums, "seq")
-    out_sum = lax.psum_scatter(out_part, "seq", scatter_dimension=0, tiled=True)
     d_proj, d_raw, d_w_out, d_conv, d_lane, d_head = mixer_backward(
         din_all, proj, raw, y, dg, sums, states, cot, conv, lanes, head_rows
     )
-    own = mine(sums[0], x_own.shape[0])[:, None]
-    block_out = (x_own + lax.rsqrt(own / din_all + epsilon) * out_sum.astype(f32)).astype(bf16)
     d_raw16 = d_raw.astype(bf16)
-    d_normed_part = (dot(d_proj, w_in, NT) + dot(d_raw16, w_dt, TN)).astype(bf16)
-    d_normed = lax.psum_scatter(d_normed_part, "seq", scatter_dimension=0, tiled=True).astype(f32)
-    d_w_in = jnp.concatenate([dot(normed, d_proj, TN), dot(normed, d_raw16, ((0,), (1,)))], axis=1).astype(bf16)
-
-    _, norm_back = jax.vjp(rms_scale, x_own, gain_norm)
-    d_xn, d_g1 = norm_back(d_normed)
-    grad_x = cotangent[0].astype(f32) + d_xn
-
-    d_w_in = lax.psum_scatter(d_w_in, "dp", scatter_dimension=0, tiled=True)
-    d_w_in = lax.all_to_all(d_w_in.reshape(ranks, rows, cols), "seq", 0, 0).astype(f32)
-    spread = d_w_in.transpose(1, 0, 2)
-    grad_in = jnp.concatenate(
-        [
-            spread[:, :, :din].reshape(rows, din_all),
-            spread[:, :, padded : padded + din].reshape(rows, din_all),
-            jnp.sum(spread[:, :, 2 * padded : main], axis=1),
-            spread[:, :, main : main + heads].reshape(rows, heads * ranks),
-        ],
-        axis=1,
-    )
-    full_out = lax.dynamic_update_slice_in_dim(
-        jnp.zeros((din_all, w_out.shape[1]), bf16), d_w_out[:din].astype(bf16), me * din, 0
-    )
-    grad_out = lax.psum_scatter(full_out, both, scatter_dimension=0, tiled=True).astype(f32)
+    d_normed_part = dot(d_proj, w_in, NT) + dot(d_raw16, w_dt, TN)
+    x_hat = tok.astype(f32)
+    x_hat = x_hat * lax.rsqrt(jnp.mean(x_hat * x_hat, axis=1, keepdims=True) + epsilon)
+    d_g1 = jnp.sum(d_normed_part * x_hat, axis=0)
+    d_w = dot(normed, d_proj, TN).astype(bf16)
+    d_wdt = dot(normed, d_raw16, ((0,), (1,))).astype(bf16)
+    d_w_main = jnp.concatenate([d_w[:, : 2 * padded], d_wdt], axis=1).reshape(planes, ranks, rows, -1)
+
+    def by_owner(array):
+        split = array.reshape((2, planes // 2, ranks) + array.shape[1:])
+        return split.transpose((2, 0, 1) + tuple(range(3, split.ndim)))
 
     def place(own, size):
         return lax.dynamic_update_slice_in_dim(
             jnp.zeros((size * ranks,) + own.shape[1:], f32), own, me * size, 0
         )
 
+    d_bc = d_w[:, 2 * padded :].reshape(planes * ranks, rows, 2 * NSTATE)
     d_cw, d_cb = d_conv[:CONVK].T, d_conv[CONVK]
     full_cw = jnp.concatenate([place(d_cw[:din], din), d_cw[padded:]], axis=0)
     full_cb = jnp.concatenate([place(d_cb[:din], din), d_cb[padded:]], axis=0)
     d_skp = jnp.sum(d_lane[0, :din].reshape(heads, HDIM), axis=1)
     d_rate, d_bias = jnp.sum(d_head, axis=2)[:, :heads]
-    g_cw, g_cb, g_gain, g_gate = (
-        lax.psum_scatter(a, both, scatter_dimension=0, tiled=True)
-        for a in (full_cw, full_cb, d_g1, place(d_lane[1, :din], din))
+    devices = planes * ranks
+    head_part = jnp.concatenate([place(a, heads) for a in (d_rate, d_bias, d_skp)])
+    fields = [
+        a.reshape(devices, -1) for a in (full_cw, full_cb, d_g1, place(d_lane[1, :din], din))
+    ] + [jnp.broadcast_to(head_part, (devices,) + head_part.shape)]
+    ends = [0]
+    for a in fields:
+        ends.append(ends[-1] + a.shape[1])
+    small = widen(jnp.concatenate(fields, axis=1), 8 * LANES, 1).reshape(devices, 8, LANES)
+    out_sum, d_normed, w_sum, grad_out, bc_sum, small_sum = reduce_all(
+        ranks, planes, out_part, d_normed_part.astype(bf16), d_w_main,
+        d_w_out[:din].astype(bf16).reshape(planes, -1, d_w_out.shape[1]), by_owner(d_bc), by_owner(small),
     )
-    head_sums = lax.psum([place(a, heads) for a in (d_rate, d_bias, d_skp)], both)
+    own = mine(sums[0], x_own.shape[0])[:, None]
+    block_out = (x_own + lax.rsqrt(own / din_all + epsilon) * out_sum).astype(bf16)
+    gain = gain_norm * d_normed
+    inv = lax.rsqrt(jnp.mean(x_own * x_own, axis=1, keepdims=True) + epsilon)
+    d_xn = inv * (gain - x_own * (inv * inv * jnp.mean(gain * x_own, axis=1, keepdims=True)))
+    grad_x = cotangent[0].astype(f32) + d_xn
+    spread = w_sum.astype(f32).transpose(1, 0, 2)
+    grad_in = jnp.concatenate(
+        [
+            spread[:, :, :din].reshape(rows, din_all),
+            spread[:, :, padded : padded + din].reshape(rows, din_all),
+            bc_sum,
+            spread[:, :, 2 * padded : 2 * padded + heads].reshape(rows, heads * ranks),
+        ],
+        axis=1,
+    )
+    small_sum = small_sum.reshape(-1)
+    g_cw, g_cb, g_gain, g_gate, head_sums = (small_sum[a:b] for a, b in zip(ends[:-1], ends[1:]))
+    g_cw = g_cw.reshape(-1, CONVK)
+    head_sums = head_sums.reshape(3, -1)
     return (
         block_out[None],
         grad_x[None],

time: 885 us -> 483 us (0.55)
  waiting for transfers between devices: 600 us -> 53.3 us
  Pallas kernels: 66.9 us -> 307 us
  blocking collectives: 108 us -> 0 us
    reduce_scatter x4 -> x0, waiting for transfers between devices: 283 us -> none  [the longest x1 138 us: per_device(): lax.psum_scatter(full_out, both, scatter_dimension=0, tiled=True)]
    pallas_call x0 -> x2, Pallas kernels: none -> 228 us  [the longest x1 130 us: reduce_all(): pl.pallas_call(reduce_kernel, in_specs=[pl.BlockSpec(memory_space=pl.ANY)...]
    unnamed x11 -> x1, waiting for transfers between devices: 132 us -> 0.02 us
    all_gather x4 -> x0, waiting for transfers between devices: 118 us -> none  [the longest x1 66 us: per_device(): lax.all_gather(out_weight, both, axis=0, tiled=True)]
    all_gather x1 -> x0, blocking collectives: 42.4 us -> none  [per_device(): lax.all_gather(a, both, axis=0, tiled=True).astype(f32)]
    unnamed x1 -> x0, blocking collectives: 40.6 us -> none
    all_to_all x1 -> x0, blocking collectives: 25 us -> none  [per_device(): got = lax.all_to_all(send, 'seq', 0, 0)]
    all_to_all x1 -> x0, waiting for transfers between devices: 13.6 us -> none  [per_device(): lax.all_to_all(d_w_in.reshape(ranks, rows, cols), 'seq', 0, 0).astype(f32)]
  transfers between devices with their start and end apart: 11 -> 1, of which waited for: 10 -> 1; matrix products, arithmetic and copies ran while one was open for 8% -> 0% of each run, Pallas kernels for 0% -> 0%
where the time goes in v2:
time: 483 us; the launch traced here: 478 us
  Pallas kernels  307 us (64%)
  waiting for transfers between devices  53.3 us (11%)
  matrix products  47.3 us (10%)
  local copies, waits for them, and re-layouts  34.6 us (7%)
  other arithmetic  21.2 us (4%)
  between operations  14.5 us (3%)
    pallas_call x1, Pallas kernels, reduce_all(): pl.pallas_call(reduce_kernel, in_specs=[pl.BlockSpec(memory_space=pl.ANY)...  130 us
    pallas_call x1, Pallas kernels, gather_all(): pl.pallas_call(gather_kernel, in_specs=[pl.BlockSpec(memory_space=pl.ANY)...  97.7 us
    psum x1, waiting for transfers between devices, per_device(): sums = lax.psum(sums, 'seq')  53.3 us
    pallas_call x1, Pallas kernels, mixer_backward(): pl.pallas_call(partial(bwd_kernel, total_din), grid=(length // block,), i...  48.9 us
    dot_general x6, matrix products, dot(): lax.dot_general(a, b, (dims, ((), ())), preferred_element_type=f32, preci...  47.3 us
    pallas_call x1, Pallas kernels, mixer_forward(): pl.pallas_call(fwd_kernel, grid=(length // block,), in_specs=[rows_spec(b...  30.2 us
  transfers between devices with their start and end apart: 1, of which 1 were waited for; matrix products, arithmetic and copies ran while one was open for 0% of the time, Pallas kernels for 0%

profile of v2, /device:TPU:0, one launch (start us, length us, event | category | flops | bytes accessed | tf_op | source)
XLA Modules:
  0.0 477.8 jit_solution(9271261533518447650)
XLA Ops:
  7.2 1.1 fusion.24
  8.3 0.7 slice.123
  9.0 0.7 slice.124
  10.0 0.8 copy.62
  11.0 0.8 fusion.21
  11.8 0.6 pad_maximum_fusion.6.common_in
  12.4 0.9 fusion.9.w_in
  13.3 97.7 %gather_all.1 = (bf16[8,2,128,1536]{3,2,1,0:T(8,128)(2,1)}, bf16[8,2,128,1536]{3,2,1,0:T(8,128)(2,1)}, bf16[4,8,48,776]{3,2,1,0:T(8,128)(2,1)}, bf16[4,96,1536]{2,1,0:T(8,128)(2,1)}, bf16[8,2,2,48,384]{4,3,2,1,0:T(8,128)(2,1)}) custom-call(bf16[2,128,1536]{2,1,0:T(8,128)(2,1)} %bitcast.100, bf16[2,128,1536]{2,1,0:T(8,128)(2,1)} %bitcast.113, ...), custom_call_target="tpu_custom_call" | custom-call | tf_op jit(solution)/shard_map/gather_all/pallas_call | solution.py:621
  111.1 1.4 copy.86
  114.5 4.3 multiply_reduce_fusion.1
  118.8 3.3 slice.159
  122.1 1.5 multiply_convert_fusion
  123.6 2.6 copy-done
  126.2 3.5 fusion.raw_ref
  130.2 0.6 pad_maximum_fusion.7.conv_ref
  130.8 11.4 %convolution_convert_fusion.1.proj_ref.rim_ref = bf16[2048,1024]{1,0:T(8,128)(2,1)} fusion(bf16[2048,1536]{1,0:T(8,128)(2,1)} %copy-done, bf16[1536,256]{1,0:T(8,128)(2,1)S(1)} %bitcast.125, bf16[1536,768]{1,0:T(8,128)(2,1)S(1)} %copy-done.7), kind=kOutput, calls=%fused_computation.6 | convolution fusion | flops 6450839552 | bytes 13631488 | tf_op jit(solution)/shard_map/dot_general | solution.py:25
  142.2 0.6 select_maximum_fusion.lane_ref
  142.9 0.7 broadcast_in_dim.12.head_ref
  143.6 30.2 %mix_forward.1 = (f32[2048,384]{1,0:T(8,128)}, f32[2048,384]{1,0:T(8,128)}, bf16[2048,1536]{1,0:T(8,128)(2,1)}, f32[16,128,384]{2,1,0:T(8,128)}, f32[8,2048]{1,0:T(8,128)}) custom-call(bf16[2048,1024]{1,0:T(8,128)(2,1)} %convolution_convert_fusion.1.proj_ref.rim_ref, f32[8,2048]{1,0:T(8,128)} %fusion.raw_ref, bf16[2048,1536]{1,0:T(8,128)(2,1)} %bitcast.97, ...), custom_call_target="tpu_custom_call" | custom-call | tf_op jit(solution)/shard_map/mix_forward/pallas_call | solution.py:293
  173.8 0.8 fusion.3
  174.6 53.3 %all-reduce.7.cloned.1.call-done.sum_ref = f32[8,2048]{1,0:T(8,128)} async-done(((f32[8,2048]{1,0:T(8,128)}), f32[8,2048]{1,0:T(8,128)}) %all-reduce.7.cloned.1.call-update) | async-done | bytes 65552 | tf_op jit(solution)/shard_map/psum | solution.py:1016
  227.8 48.9 %mix_backward.1 = (bf16[2048,1024]{1,0:T(8,128)(2,1)}, f32[8,2048]{1,0:T(8,128)}, f32[384,1536]{1,0:T(8,128)}, f32[8,640]{1,0:T(8,128)}, f32[8,384]{1,0:T(8,128)}, /*index=5*/f32[2,8,128]{2,1,0:T(8,128)}) custom-call(bf16[2048,1024]{1,0:T(8,128)(2,1)} %convolution_convert_fusion.1.proj_ref.rim_ref, ...), custom_call_target="tpu_custom_call" | custom-call | tf_op jit(solution)/shard_map/mix_backward/pallas_call | solution.py:334
  276.8 0.7 slice_reduce_fusion.2
  277.5 0.7 slice.142
  278.2 0.7 slice_bitcast_fusion.2
  278.9 12.6 %fusion.1 = f32[2048,1536]{1,0:T(8,128)} fusion(bf16[2048,1024]{1,0:T(8,128)(2,1)} %get-tuple-element.43, bf16[1536,256]{1,0:T(8,128)(2,1)S(1)} %bitcast.126, bf16[1536,768]{1,0:T(8,128)(2,1)} %slice.159), kind=kOutput, calls=%fused_computation.15 | convolution fusion | flops 6448742400 | bytes 19922944 | tf_op jit(solution)/shard_map/dot_general | solution.py:25
  291.6 7.2 %convolution_convert_fusion = bf16[1536,1024]{1,0:T(8,128)(2,1)S(1)} fusion(bf16[2048,1536]{1,0:T(8,128)(2,1)S(1)} %bitcast.92, bf16[2048,1024]{1,0:T(8,128)(2,1)S(1)} %copy-done.19), kind=kOutput, calls=%fused_computation.5 | convolution fusion | flops 6444023808 | bytes 13631488 | tf_op jit(solution)/shard_map/dot_general | solution.py:25
  298.8 1.8 slice.167
  300.6 0.6 copy-done.5
  301.2 0.8 slice_reduce_fusion
  302.8 1.8 copy.67
  304.6 1.9 reshape.276
  306.6 4.5 convolution_convert_fusion.3
  311.0 8.0 %multiply_reduce_fusion = (f32[1536]{0:T(1024)S(1)}, bf16[2048,1536]{1,0:T(8,128)(2,1)}) fusion(bf16[8,2,128,1536]{3,2,1,0:T(8,128)(2,1)S(1)} %bitcast.96, f32[2048]{0:T(1024)S(1)} %bitcast.131, f32[2048,1536]{1,0:T(8,128)} %fusion.1, bf16[1536,776]{1,0:T(8,128)(2,1)} %bitcast.110, f32[8,2048]{1,0:T(8,128)S(1)} %copy-done.10), kind=kOutput, calls=%fused_computation.1 | convolution fusion | flops 69220864 | bytes 25638912 | tf_op jit(solution)/shard_map/dot_general | solution.py:25
  320.1 0.7 copy.89
  320.8 1.0 copy.65
  321.8 1.0 copy.88
  322.8 2.8 convert_element_type.85
  325.6 1.8 pad_maximum_fusion.1
  327.3 130.0 %reduce_all.1 = (f32[2,128,1536]{2,1,0:T(8,128)}, f32[2,128,1536]{2,1,0:T(8,128)}, bf16[8,48,776]{2,1,0:T(8,128)(2,1)}, f32[96,1536]{1,0:T(8,128)}, f32[48,256]{1,0:T(8,128)}, /*index=5*/f32[8,128]{1,0:T(8,128)}) custom-call(bf16[8,2,128,1536]{3,2,1,0:T(8,128)(2,1)} %bitcast.103, bf16[8,2,128,1536]{3,2,1,0:T(8,128)(2,1)} %bitcast.99, ...), custom_call_target="tpu_custom_call" | custom-call | tf_op jit(solution)/shard_map/reduce_all/pallas_call | solution.py:899
  457.4 1.2 convert_bitcast_fusion
  458.6 0.9 slice_bitcast_fusion.1
  461.4 0.9 copy.76
  462.3 2.0 copy.77
  464.8 0.7 copy.73
  465.5 2.5 pad_maximum_fusion.4
  468.0 2.0 fusion.6
  470.1 0.8 copy.100
  (130 shorter events, 7.2 us)
Async XLA Ops:
  7.2 220.7 %all-reduce.7.cloned.1.call-start = ((), (), s32[]{:S(2)}) async-start(), calls=%async_computation | async-start | bytes 131072 | tf_op jit(solution)/shard_map/psum | solution.py:1016
  114.1 8.0 %slice-start.2 = ((s8[6291456]{0:T(1024)(128)(4,1)}), s8[2097152]{0:T(1024)(128)(4,1)S(1)}, s32[]{:S(2)}) async-start(s8[6291456]{0:T(1024)(128)(4,1)} %bitcast.93), calls=%async_computation.3 | async-start | bytes 4194304
  114.4 4.4 copy-start.11
  114.5 7.6 %copy-start.12 = (f32[1536]{0:T(1024)}, f32[1536]{0:T(1024)S(1)}, u32[]{:S(2)}) copy-start(f32[1536]{0:T(1024)S(1)} %mul.128) | copy-start | bytes 18436
  114.5 7.6 %slice-start.3 = ((s8[6291456]{0:T(1024)(128)(4,1)}), s8[4194304]{0:T(1024)(128)(4,1)S(1)}, s32[]{:S(2)}) async-start(s8[6291456]{0:T(1024)(128)(4,1)} %bitcast.93), calls=%async_computation.4 | async-start | bytes 8388608
  123.6 2.6 copy-start
  126.2 3.7 copy-start.20
  126.2 3.9 slice-start.7
  126.2 4.5 copy-start.7
  130.8 12.0 %copy-start.17 = (f32[48]{0:T(128)S(1)}, f32[48]{0:T(128)}, u32[]{:S(2)}) copy-start(f32[48]{0:T(128)} %param.20) | copy-start | bytes 580
  130.8 12.0 %copy-start.18 = (f32[48]{0:T(128)S(1)}, f32[48]{0:T(128)}, u32[]{:S(2)}) copy-start(f32[48]{0:T(128)} %param.19) | copy-start | bytes 580
  143.6 30.2 %copy-start.1 = (bf16[1,256,1536]{2,1,0:T(8,128)(2,1)S(1)}, bf16[1,256,1536]{2,1,0:T(8,128)(2,1)}, u32[]{:S(2)}) copy-start(bf16[1,256,1536]{2,1,0:T(8,128)(2,1)} %param.11) | copy-start | bytes 2359300
  227.8 63.7 %slice-start = ((s8[6291456]{0:T(1024)(128)(4,1)}), s8[2097152]{0:T(1024)(128)(4,1)S(1)}, s32[]{:S(2)}) async-start(s8[6291456]{0:T(1024)(128)(4,1)} %bitcast.91), calls=%async_computation.1 | async-start | bytes 4194304
  278.9 12.6 %slice-start.1 = ((s8[6291456]{0:T(1024)(128)(4,1)}), s8[4194304]{0:T(1024)(128)(4,1)S(1)}, s32[]{:S(2)}) async-start(s8[6291456]{0:T(1024)(128)(4,1)} %bitcast.91), calls=%async_computation.2 | async-start | bytes 8388608
  278.9 12.6 %copy-start.19 = (bf16[2048,1024]{1,0:T(8,128)(2,1)S(1)}, bf16[2048,1024]{1,0:T(8,128)(2,1)}, u32[]{:S(2)}) copy-start(bf16[2048,1024]{1,0:T(8,128)(2,1)} %get-tuple-element.43) | copy-start | bytes 12582916
  298.8 2.5 copy-start.5
  298.8 3.3 copy-start.15
  300.6 5.9 %copy-start.10 = (f32[8,2048]{1,0:T(8,128)S(1)}, f32[8,2048]{1,0:T(8,128)}, u32[]{:S(2)}) copy-start(f32[8,2048]{1,0:T(8,128)} %get-tuple-element.44) | copy-start | bytes 196612
  302.8 8.3 %slice-start.4 = ((s8[6291456]{0:T(1024)(128)(4,1)}), s8[2097152]{0:T(1024)(128)(4,1)S(1)}, s32[]{:S(2)}) async-start(s8[6291456]{0:T(1024)(128)(4,1)} %bitcast.95), calls=%async_computation.5 | async-start | bytes 4194304
  306.6 4.5 slice-start.5
  311.0 10.8 %slice-start.6 = ((bf16[1536,1024]{1,0:T(8,128)(2,1)}), bf16[1536,256]{1,0:T(8,128)(2,1)S(1)}, s32[]{:S(2)}) async-start(bf16[1536,1024]{1,0:T(8,128)(2,1)} %copy-done.5), calls=%async_computation.7 | async-start | bytes 1572864 | tf_op jit(solution)/shard_map/slice | solution.py:1038
  320.1 5.5 %copy-start.3 = (bf16[1536,768]{1,0:T(8,128)(2,1)S(1)}, bf16[1536,768]{1,0:T(8,128)(2,1)}, u32[]{:S(2)}) copy-start(bf16[1536,768]{1,0:T(8,128)(2,1)} %slice.167) | copy-start | bytes 7077892
  457.4 2.2 copy-start.14
  458.6 5.9 %copy-start.2 = (bf16[1,256,1536]{2,1,0:T(8,128)(2,1)S(1)}, bf16[1,256,1536]{2,1,0:T(8,128)(2,1)}, u32[]{:S(2)}) copy-start(bf16[1,256,1536]{2,1,0:T(8,128)(2,1)} %param.11) | copy-start | bytes 2359300
  458.6 5.9 %copy-start.4 = (f32[2,128,1536]{2,1,0:T(8,128)S(1)}, f32[2,128,1536]{2,1,0:T(8,128)}, u32[]{:S(2)}) copy-start(f32[2,128,1536]{2,1,0:T(8,128)} %get-tuple-element.50) | copy-start | bytes 4718596
  458.6 5.9 %copy-start.13 = (f32[1536]{0:T(1024)S(1)}, f32[1536]{0:T(1024)}, u32[]{:S(2)}) copy-start(f32[1536]{0:T(1024)} %copy-done.12) | copy-start | bytes 18436
  459.5 6.0 %copy-start.16 = (f32[256]{0:T(256)S(1)}, f32[256]{0:T(256)}, u32[]{:S(2)}) copy-start(f32[256]{0:T(256)} %fusion.3) | copy-start | bytes 3076
  459.5 6.0 %slice-start.8 = ((f32[8,2048]{1,0:T(8,128)}), f32[1,2048]{1,0:T(1,128)S(1)}, s32[]{:S(2)}) async-start(f32[8,2048]{1,0:T(8,128)} %all-reduce.7.cloned.1.call-done.sum_ref), calls=%async_computation.9 | async-start | bytes 16384 | tf_op jit(solution)/shard_map/slice | solution.py:1057
  462.3 5.7 %copy-start.6 = (bf16[1,256,1536]{2,1,0:T(8,128)(2,1)S(1)}, bf16[1,256,1536]{2,1,0:T(8,128)(2,1)}, u32[]{:S(2)}) copy-start(bf16[1,256,1536]{2,1,0:T(8,128)(2,1)} %param.12) | copy-start | bytes 2359300
  465.5 2.5 copy-start.8
  468.0 2.1 copy-start.9
Sparse Core Ops, SparseCore 0:
  173.9 53.8 all-reduce.6

commit v3 on v2

--- a/solution.py
+++ b/solution.py
@@ -508,12 +508,65 @@
     pl.semaphore_wait(barrier, ranks - 1 + near)
 
 
+def project(tok, w, common, normed, proj, raw, w_full):
+    ranks, planes = tok.shape[0], w.shape[0]
+    rows, width = w.shape[2:]
+    strip, tile = 32, tok.shape[2]
+    d = tok.shape[3]
+    half = planes // 2
+
+    def lay(i, gains):
+        at = pl.ds(pl.multiple_of(i * rows, 16), rows)
+        plane, rank = lax.div(i, ranks), i % ranks
+        shared = common[rank, lax.div(plane, half), plane % half]
+        w_full[at, :width] = w[plane, rank]
+        w_full[at, width:] = shared
+        return gains + shared[: d // HDIM, 2 * NSTATE :].astype(f32)
+
+    gains = lax.fori_loop(0, planes * ranks, lay, jnp.zeros((d // HDIM, LANES), f32))
+    moved = pltpu.roll(gains, HDIM, 1)
+    low = iota((1, LANES), 1) < HDIM
+    gain = [jnp.where(low, moved[2 * j : 2 * j + 1], gains[2 * j + 1 : 2 * j + 2]) for j in range(d // LANES)]
+
+    def norm(i, _):
+        per = tile // strip
+        part = lax.div(i, per)
+        at = pl.ds(pl.multiple_of((i % per) * strip, strip), strip)
+        x = tok.at[lax.div(part, 2), part % 2][at, :].astype(f32)
+        scale = lax.rsqrt(jnp.sum(x * x, axis=1, keepdims=True) * (1.0 / d) + epsilon)
+        to = pl.ds(pl.multiple_of(i * strip, strip), strip)
+        for j in range(d // LANES):
+            cut = slice(j * LANES, (j + 1) * LANES)
+            normed[to, cut] = (x[:, cut] * scale * gain[j]).astype(bf16)
+        return 0
+
+    lax.fori_loop(0, ranks * 2 * tile // strip, norm, 0)
+    main = width + 2 * NSTATE
+
+    def multiply(i, _):
+        at = pl.ds(pl.multiple_of(i * 256, 256), 256)
+        for start in range(0, main, 512):
+            cut = slice(start, min(start + 512, main))
+            proj[at, cut] = dot(normed[at, :], w_full[:, cut], NN).astype(bf16)
+        steps = dot(normed[at, :], w_full[:, main:], NN).astype(bf16).astype(f32)
+        for k in range(2):
+            to = pl.ds(pl.multiple_of(i * 256 + k * LANES, LANES), LANES)
+            raw[:, to] = steps[k * LANES : (k + 1) * LANES].T[: raw.shape[0]]
+        return 0
+
+    lax.fori_loop(0, ranks * 2 * tile // 256, multiply, 0)
+
+
 def gather_kernel(
-    tok_in, cot_in, w_in, wout_in, common_in,
-    tok, cot, w, wout, common,
-    stage, tok_s, tok_r, cot_s, cot_r, com_s, com_r, wz_s, wz_r, oz_s, oz_r, cz_s, cz_r,
-    a2a_s, a2a_r, mix_s, mix_r, local,
+    fused, tok_in, cot_in, w_in, wout_in, common_in,
+    cot, wout, common, *rest,
 ):
+    if fused:
+        normed, proj, raw, w_full, tok, w, *rest = rest
+    else:
+        tok, w, *rest = rest
+    (stage, tok_s, tok_r, cot_s, cot_r, com_s, com_r, wz_s, wz_r, oz_s, oz_r, cz_s, cz_r,
+    a2a_s, a2a_r, mix_s, mix_r, local) = rest
     ranks, planes = tok.shape[0], w.shape[0]
     me, dp = lax.axis_index("seq"), lax.axis_index("dp")
     bits = bits_of(ranks)
@@ -591,6 +644,8 @@
         def _():
             remote(stage.at[d], wout.at[place], mix_s.at[d], mix_r.at[place], (dp, to)).start()
 
+    if fused:
+        project(tok, w, common, normed, proj, raw, w_full)
     for group in range(1, cots.groups):
         cots.forward(group)
     for place in range(planes):
@@ -611,33 +666,80 @@
 def gather_all(ranks, planes, tok, cot, w, w_out, common):
     length, d = tok.shape
     halves = (2, length // 2, d)
+    total = ranks * length
+    rows, cols = w.shape[1:]
+    fused = rows % 16 == 0 and rows * HDIM >= 2 * d and length % 256 == 0
     dma = pltpu.SemaphoreType.DMA
     vmem = pl.BlockSpec(memory_space=pltpu.VMEM)
     ring, line = 2 * ranks, 2 * planes
+    buffers = [((ranks,) + halves, bf16), ((planes,) + w.shape, bf16)]
     out = [
-        (ranks,) + halves, (ranks,) + halves, (planes,) + w.shape, (planes,) + w_out.shape,
-        (ranks, 2, planes // 2) + common.shape,
+        ((ranks,) + halves, bf16), ((planes,) + w_out.shape, bf16), ((ranks, 2, planes // 2) + common.shape, bf16)
     ]
-    tok_all, cot_all, w_all, out_all, common_all = pl.pallas_call(
-        gather_kernel,
+    if fused:
+        out += [
+            ((total, d), bf16), ((total, cols + 2 * NSTATE), bf16), ((HDIM, total), f32),
+            ((d, cols + common.shape[1]), bf16),
+        ]
+    else:
+        out += buffers
+    cot_all, out_all, common_all, *rest = pl.pallas_call(
+        partial(gather_kernel, fused),
         in_specs=[pl.BlockSpec(memory_space=pl.ANY)] * 5,
-        out_specs=[vmem] * 5,
-        out_shape=[jax.ShapeDtypeStruct(s, bf16) for s in out],
-        scratch_shapes=[pltpu.VMEM((planes,) + w_out.shape, bf16)]
+        out_specs=[vmem] * len(out),
+        out_shape=[jax.ShapeDtypeStruct(*s) for s in out],
+        scratch_shapes=([pltpu.VMEM(*s) for s in buffers] if fused else [])
+        + [pltpu.VMEM((planes,) + w_out.shape, bf16)]
         + [dma((ring,))] * 6
         + [dma((line,))] * 6
         + [dma((ranks,)), dma((ranks,)), dma((planes,)), dma((planes,)), dma((5,))],
-        compiler_params=pltpu.CompilerParams(collective_id=0, has_side_effects=True),
+        compiler_params=pltpu.CompilerParams(
+            collective_id=0, has_side_effects=True, vmem_limit_bytes=67043328
+        ),
         name="gather_all",
     )(tok.reshape(halves), cot.reshape(halves), w, w_out, common)
-    rows = common.shape[0]
-    return (
-        tok_all.reshape(ranks * length, d),
-        cot_all.reshape(ranks * length, d),
-        w_all.reshape(planes * ranks * w.shape[1], w.shape[2]),
-        out_all.reshape(planes * w_out.shape[0], d),
-        common_all.reshape(ranks, planes, rows, common.shape[1]).transpose(1, 0, 2, 3),
-    )
+    common_all = common_all.reshape((ranks, planes) + common.shape).transpose(1, 0, 2, 3)
+    cot_all, out_all = cot_all.reshape(total, d), out_all.reshape(planes * w_out.shape[0], d)
+    if fused:
+        return (cot_all, out_all, common_all, True) + tuple(rest)
+    tok_all, w_all = rest
+    return cot_all, out_all, common_all, False, tok_all.reshape(total, d), w_all.reshape(-1, cols)
+
+
+def plane_sum_kernel(x_in, total, land, send, recv):
+    ranks = land.shape[0]
+    me, dp = lax.axis_index("seq"), lax.axis_index("dp")
+    bits = bits_of(ranks)
+    barrier = pltpu.get_barrier_semaphore()
+    for mask in range(1, ranks):
+        pl.semaphore_signal(barrier, inc=1, device_id=(dp, flip_mask(me, mask, bits)), device_id_type=MESH)
+    pl.semaphore_wait(barrier, ranks - 1)
+
+    def copy(mask):
+        return remote(x_in, land.at[mask], send.at[mask], recv.at[mask], (dp, flip_mask(me, mask, bits)))
+
+    for mask in range(1, ranks):
+        copy(mask).start()
+    value = x_in[...]
+    for mask in range(1, ranks):
+        copy(mask).wait_recv()
+        value = value + land[mask]
+    total[...] = value
+    for mask in range(1, ranks):
+        copy(mask).wait_send()
+
+
+def plane_sum(ranks, x):
+    vmem = pl.BlockSpec(memory_space=pltpu.VMEM)
+    return pl.pallas_call(
+        plane_sum_kernel,
+        in_specs=[vmem],
+        out_specs=vmem,
+        out_shape=jax.ShapeDtypeStruct(x.shape, f32),
+        scratch_shapes=[pltpu.VMEM((ranks,) + x.shape, f32)] + [pltpu.SemaphoreType.DMA((ranks,))] * 2,
+        compiler_params=pltpu.CompilerParams(collective_id=2, has_side_effects=True),
+        name="plane_sum",
+    )(x)
 
 
 def add_into(dst, pieces, rows):
@@ -981,50 +1083,69 @@
         [
             widen(in_weight[:, :din_all].reshape(rows, ranks, din), padded, 2),
             widen(in_weight[:, din_all : 2 * din_all].reshape(rows, ranks, din), padded, 2),
-            widen(in_weight[:, din_all + conv_all :].reshape(rows, ranks, heads), 8, 2),
         ],
         axis=2,
     ).transpose(1, 0, 2)
+    d = in_weight.shape[0] * ranks * planes
+    rank_id = lax.axis_index("dp") * ranks + me
     small = [norm_gain, gate_gain, conv_weight.reshape(-1), conv_bias]
     sizes = [a.shape[0] for a in small]
-    packed = widen(jnp.concatenate(small), rows * LANES, 0).reshape(rows, LANES)
-    shared = in_weight[:, 2 * din_all : 2 * din_all + 2 * NSTATE]
-    common = jnp.concatenate([shared, packed], axis=1)
-    tok, cot, w_all, w_out, common = gather_all(
+    room = rows * HDIM - d
+    if room >= sum(sizes):
+        placed = lax.dynamic_update_slice_in_dim(jnp.zeros((d,), bf16), norm_gain, rank_id * rows, 0)
+        packed = jnp.concatenate([placed, widen(jnp.concatenate(small), room, 0)])
+    else:
+        packed = widen(jnp.concatenate(small), rows * HDIM, 0)
+    common = jnp.concatenate(
+        [
+            in_weight[:, 2 * din_all : 2 * din_all + 2 * NSTATE],
+            widen(in_weight[:, din_all + conv_all :], HDIM, 1),
+            packed.reshape(rows, HDIM),
+        ],
+        axis=1,
+    )
+    cot, w_out, common, fused, *rest = gather_all(
         ranks, planes, tokens[0], cotangent[0], send, out_weight, common
     )
-    shared = common[..., : 2 * NSTATE].reshape(-1, 2 * NSTATE)
-    w_in = jnp.concatenate([w_all[:, : 2 * padded], shared], axis=1)
-    w_dt = w_all[:, 2 * padded :].T
     w_out = widen(w_out, padded, 0)
-    packed = common[..., 2 * NSTATE :].reshape(ranks * planes, rows * LANES).astype(f32)
+    packed = common[..., 2 * NSTATE + HDIM :].reshape(ranks * planes, rows * HDIM).astype(f32)
+    if room >= sum(sizes):
+        packed = packed[:, d:]
     gain_norm, gain_gate, conv_w, conv_b = (
         packed[:, sum(sizes[:k]) : sum(sizes[: k + 1])].reshape(-1) for k in range(4)
     )
     conv_w = conv_w.reshape(-1, CONVK)
     taps = jnp.concatenate([conv_w.T, conv_b[None], jnp.zeros((8 - CONVK - 1, conv_all), f32)], axis=0)
     conv = jnp.concatenate([widen(mine(taps, din, 1), padded, 1), taps[:, din_all:]], axis=1)
+    if fused:
+        normed, proj, raw, w_full = rest
+    else:
+        tok, w_all = rest
+        w_full = jnp.concatenate([w_all, common.reshape(-1, common.shape[-1])], axis=1)
+        normed = rms_scale(tok.astype(f32), gain_norm).astype(bf16)
+        proj = dot(normed, w_full[:, :main], NN).astype(bf16)
+        raw = dot(w_full[:, main : main + HDIM].T, normed, NT).astype(bf16).astype(f32)
+    raw = widen(mine(raw, heads), 8, 0)
     rate, bias, skip = (mine(a, heads) for a in (decay_rate, dt_bias, d_skip))
     lanes = jnp.stack([jnp.repeat(skip, HDIM), mine(gain_gate, din)])
     lanes = widen(widen(lanes, padded, 1), 8, 0)
     head_rows = jnp.broadcast_to(widen(jnp.stack([rate, bias]), 8, 1)[:, :, None], (2, 8, SUB))
 
-    normed = rms_scale(tok.astype(f32), gain_norm).astype(bf16)
-    proj = dot(normed, w_in, NN).astype(bf16)
-    raw = dot(w_dt, normed, NT).astype(bf16).astype(f32)
     y, dg, out_part, states, sums = mixer_forward(proj, raw, cot, w_out, conv, lanes, head_rows)
-    sums = lax.psum(sums, "seq")
+    sums = plane_sum(ranks, sums[::4].reshape(8, -1)).reshape(2, -1)
+    sums = jnp.repeat(sums, 4, axis=0)
     d_proj, d_raw, d_w_out, d_conv, d_lane, d_head = mixer_backward(
         din_all, proj, raw, y, dg, sums, states, cot, conv, lanes, head_rows
     )
-    d_raw16 = d_raw.astype(bf16)
-    d_normed_part = dot(d_proj, w_in, NT) + dot(d_raw16, w_dt, TN)
-    x_hat = tok.astype(f32)
-    x_hat = x_hat * lax.rsqrt(jnp.mean(x_hat * x_hat, axis=1, keepdims=True) + epsilon)
-    d_g1 = jnp.sum(d_normed_part * x_hat, axis=0)
+    d_steps = lax.dynamic_update_slice_in_dim(
+        jnp.zeros((proj.shape[0], w_full.shape[1] - main), bf16), d_raw[:heads].T.astype(bf16), me * heads, 1
+    )
+    d_proj = jnp.concatenate([d_proj, d_steps], axis=1)
+    w_live = jnp.where(jnp.arange(w_full.shape[1]) < main + HDIM, w_full, 0)
+    d_normed_part = dot(d_proj, w_live, NT)
+    d_g1 = jnp.sum(d_normed_part * normed.astype(f32), axis=0) / gain_norm
     d_w = dot(normed, d_proj, TN).astype(bf16)
-    d_wdt = dot(normed, d_raw16, ((0,), (1,))).astype(bf16)
-    d_w_main = jnp.concatenate([d_w[:, : 2 * padded], d_wdt], axis=1).reshape(planes, ranks, rows, -1)
+    d_w_main = d_w[:, : 2 * padded].reshape(planes, ranks, rows, -1)
 
     def by_owner(array):
         split = array.reshape((2, planes // 2, ranks) + array.shape[1:])
@@ -1035,7 +1156,7 @@
             jnp.zeros((size * ranks,) + own.shape[1:], f32), own, me * size, 0
         )
 
-    d_bc = d_w[:, 2 * padded :].reshape(planes * ranks, rows, 2 * NSTATE)
+    d_bc = d_w[:, 2 * padded :].reshape(planes * ranks, rows, -1)
     d_cw, d_cb = d_conv[:CONVK].T, d_conv[CONVK]
     full_cw = jnp.concatenate([place(d_cw[:din], din), d_cw[padded:]], axis=0)
     full_cb = jnp.concatenate([place(d_cb[:din], din), d_cb[padded:]], axis=0)
@@ -1065,8 +1186,7 @@
         [
             spread[:, :, :din].reshape(rows, din_all),
             spread[:, :, padded : padded + din].reshape(rows, din_all),
-            bc_sum,
-            spread[:, :, 2 * padded : 2 * padded + heads].reshape(rows, heads * ranks),
+            bc_sum[:, : 2 * NSTATE + heads * ranks],
         ],
         axis=1,
     )

time: 483 us -> 388 us (0.80)
  waiting for transfers between devices: 53.3 us -> 0 us
  matrix products: 47.3 us -> 26 us
  between operations: 14.5 us -> 1.09 us
  other arithmetic: 21.2 us -> 13.8 us
  local copies, waits for them, and re-layouts: 34.6 us -> 28.2 us
  Pallas kernels: 307 us -> 313 us
    psum x1 -> x0, waiting for transfers between devices: 53.3 us -> none  [per_device(): sums = lax.psum(sums, 'seq')]
    dot_general x6 -> x2, matrix products: 47.3 us -> 26 us  [dot(): lax.dot_general(a, b, (dims, ((), ())), preferred_element_type=f32, preci...]
    pallas_call x1 -> x2, Pallas kernels: 97.7 us -> 109 us  [the longest x1 103 us: gather_all(): pl.pallas_call(partial(gather_kernel, fused), in_specs=[pl.BlockSpec(memo...]
    pallas_call x1, Pallas kernels: 130 us -> 125 us  [reduce_all(): pl.pallas_call(reduce_kernel, in_specs=[pl.BlockSpec(memory_space=pl.ANY)...]
  transfers between devices with their start and end apart: 1 -> 0, of which waited for: 1 -> 0; matrix products, arithmetic and copies ran while one was open for 0% -> 0% of each run, Pallas kernels for 0% -> 0%
where the time goes in v3:
time: 388 us; the launch traced here: 382 us
  Pallas kernels  313 us (81%)
  local copies, waits for them, and re-layouts  28.2 us (7%)
  matrix products  26 us (7%)
  other arithmetic  13.8 us (4%)
    pallas_call x1, Pallas kernels, reduce_all(): pl.pallas_call(reduce_kernel, in_specs=[pl.BlockSpec(memory_space=pl.ANY)...  125 us
    pallas_call x1, Pallas kernels, gather_all(): pl.pallas_call(partial(gather_kernel, fused), in_specs=[pl.BlockSpec(memo...  103 us
    pallas_call x1, Pallas kernels, mixer_backward(): pl.pallas_call(partial(bwd_kernel, total_din), grid=(length // block,), i...  48.8 us
    pallas_call x1, Pallas kernels, mixer_forward(): pl.pallas_call(fwd_kernel, grid=(length // block,), in_specs=[rows_spec(b...  30.1 us
    dot_general x2, matrix products, dot(): lax.dot_general(a, b, (dims, ((), ())), preferred_element_type=f32, preci...  26 us

profile of v3, /device:TPU:0, one launch (start us, length us, event | category | flops | bytes accessed | tf_op | source)
XLA Modules:
  0.0 382.4 jit_solution(13872923948956541793)
XLA Ops:
  0.7 0.9 dynamic_update_slice.24
  1.6 0.8 copy.40
  2.5 0.8 fusion.20
  3.4 0.7 slice.126
  4.1 0.7 slice.127
  4.8 0.7 fusion.12.common_in
  5.5 1.1 fusion.24
  6.7 0.9 maximum_bitcast_fusion.w_in
  7.6 102.9 %gather_all.1 = (bf16[8,2,128,1536]{3,2,1,0:T(8,128)(2,1)}, bf16[4,96,1536]{2,1,0:T(8,128)(2,1)}, bf16[8,2,2,48,384]{4,3,2,1,0:T(8,128)(2,1)}, bf16[2048,1536]{1...) custom-call(bf16[2,128,1536]{2,1,0:T(8,128)(2,1)} %bitcast.71, ...), custom_call_target="tpu_custom_call" | custom-call | tf_op jit(solution)/shard_map/gather_all/pallas_call | solution.py:686
  110.4 1.2 slice_convert_fusion
  112.0 0.5 reshape_reshape.9
  112.6 0.5 copy.42
  113.4 0.6 pad_maximum_fusion.5.conv_ref
  114.5 0.6 select_maximum_fusion.lane_ref
  115.2 0.7 broadcast_in_dim.43.head_ref
  115.9 0.9 constant_dynamic-slice_fusion.1
  116.8 0.6 pad.26.raw_ref
  117.4 30.1 %mix_forward.1 = (f32[2048,384]{1,0:T(8,128)}, f32[2048,384]{1,0:T(8,128)}, bf16[2048,1536]{1,0:T(8,128)(2,1)}, f32[16,128,384]{2,1,0:T(8,128)}, f32[8,2048]{1,0:T(8,128)}) custom-call(bf16[2048,1024]{1,0:T(8,128)(2,1)} %get-tuple-element.35.proj_ref.rim_ref, f32[8,2048]{1,0:T(8,128)} %pad.26.raw_ref, bf16[2048,1536]{1,0:T(8,128)(2,1)} %bitcast.69, ...), custom_call_target="tpu_custom_call" | custom-call | tf_op jit(solution)/shard_map/mix_forward/pallas_call | solution.py:293
  147.5 0.9 slice.133
  148.4 0.6 reshape.245.x_in
  149.0 6.6 %plane_sum.1 = f32[8,512]{1,0:T(8,128)} custom-call(f32[8,512]{1,0:T(8,128)} %reshape.245.x_in), custom_call_target="tpu_custom_call" | custom-call | tf_op jit(solution)/shard_map/plane_sum/pallas_call | solution.py:734
  155.7 0.7 reshape.246
  156.4 0.7 reshape.247.sum_ref
  157.1 48.8 %mix_backward.1 = (bf16[2048,1024]{1,0:T(8,128)(2,1)}, f32[8,2048]{1,0:T(8,128)}, f32[384,1536]{1,0:T(8,128)}, f32[8,640]{1,0:T(8,128)}, f32[8,384]{1,0:T(8,128)}, /*index=5*/f32[2,8,128]{2,1,0:T(8,128)}) custom-call(bf16[2048,1024]{1,0:T(8,128)(2,1)} %get-tuple-element.35.proj_ref.rim_ref, bf16[2048,1024]{1,0:T(8,128)(2,1)} %get-tuple-element.35.proj_ref.rim_ref, ...), custom_call_target="tpu_custom_call" | custom-call | tf_op jit(solution)/shard_map/mix_backward/pallas_call | solution.py:334
  205.8 0.8 slice_reduce_fusion
  207.1 0.8 reduce_sum.49
  208.3 0.8 fusion.13
  209.5 2.0 dynamic_update_slice.25
  211.5 14.2 %multiply_reduce_fusion = (f32[1536]{0:T(1024)S(1)}, bf16[2048,1536]{1,0:T(8,128)(2,1)}) fusion(bf16[2048,1536]{1,0:T(8,128)(2,1)} %get-tuple-element.48, bf16[1536,1152]{1,0:T(8,128)(2,1)} %get-tuple-element.47, pred[1152]{0:T(1024)(128)(4,1)S(1)} %iota_compare_fusion.4, bf16[2048,128]{1,0:T(8,128)(2,1)S(1)} %dynamic_update_slice.25, ...), kind=kOutput, calls=%fused_computation | convolution fusion | flops 7271545344 | bytes 20847744 | tf_op jit(solution)/shard_map/dot_general | solution.py:25
  225.8 0.6 fusion.25
  226.9 0.5 copy.45
  227.4 0.5 reshape.252
  228.5 0.7 copy.60
  229.1 11.8 %convolution_convert_fusion = bf16[1536,1152]{1,0:T(8,128)(2,1)S(1)} fusion(bf16[2048,1536]{1,0:T(8,128)(2,1)} %get-tuple-element.48, bf16[2048,128]{1,0:T(8,128)(2,1)S(1)} %dynamic_update_slice.25, bf16[2048,1024]{1,0:T(8,128)(2,1)} %get-tuple-element.45), kind=kOutput, calls=%fused_computation.1 | convolution fusion | flops 7258963968 | bytes 14548992 | tf_op jit(solution)/shard_map/dot_general | solution.py:25
  240.9 1.6 slice.166
  242.6 1.2 copy.59
  243.8 0.8 copy-done.3
  244.6 1.1 convert_element_type.60
  245.7 124.9 %reduce_all.1 = (f32[2,128,1536]{2,1,0:T(8,128)}, f32[2,128,1536]{2,1,0:T(8,128)}, bf16[8,48,768]{2,1,0:T(8,128)(2,1)}, f32[96,1536]{1,0:T(8,128)}, f32[48,384]{1,0:T(8,128)}, /*index=5*/f32[8,128]{1,0:T(8,128)}) custom-call(bf16[8,2,128,1536]{3,2,1,0:T(8,128)(2,1)} %bitcast.74, bf16[8,2,128,1536]{3,2,1,0:T(8,128)(2,1)} %bitcast.75, ...), custom_call_target="tpu_custom_call" | custom-call | tf_op jit(solution)/shard_map/reduce_all/pallas_call | solution.py:1001
  370.6 1.2 convert_bitcast_fusion
  372.0 0.7 copy-done.4
  372.7 1.1 pad_maximum_fusion.3
  374.5 3.5 fusion.8
  378.1 0.7 copy.49
  378.8 0.6 fusion.26
  379.3 0.6 slice.153
  379.9 0.6 slice.155
  380.5 1.9 copy.73
  (89 shorter events, 4.9 us)
Async XLA Ops:
  111.7 2.6 copy-start.10
  111.7 3.5 copy-start.8
  111.7 3.4 copy-start.9
  211.5 14.9 %copy-start.7 = (f32[8,640]{1,0:T(8,128)S(1)}, f32[8,640]{1,0:T(8,128)}, u32[]{:S(2)}) copy-start(f32[8,640]{1,0:T(8,128)} %get-tuple-element.50) | copy-start | bytes 61444
  242.5 2.1 copy-start.3
  371.8 0.9 copy-start.4
  371.9 1.9 copy-start.5
  371.9 2.0 copy-start
  371.9 2.0 copy-start.1
  372.7 1.8 slice-start
  372.7 1.8 copy-start.2
  374.5 3.5 copy-start.6

commit v4 on v1

v4 whole, which is shorter than its diff:
```python
from functools import partial

import jax
import jax.numpy as jnp
from jax import lax
from jax.experimental import pallas as pl
from jax.experimental.pallas import tpu as pltpu
from jax.sharding import PartitionSpec as P

HDIM = 64
NSTATE = 128
CONVK = 4
LANES = 128
SUB = 128
TOKENS = 256
EDGE = 8

epsilon = 1e-05
highest = lax.Precision.HIGHEST
bf16 = jnp.bfloat16
f32 = jnp.float32


MESH = pl.DeviceIdType.MESH


def flip(index, bit):
    return index + bit * (1 - 2 * (lax.div(index, bit) % 2))


def flip_mask(index, mask, bits):
    for bit in bits:
        if mask & bit:
            index = flip(index, bit)
    return index


def bits_of(size):
    return [1 << k for k in range(size.bit_length() - 1)]


def both_orders(size):
    bits = bits_of(size)
    slow = bits[1:]
    return [slow + bits[:1], slow[::-1] + bits[:1]]


def remote(src, dst, send, recv, to):
    return pltpu.make_async_remote_copy(
        src_ref=src, dst_ref=dst, send_sem=send, recv_sem=recv, device_id=to, device_id_type=MESH
    )


class Spread:
    def __init__(self, buf, send, recv, own=None):
        self.size = buf.shape[0]
        self.bits = bits_of(self.size)
        self.orders = both_orders(self.size)
        self.buf, self.send, self.recv = buf, send, recv
        self.me, self.dp = lax.axis_index("seq"), lax.axis_index("dp")
        self.own = own

    def masks(self, half):
        order = self.orders[half]
        got = [0]
        for bit in order:
            got = got + [m | bit for m in got]
        return got

    def copy(self, half, mask, bit):
        origin = flip_mask(self.me, mask, self.bits)
        dst = self.buf.at[origin, half]
        src = self.own.at[half] if (mask == 0 and self.own is not None) else dst
        slot = half * self.size + (mask | bit)
        return remote(src, dst, self.send.at[slot], self.recv.at[slot], (self.dp, flip(self.me, bit)))

    def start(self, half, mask):
        order = self.orders[half]
        after = max((order.index(b) for b in self.bits if mask & b), default=-1) + 1
        for bit in order[after:]:
            self.copy(half, mask, bit).start()

    def arrive(self, half, mask):
        order = self.orders[half]
        top = order[max(order.index(b) for b in self.bits if mask & b)]
        self.copy(half, mask & ~top, top).wait_recv()

    def forward(self, group):
        for k in range(1 << group, 2 << group):
            for half in range(2):
                mask = self.masks(half)[k]
                self.arrive(half, mask)
                self.start(half, mask)

    def finish(self):
        for half in range(2):
            for mask in range(1, self.size):
                order = self.orders[half]
                top = order[max(order.index(b) for b in self.bits if mask & b)]
                self.copy(half, mask & ~top, top).wait_send()

    @property
    def groups(self):
        return len(self.bits)


class Line:
    def __init__(self, at, size, send, recv):
        self.at, self.size, self.send, self.recv = at, size, send, recv
        self.me, self.seq = lax.axis_index("dp"), lax.axis_index("seq")

    def copy(self, way, hop):
        block = self.me - way * (hop - 1)
        slot = (self.size if way > 0 else 0) + hop
        ref = self.at(block)
        return remote(ref, ref, self.send.at[slot], self.recv.at[slot], (self.me + way, self.seq))

    def sends(self, way, hop):
        block = self.me - way * (hop - 1)
        to = self.me + way
        return (block >= 0) & (block < self.size) & (to >= 0) & (to < self.size)

    def start(self, hop):
        for way in (1, -1):
            @pl.when(self.sends(way, hop))
            def _():
                self.copy(way, hop).start()

    def arrive(self, hop):
        for way in (1, -1):
            source = self.me - way * hop
            @pl.when((source >= 0) & (source < self.size))
            def _():
                ref = self.at(source)
                slot = (self.size if way > 0 else 0) + hop
                pltpu.make_async_copy(ref, ref, self.recv.at[slot]).wait()

    def forward(self, hop):
        self.arrive(hop)
        if hop + 1 < self.size:
            self.start(hop + 1)

    def finish(self):
        for hop in range(1, self.size):
            for way in (1, -1):
                @pl.when(self.sends(way, hop))
                def _():
                    self.copy(way, hop).wait_send()


def greet(ranks, planes):
    me, dp = lax.axis_index("seq"), lax.axis_index("dp")
    barrier = pltpu.get_barrier_semaphore()
    for mask in range(1, ranks):
        pl.semaphore_signal(
            barrier, inc=1, device_id=(dp, flip_mask(me, mask, bits_of(ranks))), device_id_type=MESH
        )
    for way in (1, -1):
        @pl.when((dp + way >= 0) & (dp + way < planes))
        def _():
            pl.semaphore_signal(barrier, inc=1, device_id=(dp + way, me), device_id_type=MESH)
    near = jnp.where(dp > 0, 1, 0) + jnp.where(dp < planes - 1, 1, 0)
    pl.semaphore_wait(barrier, ranks - 1 + near)


def norm_tokens(tok, common, normed, rows, w_full):
    ranks, planes = tok.shape[0], 2 * common.shape[2]
    width = w_full.shape[1] - common.shape[-1]
    strip, tile = 32, tok.shape[2]
    d = tok.shape[3]
    half = planes // 2

    def lay(i, gains):
        at = pl.ds(pl.multiple_of(i * rows, 16), rows)
        plane, rank = lax.div(i, ranks), i % ranks
        shared = common[rank, lax.div(plane, half), plane % half]
        w_full[at, width:] = shared
        return gains + shared[: d // HDIM, 2 * NSTATE :].astype(f32)

    gains = lax.fori_loop(0, planes * ranks, lay, jnp.zeros((d // HDIM, LANES), f32))
    moved = pltpu.roll(gains, HDIM, 1)
    low = iota((1, LANES), 1) < HDIM
    gain = [jnp.where(low, moved[2 * j : 2 * j + 1], gains[2 * j + 1 : 2 * j + 2]) for j in range(d // LANES)]

    def norm(i, _):
        per = tile // strip
        part = lax.div(i, per)
        at = pl.ds(pl.multiple_of((i % per) * strip, strip), strip)
        x = tok.at[lax.div(part, 2), part % 2][at, :].astype(f32)
        scale = lax.rsqrt(jnp.sum(x * x, axis=1, keepdims=True) * (1.0 / d) + epsilon)
        to = pl.ds(pl.multiple_of(i * strip, strip), strip)
        for j in range(d // LANES):
            cut = slice(j * LANES, (j + 1) * LANES)
            normed[to, cut] = (x[:, cut] * scale * gain[j]).astype(bf16)
        return 0

    lax.fori_loop(0, ranks * 2 * tile // strip, norm, 0)


def stored(i, flipped, proj, flip_out, proj_out, store):
    at = pl.ds(pl.multiple_of(i * 256, 256), 256)
    return (
        pltpu.make_async_copy(proj.at[at, :], proj_out.at[at, :], store.at[0, i]),
        pltpu.make_async_copy(flipped.at[:, at], flip_out.at[:, at], store.at[1, i]),
    )


def project(w, normed, flipped, proj, raw, w_full, flip_out, proj_out, store):
    planes, ranks, rows, width = w.shape
    total, d = normed.shape
    main = width + 2 * NSTATE

    def lay(i, _):
        at = pl.ds(pl.multiple_of(i * rows, 16), rows)
        w_full[at, :width] = w[lax.div(i, ranks), i % ranks]
        return 0

    lax.fori_loop(0, planes * ranks, lay, 0)

    def multiply(i, _):
        at = pl.ds(pl.multiple_of(i * 256, 256), 256)
        for start in range(0, main, 512):
            cut = slice(start, min(start + 512, main))
            proj[at, cut] = dot(normed[at, :], w_full[:, cut], NN).astype(bf16)
        for k in range(2):
            to = pl.ds(pl.multiple_of(i * 256 + k * LANES, LANES), LANES)
            for j in range(d // LANES):
                tokens = normed[to, j * LANES : (j + 1) * LANES].astype(f32)
                flipped[j * LANES : (j + 1) * LANES, to] = tokens.T.astype(bf16)
        steps = dot(normed[at, :], w_full[:, main:], NN).astype(bf16).astype(f32)
        for k in range(2):
            to = pl.ds(pl.multiple_of(i * 256 + k * LANES, LANES), LANES)
            raw[:, to] = steps[k * LANES : (k + 1) * LANES].T[: raw.shape[0]]
        for copy in stored(i, flipped, proj, flip_out, proj_out, store):
            copy.start()
        return 0

    lax.fori_loop(0, total // 256, multiply, 0)


def gather_kernel(
    fused, tok_in, cot_in, w_in, wout_in, common_in,
    cot, wout, common, *rest,
):
    if fused:
        raw, flip_out, proj_out, full_out, tok, w, normed, flipped, proj, w_full, store, *rest = rest
    else:
        tok, w, *rest = rest
    (stage, tok_s, tok_r, cot_s, cot_r, com_s, com_r, wz_s, wz_r, oz_s, oz_r, cz_s, cz_r,
    a2a_s, a2a_r, mix_s, mix_r, local) = rest
    ranks, planes = tok.shape[0], w.shape[0]
    me, dp = lax.axis_index("seq"), lax.axis_index("dp")
    bits = bits_of(ranks)
    greet(ranks, planes)
    half = planes // 2
    tokens = Spread(tok, tok_s, tok_r, tok_in)
    cots = Spread(cot, cot_s, cot_r, cot_in)
    commons = Spread(common, com_s, com_r)
    w_line = Line(lambda d: w.at[d], planes, wz_s, wz_r)
    o_line = Line(lambda d: stage.at[d], planes, oz_s, oz_r)
    c_line = Line(lambda d: common.at[me, lax.div(d, half), d % half], planes, cz_s, cz_r)

    def exchange(mask):
        peer = flip_mask(me, mask, bits)
        return remote(w_in.at[peer], w.at[dp, me], a2a_s.at[mask], a2a_r.at[mask], (dp, peer))

    def arrived(mask):
        ref = w.at[dp, flip_mask(me, mask, bits)]
        return pltpu.make_async_copy(ref, ref, a2a_r.at[mask])

    for mask in range(1, ranks):
        exchange(mask).start()
    places = [
        pltpu.make_async_copy(w_in.at[me], w.at[dp, me], local.at[0]),
        pltpu.make_async_copy(common_in, common.at[me, lax.div(dp, half), dp % half], local.at[1]),
        pltpu.make_async_copy(wout_in, stage.at[dp], local.at[2]),
        pltpu.make_async_copy(tok_in, tok.at[me], local.at[3]),
        pltpu.make_async_copy(cot_in, cot.at[me], local.at[4]),
    ]
    for place in places:
        place.start()
    for h in range(2):
        tokens.start(h, 0)
    for place in places:
        place.wait()
    c_line.start(1)
    for hop in range(1, planes):
        c_line.forward(hop)
    for mask in range(1, ranks):
        arrived(mask).wait()
    w_line.start(1)
    o_line.start(1)
    tokens.forward(0)
    for h in range(2):
        commons.start(h, 0)
    for h in range(2):
        cots.start(h, 0)
    w_line.forward(1)
    o_line.forward(1)
    for group in range(1, tokens.groups - 1):
        tokens.forward(group)
    for group in range(commons.groups - 1):
        commons.forward(group)
    for hop in range(2, planes - 1):
        w_line.forward(hop)
    tokens.forward(tokens.groups - 1)
    commons.forward(commons.groups - 1)
    if fused:
        norm_tokens(tok, common, normed, w.shape[2], w_full)
    cots.forward(0)
    for hop in range(2, planes - 1):
        o_line.forward(hop)
    w_line.forward(planes - 1)
    o_line.forward(planes - 1)

    def moved(d):
        index = d * ranks + me
        return lax.div(index, planes), index % planes

    for d in range(planes):
        to, place = moved(d)

        @pl.when(to == me)
        def _():
            pltpu.make_async_copy(stage.at[d], wout.at[place], mix_r.at[place]).start()

        @pl.when(to != me)
        def _():
            remote(stage.at[d], wout.at[place], mix_s.at[d], mix_r.at[place], (dp, to)).start()

    if fused:
        project(w, normed, flipped, proj, raw, w_full, flip_out, proj_out, store)
        full = pltpu.make_async_copy(w_full, full_out, local.at[0])
        full.start()
    for group in range(1, cots.groups):
        cots.forward(group)
    for place in range(planes):
        pltpu.make_async_copy(wout.at[place], wout.at[place], mix_r.at[place]).wait()
    for d in range(planes):
        to, place = moved(d)

        @pl.when(to != me)
        def _():
            remote(stage.at[d], wout.at[place], mix_s.at[d], mix_r.at[place], (dp, to)).wait_send()

    for mask in range(1, ranks):
        exchange(mask).wait_send()
    for ring in (tokens, cots, commons, w_line, o_line, c_line):
        ring.finish()
    if fused:
        full.wait()
        for i in range(store.shape[1]):
            for copy in stored(i, flipped, proj, flip_out, proj_out, store):
                copy.wait()


def gather_all(ranks, planes, tok, cot, w, w_out, common):
    length, d = tok.shape
    halves = (2, length // 2, d)
    total = ranks * length
    rows, cols = w.shape[1:]
    fused = rows % 16 == 0 and rows * HDIM >= 2 * d and length % 256 == 0 and cols % 384 == 0
    dma = pltpu.SemaphoreType.DMA
    vmem = pl.BlockSpec(memory_space=pltpu.VMEM)
    ring, line = 2 * ranks, 2 * planes
    anywhere = pl.BlockSpec(memory_space=pl.ANY)
    buffers = [((ranks,) + halves, bf16), ((planes,) + w.shape, bf16)]
    out = [
        ((ranks,) + halves, bf16), ((planes,) + w_out.shape, bf16), ((ranks, 2, planes // 2) + common.shape, bf16)
    ]
    places = [vmem, vmem, vmem]
    stores = []
    if fused:
        own = [((d, total), bf16), ((total, cols + 2 * NSTATE), bf16), ((d, cols + common.shape[1]), bf16)]
        out += [((HDIM, total), f32)] + own
        places += [vmem, anywhere, anywhere, anywhere]
        stores = [pltpu.VMEM(*s) for s in buffers + [((total, d), bf16)] + own] + [dma((2, total // 256))]
    else:
        out += buffers
        places += [vmem, vmem]
    cot_all, out_all, common_all, *rest = pl.pallas_call(
        partial(gather_kernel, fused),
        in_specs=[anywhere] * 5,
        out_specs=places,
        out_shape=[jax.ShapeDtypeStruct(*s) for s in out],
        scratch_shapes=stores
        + [pltpu.VMEM((planes,) + w_out.shape, bf16)]
        + [dma((ring,))] * 6
        + [dma((line,))] * 6
        + [dma((ranks,)), dma((ranks,)), dma((planes,)), dma((planes,)), dma((5,))],
        compiler_params=pltpu.CompilerParams(
            collective_id=0, has_side_effects=True, vmem_limit_bytes=67043328
        ),
        name="gather_all",
    )(tok.reshape(halves), cot.reshape(halves), w, w_out, common)
    common_all = common_all.reshape((ranks, planes) + common.shape).transpose(1, 0, 2, 3)
    cot_all, out_all = cot_all.reshape(total, d), out_all.reshape(planes * w_out.shape[0], d)
    if fused:
        return (cot_all, out_all, common_all, True) + tuple(rest)
    tok_all, w_all = rest
    return cot_all, out_all, common_all, False, tok_all.reshape(total, d), w_all.reshape(-1, cols)


def plane_sum_kernel(x_in, total, land, send, recv):
    ranks = land.shape[0]
    me, dp = lax.axis_index("seq"), lax.axis_index("dp")
    bits = bits_of(ranks)
    barrier = pltpu.get_barrier_semaphore()
    for mask in range(1, ranks):
        pl.semaphore_signal(barrier, inc=1, device_id=(dp, flip_mask(me, mask, bits)), device_id_type=MESH)
    pl.semaphore_wait(barrier, ranks - 1)

    def copy(mask):
        return remote(x_in, land.at[mask], send.at[mask], recv.at[mask], (dp, flip_mask(me, mask, bits)))

    for mask in range(1, ranks):
        copy(mask).start()
    value = x_in[...]
    for mask in range(1, ranks):
        copy(mask).wait_recv()
        value = value + land[mask]
    total[...] = value
    for mask in range(1, ranks):
        copy(mask).wait_send()


def plane_sum(ranks, x):
    vmem = pl.BlockSpec(memory_space=pltpu.VMEM)
    return pl.pallas_call(
        plane_sum_kernel,
        in_specs=[vmem],
        out_specs=vmem,
        out_shape=jax.ShapeDtypeStruct(x.shape, f32),
        scratch_shapes=[pltpu.VMEM((ranks,) + x.shape, f32)] + [pltpu.SemaphoreType.DMA((ranks,))] * 2,
        compiler_params=pltpu.CompilerParams(collective_id=2, has_side_effects=True),
        name="plane_sum",
    )(x)


def add_into(dst, pieces, rows):
    count = dst.shape[-2]
    rows = 16 if count % 16 == 0 else count

    def body(i, _):
        at = pl.ds(pl.multiple_of(i * rows, rows), rows)
        total = pieces[0][at, :].astype(f32)
        for piece in pieces[1:]:
            total = total + piece[at, :].astype(f32)
        dst[at, :] = total.astype(dst.dtype)
        return 0

    lax.fori_loop(0, count // rows, body, 0)


def flat_views(ref):
    if len(ref.shape) == 2:
        return [ref]
    return [view for k in range(ref.shape[0]) for view in flat_views(ref.at[k])]


def add_all(dst, pieces, rows):
    for views in zip(flat_views(dst), *(flat_views(p) for p in pieces)):
        add_into(views[0], views[1:], rows)


class Collect:
    def __init__(self, acc, land, send, recv, rows):
        self.size = acc.shape[0]
        self.bits = bits_of(self.size)
        self.orders = both_orders(self.size)
        self.acc, self.land, self.send, self.recv, self.rows = acc, land, send, recv, rows
        self.me, self.dp = lax.axis_index("seq"), lax.axis_index("dp")

    def copy(self, half, mask, bit):
        slot = half * (self.size - 1) + (mask | bit) - 1
        owner = flip_mask(self.me, mask | bit, self.bits)
        return remote(
            self.acc.at[owner, half], self.land.at[slot], self.send.at[slot], self.recv.at[slot],
            (self.dp, flip(self.me, bit)),
        )

    def subsets(self, bits):
        got = [0]
        for bit in bits:
            got = got + [m | bit for m in got]
        return got

    def arrivals(self, half, mask, after):
        pieces = []
        for bit in self.orders[half][after:]:
            slot = half * (self.size - 1) + (mask | bit) - 1
            pltpu.make_async_copy(self.land.at[slot], self.land.at[slot], self.recv.at[slot]).wait()
            pieces.append(self.land.at[slot])
        return pieces

    def push(self, k):
        for half in range(2):
            order = self.orders[half]
            for mask in self.subsets(order[:k]):
                full = mask | order[k]
                pieces = self.arrivals(half, full, k + 1)
                if pieces:
                    ref = self.acc.at[flip_mask(self.me, full, self.bits), half]
                    add_all(ref, [ref] + pieces, self.rows)
                self.copy(half, mask, order[k]).start()

    def total(self, dst):
        for half in range(2):
            pieces = self.arrivals(half, 0, 0)
            add_all(dst.at[half], [self.acc.at[self.me, half]] + pieces, self.rows)

    def finish(self):
        for half in range(2):
            order = self.orders[half]
            for k in range(len(order)):
                for mask in self.subsets(order[:k]):
                    self.copy(half, mask, order[k]).wait_send()


class Fold:
    def __init__(self, at, land, size, send, recv, rows):
        self.at, self.land, self.size, self.send, self.recv, self.rows = at, land, size, send, recv, rows
        self.me, self.seq = lax.axis_index("dp"), lax.axis_index("seq")

    def copy(self, way, block):
        slot = (self.size if way > 0 else 0) + block
        return remote(
            self.at(block), self.land.at[slot], self.send.at[slot], self.recv.at[slot], (self.me + way, self.seq)
        )

    def landed(self, way, block):
        slot = (self.size if way > 0 else 0) + block
        ref = self.land.at[slot]
        pltpu.make_async_copy(ref, ref, self.recv.at[slot]).wait()
        return ref

    def sends(self, way, block):
        return block > self.me if way > 0 else block < self.me

    def push(self, t):
        last = self.size - 1
        for way, block in ((1, last + self.me - t), (-1, t - last + self.me)):
            @pl.when((block >= 0) & (block <= last))
            def _():
                behind = self.me - way

                @pl.when((behind >= 0) & (behind < self.size))
                def _():
                    add_all(self.at(block), [self.at(block), self.landed(way, block)], self.rows)

                self.copy(way, block).start()

    def total(self, dst):
        me = self.me
        add_all(dst, [self.at(me)], self.rows)
        for way in (1, -1):
            behind = me - way

            @pl.when((behind >= 0) & (behind < self.size))
            def _():
                add_all(dst, [dst, self.landed(way, me)], self.rows)

    def finish(self):
        for t in range(self.size):
            for way in (1, -1):
                @pl.when(self.sends(way, t))
                def _():
                    self.copy(way, t).wait_send()


def reduce_kernel(fused, s_in, *refs):
    if fused:
        flip_in, dproj_in, wfull_in, *refs = refs
    else:
        dn_in, w_in, c_in, *refs = refs
    (dn_sum, w_sum, c_sum, s_sum, dn_acc, w_acc, c_acc, s_acc, own,
     dn_land, w_land, c_land, s_land, cz_land, sz_land,
     dn_s, dn_r, cr_s, cr_r, sr_s, sr_r, wz_s, wz_r, cz_s, cz_r, sz_s, sz_r, a2a_s, a2a_r, local, *refs) = refs
    ranks, planes = dn_acc.shape[0], w_acc.shape[0]
    me, dp = lax.axis_index("seq"), lax.axis_index("dp")
    bits = bits_of(ranks)
    half = planes // 2
    top = len(bits) - 1
    rows, cols = w_acc.shape[2:]
    tokens = dn_acc.shape[2]
    if fused:
        flipped, dproj, w_full = refs
        pairs = [(flip_in, flipped), (dproj_in, dproj), (s_in, s_acc), (wfull_in, w_full)]
    else:
        pairs = [(w_in, w_acc), (c_in, c_acc), (s_in, s_acc), (dn_in, dn_acc)]
    loads = [pltpu.make_async_copy(src, dst, local.at[k]) for k, (src, dst) in enumerate(pairs)]
    for load in loads:
        load.start()
    greet(ranks, planes)
    dns = Collect(dn_acc, dn_land, dn_s, dn_r, 16)
    cs = Collect(c_acc, c_land, cr_s, cr_r, c_acc.shape[-2])
    ss = Collect(s_acc, s_land, sr_s, sr_r, 8)

    def own_c(d):
        return c_acc.at[me, lax.div(d, half), d % half]

    def own_s(d):
        return s_acc.at[me, lax.div(d, half), d % half]

    w_fold = Fold(lambda d: w_acc.at[d], w_land, planes, wz_s, wz_r, rows)
    c_fold = Fold(own_c, cz_land, planes, cz_s, cz_r, c_acc.shape[-2])
    s_fold = Fold(own_s, sz_land, planes, sz_s, sz_r, 8)

    def weight_rows(plane):
        left = pl.ds(plane * ranks * rows, ranks * rows)
        for start in range(0, dproj.shape[1], 384):
            cut = slice(start, start + 384)
            block = dot(flipped[left, :], dproj[:, cut], NN).astype(bf16)
            for rank in range(ranks):
                piece = block[rank * rows : (rank + 1) * rows]
                if start < cols:
                    w_acc[plane, rank, :, cut] = piece
                else:
                    c_acc[rank, plane // half, plane % half, :, start - cols : start - cols + 384] = piece

    def token_half(far):
        mine = me % 2

        def body(i, _):
            rank = 2 * i + (1 - mine if far else mine)
            at = pl.ds(pl.multiple_of(2 * rank * tokens, 16), 2 * tokens)
            for start in range(0, w_full.shape[0], 512):
                cut = slice(start, start + 512)
                block = dot(dproj[at, :], w_full[cut, :], NT).astype(bf16)
                for h in range(2):
                    dn_acc[rank, h, :, cut] = block[h * tokens : (h + 1) * tokens]
            return 0

        lax.fori_loop(0, ranks // 2, body, 0)

    order = []
    for t in range(half):
        order.append((planes - 1 - t, t))
    if fused:
        for load in loads:
            load.wait()
        for plane in order[0]:
            weight_rows(plane)
        w_fold.push(0)
        token_half(True)
        dns.push(top)
        ss.push(top)
        for pair in order[1:]:
            for plane in pair:
                weight_rows(plane)
        cs.push(top)
        token_half(False)
    else:
        for load in loads:
            load.wait()
        w_fold.push(0)
        dns.push(top)
        cs.push(top)
        ss.push(top)
    for k in reversed(range(1, top)):
        for ring in (dns, ss, cs):
            ring.push(k)
    w_fold.push(1)
    for ring in (dns, ss, cs):
        ring.push(0)
    for t in range(2, planes - 1):
        w_fold.push(t)
    dns.total(dn_sum)
    for h in range(2):
        for ring in (ss, cs):
            pieces = ring.arrivals(h, 0, 0)
            ref = ring.acc.at[me, h]
            add_all(ref, [ref] + pieces, ring.rows)
    w_fold.total(own)

    def exchange(mask):
        peer = flip_mask(me, mask, bits)
        return remote(own.at[peer], w_sum.at[me], a2a_s.at[mask], a2a_r.at[mask], (dp, peer))

    for mask in range(1, ranks):
        exchange(mask).start()
    keep = pltpu.make_async_copy(own.at[me], w_sum.at[me], local.at[0])
    keep.start()
    for t in range(planes - 1):
        c_fold.push(t)
        s_fold.push(t)
    c_fold.total(c_sum)
    s_fold.total(s_sum)
    keep.wait()
    for mask in range(1, ranks):
        ref = w_sum.at[flip_mask(me, mask, bits)]
        pltpu.make_async_copy(ref, ref, a2a_r.at[mask]).wait()
    for mask in range(1, ranks):
        exchange(mask).wait_send()
    for ring in (dns, cs, ss, w_fold, c_fold, s_fold):
        ring.finish()


def reduce_all(fused, ranks, planes, rows, cols, small, *operands):
    if fused:
        flipped, dproj, w_full = operands
        d, length = flipped.shape[0], dproj.shape[0] // ranks
        wide = w_full.shape[1] - cols
    else:
        dn, w, common = operands
        d, length, wide = dn.shape[-1], 2 * dn.shape[2], common.shape[-1]
    part = (2, length // 2, d)
    wshape = (planes, ranks, rows, cols)
    cshape = (ranks, 2, planes // 2, rows, wide)
    dma = pltpu.SemaphoreType.DMA
    vmem = pl.BlockSpec(memory_space=pltpu.VMEM)
    ring, line = 2 * (ranks - 1), 2 * planes
    results = pl.pallas_call(
        partial(reduce_kernel, fused),
        in_specs=[pl.BlockSpec(memory_space=pl.ANY)] * 4,
        out_specs=[vmem] * 4,
        out_shape=[
            jax.ShapeDtypeStruct(part, f32),
            jax.ShapeDtypeStruct((ranks, rows, cols), bf16),
            jax.ShapeDtypeStruct((rows, wide), f32),
            jax.ShapeDtypeStruct(small.shape[3:], f32),
        ],
        scratch_shapes=[
            pltpu.VMEM((ranks,) + part, bf16),
            pltpu.VMEM(wshape, bf16),
            pltpu.VMEM(cshape, bf16),
            pltpu.VMEM(small.shape, f32),
            pltpu.VMEM(wshape[1:], bf16),
            pltpu.VMEM((ring,) + part[1:], bf16),
            pltpu.VMEM((line,) + wshape[1:], bf16),
            pltpu.VMEM((ring,) + cshape[2:], bf16),
            pltpu.VMEM((ring,) + small.shape[2:], f32),
            pltpu.VMEM((line,) + cshape[3:], bf16),
            pltpu.VMEM((line,) + small.shape[3:], f32),
        ]
        + [dma((ring,))] * 6
        + [dma((line,))] * 6
        + [dma((ranks,)), dma((ranks,)), dma((4,))]
        + ([pltpu.VMEM(a.shape, bf16) for a in operands] if fused else []),
        compiler_params=pltpu.CompilerParams(
            collective_id=1, has_side_effects=True, vmem_limit_bytes=67043328
        ),
        name="reduce_all",
    )(small, *operands)
    dn_sum, w_sum, c_sum, s_sum = results
    return dn_sum.reshape(length, d), w_sum, c_sum, s_sum


def dot(a, b, dims, precision=None):
    return lax.dot_general(
        a, b, (dims, ((), ())), preferred_element_type=f32, precision=precision
    )


NN, NT, TN = ((1,), (0,)), ((1,), (1,)), ((0,), (0,))


def sigmoid(a):
    return 0.5 * jnp.tanh(0.5 * a) + 0.5


def iota(shape, axis):
    return lax.broadcasted_iota(jnp.int32, shape, axis)


def parts(a):
    high = a.astype(bf16)
    return high, (a - high.astype(f32)).astype(bf16)


def fine(a, b, dims):
    left = jnp.concatenate([a[0], a[0], a[1]], axis=dims[0][0])
    right = jnp.concatenate([b[0], b[1], b[0]], axis=dims[1][0])
    return dot(left, right, dims)


def steps_of(raw, bias):
    shifted = raw + bias
    return jnp.maximum(shifted, 0.0) + jnp.log1p(jnp.exp(-jnp.abs(shifted)))


def convolve(pad, conv_ref, tile, count):
    total = conv_ref[CONVK : CONVK + 1, tile]
    for k in range(CONVK):
        total = total + pad[EDGE - CONVK + 1 + k : EDGE - CONVK + 1 + k + count, tile] * conv_ref[k : k + 1, tile]
    return total


class Chunk:
    def __init__(self, step, rate):
        n = SUB
        upper = jnp.where(iota((n, n), 0) <= iota((n, n), 1), 1.0, 0.0)
        self.step = step
        self.rows = dot(step * -rate, upper, NN, highest)
        self.cols = self.rows.T
        self.step_cols = step.T

    def col(self, h):
        return jnp.broadcast_to(self.cols[:, h : h + 1], (SUB, SUB))

    def decay(self, h, col, hide):
        return jnp.exp(col - self.rows[h : h + 1, :] + hide)

    def step_col(self, h):
        return jnp.broadcast_to(self.step_cols[:, h : h + 1], (SUB, SUB))


def fwd_kernel(
    proj_ref, raw_ref, cot_ref, wout_ref, conv_ref, lane_ref, head_ref,
    y_ref, dg_ref, out_ref, state_ref, sum_ref, gated,
    pad, act, carry,
):
    block = proj_ref.shape[0]
    din = y_ref.shape[1]
    conv = conv_ref.shape[1]

    @pl.when(pl.program_id(0) == 0)
    def _():
        carry[...] = jnp.zeros_like(carry)
        pad[0:EDGE, :] = jnp.zeros((EDGE, conv), f32)

    @pl.when(pl.program_id(0) > 0)
    def _():
        pad[0:EDGE, :] = pad[block : block + EDGE, :]

    for j in range(conv // LANES):
        tile = slice(j * LANES, (j + 1) * LANES)
        pad[EDGE:, tile] = proj_ref[:, din + j * LANES : din + (j + 1) * LANES].astype(f32)
        filtered = convolve(pad, conv_ref, tile, block)
        act[:, tile] = filtered * sigmoid(filtered)
    dg_ref[...] = dot(cot_ref[...], wout_ref[...], NT)

    low = iota((SUB, LANES), 1) < HDIM
    hide = jnp.where(iota((SUB, SUB), 0) >= iota((SUB, SUB), 1), 0.0, -1e30)
    for i in range(block // SUB):
        rows = slice(i * SUB, (i + 1) * SUB)
        b, c = parts(act[rows, din : din + NSTATE]), parts(act[rows, din + NSTATE :])
        chunk = Chunk(steps_of(raw_ref[:, rows], head_ref[1]), head_ref[0])
        scores = fine(c, b, NT)
        sq = jnp.zeros((SUB, LANES), f32)
        cross = jnp.zeros((SUB, LANES), f32)
        for j in range(din // LANES):
            tile = slice(j * LANES, (j + 1) * LANES)
            x = act[rows, tile]
            col0, col1 = chunk.col(2 * j), chunk.col(2 * j + 1)
            m0 = chunk.decay(2 * j, col0, hide) * scores
            m1 = chunk.decay(2 * j + 1, col1, hide) * scores
            cexp = jnp.where(low, col0, col1)
            xs = x * jnp.where(low, chunk.step_col(2 * j), chunk.step_col(2 * j + 1))
            zero = jnp.zeros_like(xs)
            split = jnp.concatenate([jnp.where(low, xs, zero), jnp.where(low, zero, xs)], axis=0)
            before = carry[:, tile]
            state_ref[i, :, tile] = before
            y = fine(parts(jnp.concatenate([m0, m1], axis=1)), parts(split), NN)
            y = y + fine(c, parts(before), NN) * jnp.exp(cexp)
            y_ref[rows, tile] = y
            last = cexp[SUB - 1 :, :]
            carry[:, tile] = before * jnp.exp(last) + fine(b, parts(xs * jnp.exp(last - cexp)), TN)
            z = proj_ref[rows, tile].astype(f32)
            v = (y + lane_ref[0:1, tile] * x) * (z * sigmoid(z))
            scaled = v * lane_ref[1:2, tile]
            gated[rows, tile] = scaled.astype(bf16)
            sq = sq + v * v
            cross = cross + scaled * dg_ref[rows, tile]
        ones = jnp.ones((4, LANES), f32)
        sum_ref[0:4, rows] = dot(ones, sq, NT, highest)
        sum_ref[4:8, rows] = dot(ones, cross, NT, highest)
    out_ref[...] = dot(gated[...], wout_ref[...], NN).astype(bf16)


def bwd_kernel(
    total_din,
    proj_ref, rim_ref, raw_ref, y_ref, dg_ref, sum_ref, state_ref, conv_ref, lane_ref, head_ref, spot_ref,
    out_in, o_in,
    dproj_ref, dconv_ref, dlane_ref, dhead_ref, out_sum, o_sum,
    pad, act, slope, dpad, carry, edge, dact,
    *links,
):
    side_reduce(out_in, o_in, out_sum, o_sum, *links)

    block = proj_ref.shape[0]
    din = y_ref.shape[1]
    conv = conv_ref.shape[1]
    step_id = pl.program_id(0)
    first = step_id == pl.num_programs(0) - 1

    @pl.when(step_id == 0)
    def _():
        carry[...] = jnp.zeros_like(carry)
        edge[...] = jnp.zeros_like(edge)
        dpad[0:EDGE, :] = jnp.zeros((EDGE, conv), f32)
        dconv_ref[...] = jnp.zeros_like(dconv_ref)
        dlane_ref[...] = jnp.zeros_like(dlane_ref)
        dhead_ref[...] = jnp.zeros_like(dhead_ref)

    dpad[block : block + EDGE, :] = dpad[0:EDGE, :]
    keep = jnp.where(first, 0.0, 1.0)
    for j in range(conv // LANES):
        tile = slice(j * LANES, (j + 1) * LANES)
        src = slice(din + j * LANES, din + (j + 1) * LANES)
        pad[0:EDGE, tile] = rim_ref[rim_ref.shape[0] - EDGE :, src].astype(f32) * keep
        pad[EDGE:, tile] = proj_ref[:, src].astype(f32)
        filtered = convolve(pad, conv_ref, tile, block)
        s = sigmoid(filtered)
        act[:, tile] = filtered * s
        slope[:, tile] = s * (1.0 + filtered * (1.0 - s))

    low = iota((SUB, LANES), 1) < HDIM
    hide = jnp.where(iota((SUB, SUB), 0) >= iota((SUB, SUB), 1), 0.0, -1e30)
    lower = jnp.where(iota((SUB, SUB), 0) >= iota((SUB, SUB), 1), 1.0, 0.0)
    heads = raw_ref.shape[0]
    dgain = [jnp.zeros((1, LANES), f32) for _ in range(din // LANES)]
    dskip = [jnp.zeros((1, LANES), f32) for _ in range(din // LANES)]
    for i in reversed(range(block // SUB)):
        rows = slice(i * SUB, (i + 1) * SUB)
        b_parts, c_parts = parts(act[rows, din : din + NSTATE]), parts(act[rows, din + NSTATE :])
        chunk = Chunk(steps_of(raw_ref[:, rows], head_ref[1]), head_ref[0])
        scores = fine(c_parts, b_parts, NT)
        sums = sum_ref[:, rows].T
        scale = lax.rsqrt(jnp.broadcast_to(sums[:, 0:1], (SUB, LANES)) * (1.0 / total_din) + epsilon)
        mean = jnp.broadcast_to(sums[:, 4:5], (SUB, LANES)) * (1.0 / total_din) * (scale * scale * scale)
        dscores = jnp.zeros((SUB, SUB), f32)
        d_b = jnp.zeros((SUB, NSTATE), f32)
        d_c = jnp.zeros((SUB, NSTATE), f32)
        d_cum = jnp.zeros((heads, SUB), f32)
        d_step = jnp.zeros((heads, SUB), f32)
        reach = jnp.zeros((heads, 8), f32)
        for j in range(din // LANES):
            tile = slice(j * LANES, (j + 1) * LANES)
            x = act[rows, tile]
            y = y_ref[rows, tile]
            skip, gain = lane_ref[0:1, tile], lane_ref[1:2, tile]
            z = proj_ref[rows, tile].astype(f32)
            sz = sigmoid(z)
            mixed = y + skip * x
            silu = z * sz
            v = mixed * silu
            dg = dg_ref[rows, tile]
            vs = v * scale
            dgain[j] = dgain[j] + jnp.sum(dg * vs, axis=0, keepdims=True)
            dv = scale * (gain * dg) - v * mean
            dy = dv * silu
            dproj_ref[rows, tile] = (dv * mixed * (sz * (1.0 + z * (1.0 - sz)))).astype(bf16)
            dskip[j] = dskip[j] + jnp.sum(dy * x, axis=0, keepdims=True)

            col0, col1 = chunk.col(2 * j), chunk.col(2 * j + 1)
            l0, l1 = chunk.decay(2 * j, col0, hide), chunk.decay(2 * j + 1, col1, hide)
            m = parts(jnp.concatenate([l0 * scores, l1 * scores], axis=0))
            cexp = jnp.where(low, col0, col1)
            step = jnp.where(low, chunk.step_col(2 * j), chunk.step_col(2 * j + 1))
            last = cexp[SUB - 1 :, :]
            grow, tail = jnp.exp(cexp), jnp.exp(last - cexp)
            xs = x * step
            zero = jnp.zeros_like(dy)
            dsplit = parts(jnp.concatenate([jnp.where(low, dy, zero), jnp.where(low, zero, dy)], axis=0))
            xs_parts = parts(xs)
            dm = fine(dsplit, xs_parts, NT)
            dscores = dscores + dm[:SUB] * l0 + dm[SUB:] * l1
            dend = carry[:, tile]
            dend_parts = parts(dend)
            before = state_ref[i, :, tile]
            dxs = fine(m, dsplit, TN) + fine(b_parts, dend_parts, NN) * tail
            grown = parts(dy * grow)
            d_c = d_c + fine(grown, parts(before), NT)
            d_b = d_b + fine(parts(xs * tail), dend_parts, NT)
            dprev = dend * jnp.exp(last) + fine(c_parts, grown, TN)
            carry[:, tile] = dprev
            pick = jnp.where(lax.shift_right_logical(iota((heads, LANES), 1), 6) + 2 * j == iota((heads, LANES), 0), 1.0, 0.0)
            balance = dy * y - xs * dxs
            d_cum = d_cum + dot(pick, balance, NT, highest)
            d_step = d_step + dot(pick, x * dxs, NT, highest)
            crossing = jnp.sum(dprev * before, axis=0, keepdims=True)
            reach = reach + dot(pick, jnp.broadcast_to(crossing, (8, LANES)), NT, highest)
            dact[rows, tile] = dxs * step + skip * dy
        ds_parts = parts(dscores)
        dact[rows, din : din + NSTATE] = d_b + fine(ds_parts, c_parts, TN)
        dact[rows, din + NSTATE :] = d_c + fine(ds_parts, b_parts, NN)
        d_log = dot(d_cum, lower, NN, highest) + edge[...]
        edge[...] = jnp.broadcast_to(reach[:, 0:1], edge.shape)
        raw = raw_ref[:, rows] + head_ref[1]
        draw = (d_step - head_ref[0] * d_log) * sigmoid(raw)
        dproj_ref[rows, din + conv :] = dot(draw.astype(bf16), spot_ref[...], TN).astype(bf16)
        dhead_ref[0] += -chunk.step * d_log
        dhead_ref[1] += draw
    for j in range(din // LANES):
        tile = slice(j * LANES, (j + 1) * LANES)
        dlane_ref[0:1, tile] += dskip[j]
        dlane_ref[1:2, tile] += dgain[j]
    for j in range(conv // LANES):
        tile = slice(j * LANES, (j + 1) * LANES)
        df = dact[:, tile] * slope[:, tile]
        dpad[0:block, tile] = df
        dconv_ref[CONVK : CONVK + 1, tile] += jnp.sum(df, axis=0, keepdims=True)
        back = jnp.zeros((block, LANES), f32)
        for k in range(CONVK):
            shift = CONVK - 1 - k
            dconv_ref[k : k + 1, tile] += jnp.sum(
                df * pad[EDGE - shift : EDGE - shift + block, tile], axis=0, keepdims=True
            )
            back = back + conv_ref[k : k + 1, tile] * dpad[shift : shift + block, tile]
        dproj_ref[:, din + j * LANES : din + (j + 1) * LANES] = back.astype(bf16)


def rows_spec(block, width):
    return pl.BlockSpec((block, width), lambda t: (t, 0))


def whole(shape):
    return pl.BlockSpec(shape, lambda t: (0,) * len(shape))


def mixer_forward(proj, raw, cot, w_out, conv, lanes, heads):
    length, width = proj.shape
    din, d = w_out.shape
    cc = conv.shape[1]
    block = min(TOKENS, length)
    n = block // SUB
    cols = pl.BlockSpec((8, block), lambda t: (0, t))
    return pl.pallas_call(
        fwd_kernel,
        grid=(length // block,),
        in_specs=[
            rows_spec(block, width), cols, rows_spec(block, d), whole(w_out.shape),
            whole(conv.shape), whole(lanes.shape), whole(heads.shape),
        ],
        out_specs=[
            rows_spec(block, din), rows_spec(block, din), rows_spec(block, d),
            pl.BlockSpec((n, NSTATE, din), lambda t: (t, 0, 0)), cols, rows_spec(block, din),
        ],
        out_shape=[
            jax.ShapeDtypeStruct((length, din), f32),
            jax.ShapeDtypeStruct((length, din), f32),
            jax.ShapeDtypeStruct((length, d), bf16),
            jax.ShapeDtypeStruct((length // SUB, NSTATE, din), f32),
            jax.ShapeDtypeStruct((8, length), f32),
            jax.ShapeDtypeStruct((length, din), bf16),
        ],
        scratch_shapes=[
            pltpu.VMEM((block + EDGE, cc), f32),
            pltpu.VMEM((block, cc), f32),
            pltpu.VMEM((NSTATE, din), f32),
        ],
        name="mix_forward",
    )(proj, raw, cot, w_out, conv, lanes, heads)


def side_reduce(out_in, o_in, out_sum, o_sum, acc, land, stage, o_land, out_s, out_r, oz_s, oz_r, mix_s, mix_r, local):
    ranks, planes = acc.shape[0], stage.shape[0]
    me, dp = lax.axis_index("seq"), lax.axis_index("dp")
    outs = Collect(acc, land, out_s, out_r, 16)
    fold = Fold(lambda d: stage.at[d], o_land, planes, oz_s, oz_r, stage.shape[1])
    top = len(bits_of(ranks)) - 1
    load = pltpu.make_async_copy(out_in, acc, local.at[0])

    def move(k, act):
        index = me * planes + k
        plane, to = lax.div(index, ranks), index % ranks

        @pl.when(to != me)
        def _():
            copy = remote(o_in.at[k], stage.at[plane], mix_s.at[k], mix_r.at[plane], (dp, to))
            copy.start() if act else copy.wait_send()

        if act:
            @pl.when(to == me)
            def _():
                pltpu.make_async_copy(o_in.at[k], stage.at[plane], mix_r.at[plane]).start()

    def begin():
        load.start()
        greet(ranks, planes)
        for k in range(planes):
            move(k, True)
        load.wait()
        outs.push(top)

    def settle():
        for d in range(planes):
            pltpu.make_async_copy(stage.at[d], stage.at[d], mix_r.at[d]).wait()
        fold.push(0)

    def end():
        outs.total(out_sum)
        fold.total(o_sum)
        for k in range(planes):
            move(k, False)
        outs.finish()
        fold.finish()

    pushes = {4 * i + 1: partial(outs.push, top - 1 - i) for i in range(top)}
    folds = [settle] + [partial(fold.push, t) for t in range(1, planes - 1)]
    spare = [t for t in range(3, 64) if t not in pushes]
    stages = {0: begin, **pushes, **dict(zip(spare, folds))}
    last = pl.num_programs(0) - 1
    for k, run in sorted(stages.items()):
        pl.when(pl.program_id(0) == k)(run)
    pl.when(pl.program_id(0) == last)(end)


def mixer_backward(ranks, planes, total_din, proj, raw, y, dg, sums, states, conv, lanes, heads, spot, out_part, d_w_out):
    length, width = proj.shape
    din, d = y.shape[1], out_part.shape[1]
    cc = conv.shape[1]
    block = min(TOKENS, length)
    n = block // SUB
    last = length // block - 1
    rim = 16
    assert last > max(4 * len(bits_of(ranks)) - 7, planes + 1 + (planes > 3))
    part = (2, length // ranks // 2, d)
    ring, line = 2 * (ranks - 1), 2 * planes
    dma = pltpu.SemaphoreType.DMA

    def back(block, width):
        return pl.BlockSpec((block, width), lambda t: (last - t, 0))

    cols = pl.BlockSpec((8, block), lambda t: (0, last - t))
    anywhere = pl.BlockSpec(memory_space=pl.ANY)
    *results, out_sum, o_sum = pl.pallas_call(
        partial(bwd_kernel, total_din),
        grid=(length // block,),
        in_specs=[
            back(block, width),
            pl.BlockSpec((rim, width), lambda t: (jnp.maximum((last - t) * (block // rim) - 1, 0), 0)),
            cols, back(block, din), back(block, din), cols,
            pl.BlockSpec((n, NSTATE, din), lambda t: (last - t, 0, 0)),
            whole(conv.shape), whole(lanes.shape), whole(heads.shape), whole(spot.shape), anywhere, anywhere,
        ],
        out_specs=[
            back(block, width + LANES), whole((8, cc)), whole((8, din)), whole((2, 8, SUB)),
            whole(part), whole(d_w_out.shape[1:]),
        ],
        out_shape=[
            jax.ShapeDtypeStruct((length, width + LANES), bf16),
            jax.ShapeDtypeStruct((8, cc), f32),
            jax.ShapeDtypeStruct((8, din), f32),
            jax.ShapeDtypeStruct((2, 8, SUB), f32),
            jax.ShapeDtypeStruct(part, f32),
            jax.ShapeDtypeStruct(d_w_out.shape[1:], f32),
        ],
        scratch_shapes=[
            pltpu.VMEM((block + EDGE, cc), f32),
            pltpu.VMEM((block, cc), f32),
            pltpu.VMEM((block, cc), f32),
            pltpu.VMEM((block + EDGE, cc), f32),
            pltpu.VMEM((NSTATE, din), f32),
            pltpu.VMEM((8, SUB), f32),
            pltpu.VMEM((block, cc), f32),
            pltpu.VMEM((ranks,) + part, bf16),
            pltpu.VMEM((ring,) + part[1:], bf16),
            pltpu.VMEM(d_w_out.shape, bf16),
            pltpu.VMEM((line,) + d_w_out.shape[1:], bf16),
            dma((ring,)), dma((ring,)), dma((line,)), dma((line,)), dma((planes,)), dma((planes,)), dma((1,)),
        ],
        compiler_params=pltpu.CompilerParams(
            collective_id=3, has_side_effects=True, vmem_limit_bytes=67043328
        ),
        name="mix_backward",
    )(
        proj, proj, raw, y, dg, sums, states, conv, lanes, heads, spot,
        out_part.reshape((ranks,) + part), d_w_out,
    )
    return results + [out_sum.reshape(length // ranks, d), o_sum]


def rms_scale(values, gain):
    mean_sq = jnp.mean(values * values, axis=-1, keepdims=True)
    return values * lax.rsqrt(mean_sq + epsilon) * gain


def widen(array, size, axis):
    pads = [(0, 0)] * array.ndim
    pads[axis] = (0, size - array.shape[axis])
    return jnp.pad(array, pads)


def per_device(
    tokens,
    cotangent,
    in_weight,
    out_weight,
    conv_weight,
    conv_bias,
    norm_gain,
    gate_gain,
    decay_rate,
    dt_bias,
    d_skip,
):
    ranks = lax.axis_size("seq")
    me = lax.axis_index("seq")
    both = ("dp", "seq")
    heads = decay_rate.shape[0] // ranks
    din = heads * HDIM
    padded = -(-din // LANES) * LANES
    din_all = din * ranks
    rows, width = in_weight.shape
    conv_all = din_all + 2 * NSTATE
    main = 2 * padded + 2 * NSTATE

    def mine(array, size, axis=0):
        return lax.dynamic_slice_in_dim(array, me * size, size, axis)

    planes = lax.axis_size("dp")
    x_own = tokens[0].astype(f32)
    send = jnp.concatenate(
        [
            widen(in_weight[:, :din_all].reshape(rows, ranks, din), padded, 2),
            widen(in_weight[:, din_all : 2 * din_all].reshape(rows, ranks, din), padded, 2),
        ],
        axis=2,
    ).transpose(1, 0, 2)
    d = in_weight.shape[0] * ranks * planes
    rank_id = lax.axis_index("dp") * ranks + me
    small = [norm_gain, gate_gain, conv_weight.reshape(-1), conv_bias]
    sizes = [a.shape[0] for a in small]
    room = rows * HDIM - d
    if room >= sum(sizes):
        placed = lax.dynamic_update_slice_in_dim(jnp.zeros((d,), bf16), norm_gain, rank_id * rows, 0)
        packed = jnp.concatenate([placed, widen(jnp.concatenate(small), room, 0)])
    else:
        packed = widen(jnp.concatenate(small), rows * HDIM, 0)
    common = jnp.concatenate(
        [
            in_weight[:, 2 * din_all : 2 * din_all + 2 * NSTATE],
            widen(in_weight[:, din_all + conv_all :], HDIM, 1),
            packed.reshape(rows, HDIM),
        ],
        axis=1,
    )
    cot, w_out, common, fused, *rest = gather_all(
        ranks, planes, tokens[0], cotangent[0], send, out_weight, common
    )
    w_out = widen(w_out, padded, 0)
    packed = common[..., 2 * NSTATE + HDIM :].reshape(ranks * planes, rows * HDIM).astype(f32)
    if room >= sum(sizes):
        packed = packed[:, d:]
    gain_norm, gain_gate, conv_w, conv_b = (
        packed[:, sum(sizes[:k]) : sum(sizes[: k + 1])].reshape(-1) for k in range(4)
    )
    conv_w = conv_w.reshape(-1, CONVK)
    taps = jnp.concatenate([conv_w.T, conv_b[None], jnp.zeros((8 - CONVK - 1, conv_all), f32)], axis=0)
    conv = jnp.concatenate([widen(mine(taps, din, 1), padded, 1), taps[:, din_all:]], axis=1)
    if fused:
        raw, flipped, proj, w_full = rest
    else:
        tok, w_all = rest
        w_full = jnp.concatenate([w_all, common.reshape(-1, common.shape[-1])], axis=1)
        normed = rms_scale(tok.astype(f32), gain_norm).astype(bf16)
        proj = dot(normed, w_full[:, :main], NN).astype(bf16)
        raw = dot(w_full[:, main : main + HDIM].T, normed, NT).astype(bf16).astype(f32)
    raw = widen(mine(raw, heads), 8, 0)
    rate, bias, skip = (mine(a, heads) for a in (decay_rate, dt_bias, d_skip))
    lanes = jnp.stack([jnp.repeat(skip, HDIM), mine(gain_gate, din)])
    lanes = widen(widen(lanes, padded, 1), 8, 0)
    head_rows = jnp.broadcast_to(widen(jnp.stack([rate, bias]), 8, 1)[:, :, None], (2, 8, SUB))

    y, dg, out_part, states, sums, gated = mixer_forward(proj, raw, cot, w_out, conv, lanes, head_rows)
    sums = plane_sum(ranks, sums[::4].reshape(8, -1)).reshape(2, -1)
    inverse = lax.rsqrt(sums[0] / din_all + epsilon)[:, None]
    d_w_out = dot((gated * inverse).astype(bf16), cot, TN)[:din].astype(bf16)
    spot = (jnp.arange(LANES)[None] == me * heads + jnp.arange(8)[:, None]) & (jnp.arange(8)[:, None] < heads)
    d_proj, d_conv, d_lane, d_head, out_sum, grad_out = mixer_backward(
        ranks, planes, din_all, proj, raw, y, dg, jnp.repeat(sums, 4, axis=0), states, conv, lanes, head_rows,
        spot.astype(bf16), out_part, d_w_out.reshape(planes, -1, d),
    )

    def by_owner(array):
        split = array.reshape((2, planes // 2, ranks) + array.shape[1:])
        return split.transpose((2, 0, 1) + tuple(range(3, split.ndim)))

    def place(own, size):
        return lax.dynamic_update_slice_in_dim(
            jnp.zeros((size * ranks,) + own.shape[1:], f32), own, me * size, 0
        )

    d_cw, d_cb = d_conv[:CONVK].T, d_conv[CONVK]
    full_cw = jnp.concatenate([place(d_cw[:din], din), d_cw[padded:]], axis=0)
    full_cb = jnp.concatenate([place(d_cb[:din], din), d_cb[padded:]], axis=0)
    d_skp = jnp.sum(d_lane[0, :din].reshape(heads, HDIM), axis=1)
    d_rate, d_bias = jnp.sum(d_head, axis=2)[:, :heads]
    devices = planes * ranks
    head_part = jnp.concatenate([place(a, heads) for a in (d_rate, d_bias, d_skp)])
    fields = [
        a.reshape(devices, -1) for a in (full_cw, full_cb, place(d_lane[1, :din], din))
    ] + [jnp.broadcast_to(head_part, (devices,) + head_part.shape)]
    ends = [0]
    for a in fields:
        ends.append(ends[-1] + a.shape[1])
    small = widen(jnp.concatenate(fields, axis=1), 8 * LANES, 1).reshape(devices, 8, LANES)
    if fused:
        operands = flipped, d_proj, w_full
    else:
        d_w = dot(normed, d_proj, TN).astype(bf16)
        part = dot(d_proj, w_full, NT).astype(bf16)
        operands = (
            part.reshape(ranks, 2, -1, d),
            d_w[:, : 2 * padded].reshape(planes, ranks, rows, -1),
            by_owner(d_w[:, 2 * padded :].reshape(planes * ranks, rows, -1)),
        )
    d_normed, w_sum, bc_sum, small_sum = reduce_all(
        fused, ranks, planes, rows, 2 * padded, by_owner(small), *operands
    )
    block_out = (x_own + mine(inverse, x_own.shape[0]) * out_sum).astype(bf16)
    gain = gain_norm * d_normed
    inv = lax.rsqrt(jnp.mean(x_own * x_own, axis=1, keepdims=True) + epsilon)
    d_xn = inv * (gain - x_own * (inv * inv * jnp.mean(gain * x_own, axis=1, keepdims=True)))
    grad_x = cotangent[0].astype(f32) + d_xn
    spread = w_sum.astype(f32).transpose(1, 0, 2)
    grad_in = jnp.concatenate(
        [
            spread[:, :, :din].reshape(rows, din_all),
            spread[:, :, padded : padded + din].reshape(rows, din_all),
            bc_sum[:, : 2 * NSTATE + heads * ranks],
        ],
        axis=1,
    )
    g_gain = jnp.sum(grad_in * in_weight.astype(f32), axis=1) / norm_gain.astype(f32)
    small_sum = small_sum.reshape(-1)
    g_cw, g_cb, g_gate, head_sums = (small_sum[a:b] for a, b in zip(ends[:-1], ends[1:]))
    g_cw = g_cw.reshape(-1, CONVK)
    head_sums = head_sums.reshape(3, -1)
    return (
        block_out[None],
        grad_x[None],
        grad_in,
        grad_out,
        g_cw,
        g_cb,
        g_gain,
        g_gate,
        head_sums[0],
        head_sums[1],
        head_sums[2],
    )


def solution(mesh):
    rows = P(("dp", "seq"), None)
    flat = P(("dp", "seq"))
    act = P("dp", "seq", None)
    return jax.shard_map(
        per_device,
        mesh=mesh,
        in_specs=(act, act, rows, rows, rows, flat, flat, flat, P(), P(), P()),
        out_specs=(act, act, rows, rows, rows, flat, flat, flat, P(), P(), P()),
        check_vma=False,
    )
```

time: 885 us -> 320 us (0.36)
  waiting for transfers between devices: 600 us -> 0 us
  Pallas kernels: 66.9 us -> 267 us
  blocking collectives: 108 us -> 0 us
  matrix products: 46.1 us -> 7.01 us
  between operations: 14.6 us -> 1.1 us
    reduce_scatter x4 -> x0, waiting for transfers between devices: 283 us -> none  [the longest x1 138 us: per_device(): lax.psum_scatter(full_out, both, scatter_dimension=0, tiled=True)]
    pallas_call x0 -> x3, Pallas kernels: none -> 179 us  [the longest x1 98.5 us: gather_all(): pl.pallas_call(partial(gather_kernel, fused), in_specs=[anywhere] * 5, ou...]
    unnamed x11 -> x0, waiting for transfers between devices: 132 us -> none
    all_gather x4 -> x0, waiting for transfers between devices: 118 us -> none  [the longest x1 66 us: per_device(): lax.all_gather(out_weight, both, axis=0, tiled=True)]
    psum x1 -> x0, waiting for transfers between devices: 53.1 us -> none  [per_device(): sums = lax.psum(sums, 'seq')]
    all_gather x1 -> x0, blocking collectives: 42.4 us -> none  [per_device(): lax.all_gather(a, both, axis=0, tiled=True).astype(f32)]
    unnamed x1 -> x0, blocking collectives: 40.6 us -> none
    dot_general x6 -> x1, matrix products: 46.1 us -> 7.01 us  [dot(): lax.dot_general(a, b, (dims, ((), ())), preferred_element_type=f32, preci...]
  transfers between devices with their start and end apart: 11 -> 0, of which waited for: 10 -> 0; matrix products, arithmetic and copies ran while one was open for 8% -> 0% of each run, Pallas kernels for 0% -> 0%
where the time goes in v4:
time: 320 us; the launch traced here: 319 us
  Pallas kernels  267 us (83%)
  local copies, waits for them, and re-layouts  27.4 us (9%)
  other arithmetic  16.8 us (5%)
  matrix products  7.01 us (2%)
    pallas_call x1, Pallas kernels, gather_all(): pl.pallas_call(partial(gather_kernel, fused), in_specs=[anywhere] * 5, ou...  98.5 us
    pallas_call x1, Pallas kernels, reduce_all(): pl.pallas_call(partial(reduce_kernel, fused), in_specs=[pl.BlockSpec(memo...  72.8 us
    pallas_call x1, Pallas kernels, mixer_backward(): pl.pallas_call(partial(bwd_kernel, total_din), grid=(length // block,), i...  58.2 us
    pallas_call x1, Pallas kernels, mixer_forward(): pl.pallas_call(fwd_kernel, grid=(length // block,), in_specs=[rows_spec(b...  30.1 us
    pallas_call x1, Pallas kernels, plane_sum(): pl.pallas_call(plane_sum_kernel, in_specs=[vmem], out_specs=vmem, out_sha...  7.33 us
    dot_general x1, matrix products, dot(): lax.dot_general(a, b, (dims, ((), ())), preferred_element_type=f32, preci...  7.01 us

profile of v4, /device:TPU:0, one launch (start us, length us, event | category | flops | bytes accessed | tf_op | source)
XLA Modules:
  0.0 319.3 jit_solution(14985335942336805409)
XLA Ops:
  0.7 0.7 dynamic_slice.21
  1.4 0.6 pad.52.clone
  2.0 0.7 fusion.18.spot_ref
  2.6 1.9 fusion.1
  4.6 0.7 dynamic-slice_bitcast_fusion
  5.4 0.6 stack_reshape.3
  6.1 0.8 dynamic_update_slice.21
  7.0 0.7 broadcast_in_dim.17.head_ref
  7.7 0.7 slice.115
  8.4 0.7 slice.114
  9.1 0.8 copy.37
  10.0 0.8 fusion.16
  10.9 0.7 fusion.9.common_in
  11.6 1.1 fusion.19
  12.7 0.9 maximum_bitcast_fusion.w_in
  13.6 98.5 %gather_all.1 = (bf16[8,2,128,1536]{3,2,1,0:T(8,128)(2,1)}, bf16[4,96,1536]{2,1,0:T(8,128)(2,1)}, bf16[8,2,2,48,384]{4,3,2,1,0:T(8,128)(2,1)}, f32[64,2048]{1,0:...) custom-call(bf16[2,128,1536]{2,1,0:T(8,128)(2,1)} %bitcast.63, ...), custom_call_target="tpu_custom_call" | custom-call | tf_op jit(solution)/shard_map/gather_all/pallas_call | solution.py:381
  112.2 0.9 constant_dynamic-slice_fusion.1
  113.1 0.6 pad.26.raw_ref
  113.7 1.2 slice_convert_fusion
  115.2 0.7 mul.127
  116.1 0.6 select_maximum_fusion.lane_ref
  118.2 0.6 pad_maximum_fusion.2.conv_ref
  118.8 30.1 %mix_forward.1 = (f32[2048,384]{1,0:T(8,128)}, f32[2048,384]{1,0:T(8,128)}, bf16[2048,1536]{1,0:T(8,128)(2,1)}, f32[16,128,384]{2,1,0:T(8,128)}, f32[8,2048]{1,0:T(8,128)}, /*index=5*/bf16[2048,384]{1,0:T(8,128)(2,1)}) custom-call(bf16[2048,1024]{1,0:T(8,128)(2,1)} %get-tuple-element.34.proj_ref.rim_ref, f32[8,2048]{1,0:T(8,128)} %pad.26.raw_ref, ...), custom_call_target="tpu_custom_call" | custom-call | tf_op jit(solution)/shard_map/mix_forward/pallas_call | solution.py:1019
  148.9 0.9 slice.121
  149.8 0.6 reshape.242.x_in
  150.4 7.3 %plane_sum.1 = f32[8,512]{1,0:T(8,128)} custom-call(f32[8,512]{1,0:T(8,128)} %reshape.242.x_in), custom_call_target="tpu_custom_call" | custom-call | tf_op jit(solution)/shard_map/plane_sum/pallas_call | solution.py:429
  157.7 0.7 rsqrt_bitcast_fusion
  158.5 0.7 reshape.243
  159.2 7.0 %convolution_convert_fusion = bf16[384,1536]{1,0:T(8,128)(2,1)} fusion(bf16[2048,1536]{1,0:T(8,128)(2,1)} %bitcast.66, bf16[2048,384]{1,0:T(8,128)(2,1)} %get-tuple-element.44, f32[2048]{0:T(1024)S(1)} %bitcast.82), kind=kOutput, calls=%fused_computation.1 | convolution fusion | flops 2418868224 | bytes 9052160 | tf_op jit(solution)/shard_map/dot_general | solution.py:750
  166.2 0.6 dynamic-slice.3
  166.9 0.7 reshape.244.sum_ref
  167.5 58.2 %mix_backward.1 = (bf16[2048,1152]{1,0:T(8,128)(2,1)}, f32[8,640]{1,0:T(8,128)}, f32[8,384]{1,0:T(8,128)}, f32[2,8,128]{2,1,0:T(8,128)}, f32[2,128,1536]{2,1,0:T(8,128)}, /*index=5*/f32[96,1536]{1,0:T(8,128)}) custom-call(bf16[2048,1024]{1,0:T(8,128)(2,1)} %get-tuple-element.34.proj_ref.rim_ref, bf16[2048,1024]{1,0:T(8,128)(2,1)} %get-tuple-element.34.proj_ref.rim_ref, ...), custom_call_target="tpu_custom_call" | custom-call | tf_op jit(solution)/shard_map/mix_backward/pallas_call | solution.py:1118
  225.7 0.8 reduce_sum.46
  226.7 0.7 slice.129
  227.4 0.7 slice_reduce_fusion.2
  228.1 0.7 slice_bitcast_fusion.2
  229.2 0.8 slice_reduce_fusion
  232.1 0.7 copy.54
  232.7 72.8 %reduce_all.1 = (f32[2,128,1536]{2,1,0:T(8,128)}, bf16[8,48,768]{2,1,0:T(8,128)(2,1)}, f32[48,384]{1,0:T(8,128)}, f32[8,128]{1,0:T(8,128)}) custom-call(f32[8,2,2,8,128]{4,3,2,1,0:T(8,128)} %bitcast.77, bf16[1536,2048]{1,0:T(8,128)(2,1)} %get-tuple-element.49.refs_0_, bf16[2048,1152]{1,0:T(8,128)(2,1)} %get-tuple-element.50.refs_1_, ...), custom_call_target="tpu_custom_call" | custom-call | tf_op jit(solution)/shard_map/reduce_all/pallas_call | solution.py:713
  305.6 1.4 slice.139
  307.0 1.3 slice.138
  308.3 1.9 multiply_reduce_fusion
  310.2 3.8 %fusion.4 = (f32[1,256,1536]{2,1,0:T(8,128)}, bf16[1,256,1536]{2,1,0:T(8,128)(2,1)}) fusion(bf16[1,256,1536]{2,1,0:T(8,128)(2,1)S(1)} %copy-done, bf16[1,256,1536]{2,1,0:T(8,128)(2,1)} %param.12, f32[256]{0:T(256)S(1)} %get-tuple-element.93, f32[1536]{0:T(1024)S(1)} %copy-done.5, f32[256]{0:T(256)S(1)} %get-tuple-element.92, f32[256]{0:T(256)S(1)} %copy-done.9, ...), kind=kLoop, calls=%fused_computation.9 | loop fusion | flops 3932160 | bytes 7087104 | tf_op jit(solution)/shard_map/add | solution.py:1307
  314.0 0.6 fusion.20
  314.7 0.7 copy.44
  315.7 0.9 copy-done.2
  316.7 1.3 multiply_reduce_fusion.1
  318.5 0.8 copy.66
  (85 shorter events, 5.9 us)
Async XLA Ops:
  114.9 1.2 copy-start.8
  117.0 1.0 copy-start.11
  305.5 4.6 %copy-start.10 = (f32[256]{0:T(256)S(1)}, f32[256]{0:T(256)}, u32[]{:S(2)}) copy-start(f32[256]{0:T(256)} %fusion.1) | copy-start | bytes 3076
  305.5 4.6 %copy-start = (bf16[1,256,1536]{2,1,0:T(8,128)(2,1)S(1)}, bf16[1,256,1536]{2,1,0:T(8,128)(2,1)}, u32[]{:S(2)}) copy-start(bf16[1,256,1536]{2,1,0:T(8,128)(2,1)} %param.11) | copy-start | bytes 2359300
  305.6 4.6 %copy-start.1 = (f32[2,128,1536]{2,1,0:T(8,128)S(1)}, f32[2,128,1536]{2,1,0:T(8,128)}, u32[]{:S(2)}) copy-start(f32[2,128,1536]{2,1,0:T(8,128)} %get-tuple-element.52) | copy-start | bytes 4718596
  305.6 4.6 %copy-start.5 = (f32[1536]{0:T(1024)S(1)}, f32[1536]{0:T(1024)}, u32[]{:S(2)}) copy-start(f32[1536]{0:T(1024)} %mul.127) | copy-start | bytes 18436
  305.6 4.6 %copy-start.9 = (f32[256]{0:T(256)S(1)}, f32[256]{0:T(256)}, u32[]{:S(2)}) copy-start(f32[256]{0:T(256)} %dynamic-slice.3) | copy-start | bytes 3076
  310.2 3.8 %copy-start.7 = (f32[8,128]{1,0:T(8,128)S(1)}, f32[8,128]{1,0:T(8,128)}, u32[]{:S(2)}) copy-start(f32[8,128]{1,0:T(8,128)} %get-tuple-element.56) | copy-start | bytes 12292
  310.2 5.2 %copy-start.3 = (bf16[8,48,768]{2,1,0:T(8,128)(2,1)S(1)}, bf16[8,48,768]{2,1,0:T(8,128)(2,1)}, u32[]{:S(2)}) copy-start(bf16[8,48,768]{2,1,0:T(8,128)(2,1)} %get-tuple-element.53) | copy-start | bytes 1769476
  315.6 1.1 copy-start.2
  315.6 1.1 copy-start.6
  315.7 2.3 copy-start.12
  315.7 2.8 copy-start.4

commit v5 on v4

--- a/solution.py
+++ b/solution.py
@@ -299,6 +299,8 @@
     o_line.forward(1)
     for group in range(1, tokens.groups - 1):
         tokens.forward(group)
+    for hop in range(2, planes - 1):
+        o_line.forward(hop)
     for group in range(commons.groups - 1):
         commons.forward(group)
     for hop in range(2, planes - 1):
@@ -308,9 +310,6 @@
     if fused:
         norm_tokens(tok, common, normed, w.shape[2], w_full)
     cots.forward(0)
-    for hop in range(2, planes - 1):
-        o_line.forward(hop)
-    w_line.forward(planes - 1)
     o_line.forward(planes - 1)
 
     def moved(d):
@@ -328,6 +327,7 @@
         def _():
             remote(stage.at[d], wout.at[place], mix_s.at[d], mix_r.at[place], (dp, to)).start()
 
+    w_line.forward(planes - 1)
     if fused:
         project(w, normed, flipped, proj, raw, w_full, flip_out, proj_out, store)
         full = pltpu.make_async_copy(w_full, full_out, local.at[0])
@@ -359,7 +359,7 @@
     halves = (2, length // 2, d)
     total = ranks * length
     rows, cols = w.shape[1:]
-    fused = rows % 16 == 0 and rows * HDIM >= 2 * d and length % 256 == 0 and cols % 384 == 0
+    fused = rows % 16 == 0 and rows * HDIM >= 2 * d and length % 256 == 0 and cols % 768 == 0
     dma = pltpu.SemaphoreType.DMA
     vmem = pl.BlockSpec(memory_space=pltpu.VMEM)
     ring, line = 2 * ranks, 2 * planes
@@ -568,12 +568,32 @@
                     self.copy(way, t).wait_send()
 
 
-def reduce_kernel(fused, s_in, *refs):
+def input_grad(dn, tok, cot, gain):
+    count, d = dn.shape[1:]
+
+    for h in range(dn.shape[0]):
+        def body(i, _):
+            at = pl.ds(pl.multiple_of(i * 16, 16), 16)
+            x = tok[h, at, :].astype(f32)
+            g = gain[...] * dn[h, at, :]
+            inv = lax.rsqrt(jnp.sum(x * x, axis=1, keepdims=True) * (1.0 / d) + epsilon)
+            along = jnp.sum(g * x, axis=1, keepdims=True) * (1.0 / d)
+            dn[h, at, :] = cot[h, at, :].astype(f32) + inv * (g - x * (inv * inv * along))
+            return 0
+
+        lax.fori_loop(0, count // 16, body, 0)
+
+
+def reduce_kernel(fused, s_in, tok_own, cot_own, gain_in, *refs):
     if fused:
         flip_in, dproj_in, wfull_in, *refs = refs
     else:
         dn_in, w_in, c_in, *refs = refs
-    (dn_sum, w_sum, c_sum, s_sum, dn_acc, w_acc, c_acc, s_acc, own,
+    if fused:
+        dn_sum, g_in, s_sum, *refs = refs
+    else:
+        dn_sum, w_sum, c_sum, s_sum, *refs = refs
+    (dn_acc, w_acc, c_acc, s_acc, own,
      dn_land, w_land, c_land, s_land, cz_land, sz_land,
      dn_s, dn_r, cr_s, cr_r, sr_s, sr_r, wz_s, wz_r, cz_s, cz_r, sz_s, sz_r, a2a_s, a2a_r, local, *refs) = refs
     ranks, planes = dn_acc.shape[0], w_acc.shape[0]
@@ -584,7 +604,7 @@
     rows, cols = w_acc.shape[2:]
     tokens = dn_acc.shape[2]
     if fused:
-        flipped, dproj, w_full = refs
+        flipped, dproj, w_full, w_sum, c_sum = refs
         pairs = [(flip_in, flipped), (dproj_in, dproj), (s_in, s_acc), (wfull_in, w_full)]
     else:
         pairs = [(w_in, w_acc), (c_in, c_acc), (s_in, s_acc), (dn_in, dn_acc)]
@@ -666,6 +686,7 @@
     for t in range(2, planes - 1):
         w_fold.push(t)
     dns.total(dn_sum)
+    input_grad(dn_sum, tok_own, cot_own, gain_in)
     for h in range(2):
         for ring in (ss, cs):
             pieces = ring.arrivals(h, 0, 0)
@@ -692,11 +713,18 @@
         pltpu.make_async_copy(ref, ref, a2a_r.at[mask]).wait()
     for mask in range(1, ranks):
         exchange(mask).wait_send()
+    if fused:
+        din = cols // 2
+        for rank in range(ranks):
+            for part in range(2):
+                start = (part * ranks + rank) * din
+                g_in[:, start : start + din] = w_sum[rank, :, part * din : (part + 1) * din].astype(f32)
+        g_in[:, ranks * cols :] = c_sum[:, : g_in.shape[1] - ranks * cols]
     for ring in (dns, cs, ss, w_fold, c_fold, s_fold):
         ring.finish()
 
 
-def reduce_all(fused, ranks, planes, rows, cols, small, *operands):
+def reduce_all(fused, ranks, planes, rows, cols, width, small, tok, cot, gain, *operands):
     if fused:
         flipped, dproj, w_full = operands
         d, length = flipped.shape[0], dproj.shape[0] // ranks
@@ -710,16 +738,14 @@
     dma = pltpu.SemaphoreType.DMA
     vmem = pl.BlockSpec(memory_space=pltpu.VMEM)
     ring, line = 2 * (ranks - 1), 2 * planes
-    results = pl.pallas_call(
+    sums = [((ranks, rows, cols), bf16), ((rows, wide), f32)]
+    dn_sum, *weights, s_sum = pl.pallas_call(
         partial(reduce_kernel, fused),
-        in_specs=[pl.BlockSpec(memory_space=pl.ANY)] * 4,
-        out_specs=[vmem] * 4,
-        out_shape=[
-            jax.ShapeDtypeStruct(part, f32),
-            jax.ShapeDtypeStruct((ranks, rows, cols), bf16),
-            jax.ShapeDtypeStruct((rows, wide), f32),
-            jax.ShapeDtypeStruct(small.shape[3:], f32),
-        ],
+        in_specs=[pl.BlockSpec(memory_space=pl.ANY)] + [vmem] * 3 + [pl.BlockSpec(memory_space=pl.ANY)] * 3,
+        out_specs=[vmem] * (3 if fused else 4),
+        out_shape=[jax.ShapeDtypeStruct(part, f32)]
+        + [jax.ShapeDtypeStruct(*s) for s in ([((rows, width), f32)] if fused else sums)]
+        + [jax.ShapeDtypeStruct(small.shape[3:], f32)],
         scratch_shapes=[
             pltpu.VMEM((ranks,) + part, bf16),
             pltpu.VMEM(wshape, bf16),
@@ -736,14 +762,13 @@
         + [dma((ring,))] * 6
         + [dma((line,))] * 6
         + [dma((ranks,)), dma((ranks,)), dma((4,))]
-        + ([pltpu.VMEM(a.shape, bf16) for a in operands] if fused else []),
+        + ([pltpu.VMEM(a.shape, bf16) for a in operands] + [pltpu.VMEM(*s) for s in sums] if fused else []),
         compiler_params=pltpu.CompilerParams(
             collective_id=1, has_side_effects=True, vmem_limit_bytes=67043328
         ),
         name="reduce_all",
-    )(small, *operands)
-    dn_sum, w_sum, c_sum, s_sum = results
-    return dn_sum.reshape(length, d), w_sum, c_sum, s_sum
+    )(small, tok.reshape(part), cot.reshape(part), gain, *operands)
+    return [dn_sum.reshape(length, d), s_sum] + weights
 
 
 def dot(a, b, dims, precision=None):
@@ -869,8 +894,8 @@
 
 
 def bwd_kernel(
-    total_din,
-    proj_ref, rim_ref, raw_ref, y_ref, dg_ref, sum_ref, state_ref, conv_ref, lane_ref, head_ref, spot_ref,
+    total_din, live,
+    proj_ref, rim_ref, raw_ref, y_ref, dg_ref, sum_ref, state_ref, conv_ref, lane_ref, head_ref,
     out_in, o_in,
     dproj_ref, dconv_ref, dlane_ref, dhead_ref, out_sum, o_sum,
     pad, act, slope, dpad, carry, edge, dact,
@@ -909,6 +934,8 @@
     hide = jnp.where(iota((SUB, SUB), 0) >= iota((SUB, SUB), 1), 0.0, -1e30)
     lower = jnp.where(iota((SUB, SUB), 0) >= iota((SUB, SUB), 1), 1.0, 0.0)
     heads = raw_ref.shape[0]
+    row, lane = iota((heads, LANES), 0), iota((heads, LANES), 1)
+    spot = jnp.where((row < live) & (lane == row + lax.axis_index("seq") * live), 1.0, 0.0).astype(bf16)
     dgain = [jnp.zeros((1, LANES), f32) for _ in range(din // LANES)]
     dskip = [jnp.zeros((1, LANES), f32) for _ in range(din // LANES)]
     for i in reversed(range(block // SUB)):
@@ -979,7 +1006,7 @@
         edge[...] = jnp.broadcast_to(reach[:, 0:1], edge.shape)
         raw = raw_ref[:, rows] + head_ref[1]
         draw = (d_step - head_ref[0] * d_log) * sigmoid(raw)
-        dproj_ref[rows, din + conv :] = dot(draw.astype(bf16), spot_ref[...], TN).astype(bf16)
+        dproj_ref[rows, din + conv :] = dot(draw.astype(bf16), spot, TN).astype(bf16)
         dhead_ref[0] += -chunk.step * d_log
         dhead_ref[1] += draw
     for j in range(din // LANES):
@@ -1097,7 +1124,7 @@
     pl.when(pl.program_id(0) == last)(end)
 
 
-def mixer_backward(ranks, planes, total_din, proj, raw, y, dg, sums, states, conv, lanes, heads, spot, out_part, d_w_out):
+def mixer_backward(ranks, planes, total_din, proj, raw, y, dg, sums, states, conv, lanes, heads, live, out_part, d_w_out):
     length, width = proj.shape
     din, d = y.shape[1], out_part.shape[1]
     cc = conv.shape[1]
@@ -1116,14 +1143,14 @@
     cols = pl.BlockSpec((8, block), lambda t: (0, last - t))
     anywhere = pl.BlockSpec(memory_space=pl.ANY)
     *results, out_sum, o_sum = pl.pallas_call(
-        partial(bwd_kernel, total_din),
+        partial(bwd_kernel, total_din, live),
         grid=(length // block,),
         in_specs=[
             back(block, width),
             pl.BlockSpec((rim, width), lambda t: (jnp.maximum((last - t) * (block // rim) - 1, 0), 0)),
             cols, back(block, din), back(block, din), cols,
             pl.BlockSpec((n, NSTATE, din), lambda t: (last - t, 0, 0)),
-            whole(conv.shape), whole(lanes.shape), whole(heads.shape), whole(spot.shape), anywhere, anywhere,
+            whole(conv.shape), whole(lanes.shape), whole(heads.shape), anywhere, anywhere,
         ],
         out_specs=[
             back(block, width + LANES), whole((8, cc)), whole((8, din)), whole((2, 8, SUB)),
@@ -1156,7 +1183,7 @@
         ),
         name="mix_backward",
     )(
-        proj, proj, raw, y, dg, sums, states, conv, lanes, heads, spot,
+        proj, proj, raw, y, dg, sums, states, conv, lanes, heads,
         out_part.reshape((ranks,) + part), d_w_out,
     )
     return results + [out_sum.reshape(length // ranks, d), o_sum]
@@ -1258,10 +1285,9 @@
     sums = plane_sum(ranks, sums[::4].reshape(8, -1)).reshape(2, -1)
     inverse = lax.rsqrt(sums[0] / din_all + epsilon)[:, None]
     d_w_out = dot((gated * inverse).astype(bf16), cot, TN)[:din].astype(bf16)
-    spot = (jnp.arange(LANES)[None] == me * heads + jnp.arange(8)[:, None]) & (jnp.arange(8)[:, None] < heads)
     d_proj, d_conv, d_lane, d_head, out_sum, grad_out = mixer_backward(
         ranks, planes, din_all, proj, raw, y, dg, jnp.repeat(sums, 4, axis=0), states, conv, lanes, head_rows,
-        spot.astype(bf16), out_part, d_w_out.reshape(planes, -1, d),
+        heads, out_part, d_w_out.reshape(planes, -1, d),
     )
 
     def by_owner(array):
@@ -1297,23 +1323,24 @@
             d_w[:, : 2 * padded].reshape(planes, ranks, rows, -1),
             by_owner(d_w[:, 2 * padded :].reshape(planes * ranks, rows, -1)),
         )
-    d_normed, w_sum, bc_sum, small_sum = reduce_all(
-        fused, ranks, planes, rows, 2 * padded, by_owner(small), *operands
+    grad_x, small_sum, *sums_in = reduce_all(
+        fused, ranks, planes, rows, 2 * padded, width, by_owner(small), tokens[0], cotangent[0],
+        gain_norm[None], *operands,
     )
     block_out = (x_own + mine(inverse, x_own.shape[0]) * out_sum).astype(bf16)
-    gain = gain_norm * d_normed
-    inv = lax.rsqrt(jnp.mean(x_own * x_own, axis=1, keepdims=True) + epsilon)
-    d_xn = inv * (gain - x_own * (inv * inv * jnp.mean(gain * x_own, axis=1, keepdims=True)))
-    grad_x = cotangent[0].astype(f32) + d_xn
-    spread = w_sum.astype(f32).transpose(1, 0, 2)
-    grad_in = jnp.concatenate(
-        [
-            spread[:, :, :din].reshape(rows, din_all),
-            spread[:, :, padded : padded + din].reshape(rows, din_all),
-            bc_sum[:, : 2 * NSTATE + heads * ranks],
-        ],
-        axis=1,
-    )
+    if fused:
+        (grad_in,) = sums_in
+    else:
+        w_sum, bc_sum = sums_in
+        spread = w_sum.astype(f32).transpose(1, 0, 2)
+        grad_in = jnp.concatenate(
+            [
+                spread[:, :, :din].reshape(rows, din_all),
+                spread[:, :, padded : padded + din].reshape(rows, din_all),
+                bc_sum[:, : 2 * NSTATE + heads * ranks],
+            ],
+            axis=1,
+        )
     g_gain = jnp.sum(grad_in * in_weight.astype(f32), axis=1) / norm_gain.astype(f32)
     small_sum = small_sum.reshape(-1)
     g_cw, g_cb, g_gate, head_sums = (small_sum[a:b] for a, b in zip(ends[:-1], ends[1:]))

time: 320 us -> 315 us (0.984)
  other arithmetic: 16.8 us -> 11.1 us
    reduce_sum x2 -> x0, other arithmetic: 3.84 us -> none  [the longest x1 1.94 us: per_device(): inv = lax.rsqrt(jnp.mean(x_own * x_own, axis=1, keepdims=True) + epsilon)]
    add x2 -> x0, other arithmetic: 3.78 us -> none  [the longest x1 3.77 us: per_device(): grad_x = cotangent[0].astype(f32) + d_xn]
where the time goes in v5:
time: 315 us; the launch traced here: 314 us
  Pallas kernels  269 us (85%)
  local copies, waits for them, and re-layouts  26.1 us (8%)
  other arithmetic  11.1 us (4%)
  matrix products  7.01 us (2%)
    pallas_call x1, Pallas kernels, gather_all(): pl.pallas_call(partial(gather_kernel, fused), in_specs=[anywhere] * 5, ou...  95.9 us
    pallas_call x1, Pallas kernels, reduce_all(): pl.pallas_call(partial(reduce_kernel, fused), in_specs=[pl.BlockSpec(memo...  75.4 us
    pallas_call x1, Pallas kernels, mixer_backward(): pl.pallas_call(partial(bwd_kernel, total_din, live), grid=(length // bloc...  58.1 us
    pallas_call x1, Pallas kernels, mixer_forward(): pl.pallas_call(fwd_kernel, grid=(length // block,), in_specs=[rows_spec(b...  30.1 us
    pallas_call x1, Pallas kernels, plane_sum(): pl.pallas_call(plane_sum_kernel, in_specs=[vmem], out_specs=vmem, out_sha...  9.04 us
    dot_general x1, matrix products, dot(): lax.dot_general(a, b, (dims, ((), ())), preferred_element_type=f32, preci...  7.01 us

profile of v5, /device:TPU:0, one launch (start us, length us, event | category | flops | bytes accessed | tf_op | source)
XLA Modules:
  0.0 313.7 jit_solution(6860232950894111056)
XLA Ops:
  0.7 0.7 dynamic_slice.21
  1.4 0.6 pad.49.clone
  2.0 0.7 dynamic-slice_bitcast_fusion
  2.8 0.6 stack_reshape.3
  3.5 0.8 dynamic_update_slice.21
  4.4 0.7 broadcast_in_dim.29.head_ref
  5.0 0.7 slice.106
  5.8 0.7 slice.105
  6.5 0.8 copy.35
  7.4 0.8 fusion.13
  8.3 0.7 fusion.6.common_in
  9.0 1.1 fusion.14
  10.1 0.9 maximum_bitcast_fusion.w_in
  11.0 95.9 %gather_all.1 = (bf16[8,2,128,1536]{3,2,1,0:T(8,128)(2,1)}, bf16[4,96,1536]{2,1,0:T(8,128)(2,1)}, bf16[8,2,2,48,384]{4,3,2,1,0:T(8,128)(2,1)}, f32[64,2048]{1,0:...) custom-call(bf16[2,128,1536]{2,1,0:T(8,128)(2,1)} %bitcast.51, ...), custom_call_target="tpu_custom_call" | custom-call | tf_op jit(solution)/shard_map/gather_all/pallas_call | solution.py:381
  106.9 0.9 constant_dynamic-slice_fusion.1
  107.8 0.6 pad.26.raw_ref
  108.5 1.2 slice_convert_fusion
  110.0 0.7 broadcast_in_dim_reshape.10.gain_in
  110.9 0.6 select_maximum_fusion.lane_ref
  111.8 0.5 reshape_reshape.6
  112.3 0.5 copy.37
  112.9 0.6 pad_maximum_fusion.1.conv_ref
  113.5 30.1 %mix_forward.1 = (f32[2048,384]{1,0:T(8,128)}, f32[2048,384]{1,0:T(8,128)}, bf16[2048,1536]{1,0:T(8,128)(2,1)}, f32[16,128,384]{2,1,0:T(8,128)}, f32[8,2048]{1,0:T(8,128)}, /*index=5*/bf16[2048,384]{1,0:T(8,128)(2,1)}) custom-call(bf16[2048,1024]{1,0:T(8,128)(2,1)} %get-tuple-element.33.proj_ref.rim_ref, f32[8,2048]{1,0:T(8,128)} %pad.26.raw_ref, ...), custom_call_target="tpu_custom_call" | custom-call | tf_op jit(solution)/shard_map/mix_forward/pallas_call | solution.py:1046
  143.7 0.9 slice.112
  144.5 0.6 reshape.142.x_in
  145.1 9.0 %plane_sum.1 = f32[8,512]{1,0:T(8,128)} custom-call(f32[8,512]{1,0:T(8,128)} %reshape.142.x_in), custom_call_target="tpu_custom_call" | custom-call | tf_op jit(solution)/shard_map/plane_sum/pallas_call | solution.py:429
  154.2 0.7 rsqrt_bitcast_fusion
  154.9 0.7 reshape.143
  155.7 7.0 %convolution_convert_fusion = bf16[384,1536]{1,0:T(8,128)(2,1)} fusion(bf16[2048,1536]{1,0:T(8,128)(2,1)} %bitcast.54, bf16[2048,384]{1,0:T(8,128)(2,1)} %get-tuple-element.43, f32[2048]{0:T(1024)S(1)} %bitcast.68), kind=kOutput, calls=%fused_computation.1 | convolution fusion | flops 2418868224 | bytes 9052160 | tf_op jit(solution)/shard_map/dot_general | solution.py:775
  162.7 0.6 dynamic-slice.3
  163.3 0.7 reshape.144.sum_ref
  164.0 58.1 %mix_backward.1 = (bf16[2048,1152]{1,0:T(8,128)(2,1)}, f32[8,640]{1,0:T(8,128)}, f32[8,384]{1,0:T(8,128)}, f32[2,8,128]{2,1,0:T(8,128)}, f32[2,128,1536]{2,1,0:T(8,128)}, /*index=5*/f32[96,1536]{1,0:T(8,128)}) custom-call(bf16[2048,1024]{1,0:T(8,128)(2,1)} %get-tuple-element.33.proj_ref.rim_ref, bf16[2048,1024]{1,0:T(8,128)(2,1)} %get-tuple-element.33.proj_ref.rim_ref, ...), custom_call_target="tpu_custom_call" | custom-call | tf_op jit(solution)/shard_map/mix_backward/pallas_call | solution.py:1145
  222.1 2.8 fusion.1
  225.7 0.8 slice_reduce_fusion
  227.4 0.5 copy.38
  227.9 0.5 reshape.148
  228.6 0.7 copy.48
  229.2 75.4 %reduce_all.1 = (f32[2,128,1536]{2,1,0:T(8,128)}, f32[48,6448]{1,0:T(8,128)}, f32[8,128]{1,0:T(8,128)}) custom-call(f32[8,2,2,8,128]{4,3,2,1,0:T(8,128)} %bitcast.64, bf16[2,128,1536]{2,1,0:T(8,128)(2,1)} %bitcast.52, bf16[2,128,1536]{2,1,0:T(8,128)(2,1)} %bitcast.57, f32[1,1536]{1,0:T(1,128)} %broadcast_in_dim_reshape.10.gain_in, ...), custom_call_target="tpu_custom_call" | custom-call | tf_op jit(solution)/shard_map/reduce_all/pallas_call | solution.py:742
  304.7 1.8 multiply_reduce_fusion
  306.5 0.5 convert_divide_fusion
  307.0 0.6 slice.127
  307.6 0.6 slice.126
  308.2 0.6 fusion.15
  308.9 0.7 copy.40
  309.6 1.1 copy.62
  310.7 0.7 copy-done
  311.4 1.0 copy.63
  312.9 0.8 copy.64
  (69 shorter events, 3.6 us)
Async XLA Ops:
  109.6 1.2 copy-start.6
  111.7 1.0 copy-start.7
  222.1 2.8 copy-start.3
  222.1 3.1 copy-start.4
  304.6 1.8 copy-start.8
  304.6 2.4 copy-start.5
  304.7 4.9 %copy-start.1 = (f32[2,128,1536]{2,1,0:T(8,128)S(1)}, f32[2,128,1536]{2,1,0:T(8,128)}, u32[]{:S(2)}) copy-start(f32[2,128,1536]{2,1,0:T(8,128)} %get-tuple-element.51) | copy-start | bytes 4718596
  309.6 1.9 copy-start
  311.4 1.5 copy-start.2

commit v6 on v5

--- a/solution.py
+++ b/solution.py
@@ -1040,7 +1040,7 @@
     length, width = proj.shape
     din, d = w_out.shape
     cc = conv.shape[1]
-    block = min(TOKENS, length)
+    block = min(2 * TOKENS, length)
     n = block // SUB
     cols = pl.BlockSpec((8, block), lambda t: (0, t))
     return pl.pallas_call(

time: 315 us -> 314 us (level)
  no operation moved by 1% of the time
where the time goes in v6:
time: 314 us; the launch traced here: 313 us
  Pallas kernels  268 us (85%)
  local copies, waits for them, and re-layouts  26.1 us (8%)
  other arithmetic  11.1 us (4%)
  matrix products  7.01 us (2%)
    pallas_call x1, Pallas kernels, gather_all(): pl.pallas_call(partial(gather_kernel, fused), in_specs=[anywhere] * 5, ou...  95.9 us
    pallas_call x1, Pallas kernels, reduce_all(): pl.pallas_call(partial(reduce_kernel, fused), in_specs=[pl.BlockSpec(memo...  75.4 us
    pallas_call x1, Pallas kernels, mixer_backward(): pl.pallas_call(partial(bwd_kernel, total_din, live), grid=(length // bloc...  58.1 us
    pallas_call x1, Pallas kernels, mixer_forward(): pl.pallas_call(fwd_kernel, grid=(length // block,), in_specs=[rows_spec(b...  29.7 us
    pallas_call x1, Pallas kernels, plane_sum(): pl.pallas_call(plane_sum_kernel, in_specs=[vmem], out_specs=vmem, out_sha...  9.05 us
    dot_general x1, matrix products, dot(): lax.dot_general(a, b, (dims, ((), ())), preferred_element_type=f32, preci...  7.01 us

profile of v6, /device:TPU:0, one launch (start us, length us, event | category | flops | bytes accessed | tf_op | source)
XLA Modules:
  0.0 313.3 jit_solution(11949345353261138872)
XLA Ops:
  0.7 0.7 dynamic_slice.21
  1.4 0.6 pad.49.clone
  2.0 0.7 dynamic-slice_bitcast_fusion
  2.8 0.6 stack_reshape.3
  3.5 0.8 dynamic_update_slice.21
  4.4 0.7 broadcast_in_dim.29.head_ref
  5.0 0.7 slice.106
  5.8 0.7 slice.105
  6.5 0.8 copy.35
  7.4 0.8 fusion.13
  8.3 0.7 fusion.6.common_in
  9.0 1.1 fusion.14
  10.1 0.9 maximum_bitcast_fusion.w_in
  11.0 95.9 %gather_all.1 = (bf16[8,2,128,1536]{3,2,1,0:T(8,128)(2,1)}, bf16[4,96,1536]{2,1,0:T(8,128)(2,1)}, bf16[8,2,2,48,384]{4,3,2,1,0:T(8,128)(2,1)}, f32[64,2048]{1,0:...) custom-call(bf16[2,128,1536]{2,1,0:T(8,128)(2,1)} %bitcast.51, ...), custom_call_target="tpu_custom_call" | custom-call | tf_op jit(solution)/shard_map/gather_all/pallas_call | solution.py:381
  106.9 0.9 constant_dynamic-slice_fusion.1
  107.8 0.6 pad.26.raw_ref
  108.5 1.2 slice_convert_fusion
  110.0 0.7 broadcast_in_dim_reshape.10.gain_in
  110.9 0.6 select_maximum_fusion.lane_ref
  111.8 0.5 reshape_reshape.6
  112.3 0.5 copy.37
  112.9 0.6 pad_maximum_fusion.1.conv_ref
  113.5 29.7 %mix_forward.1 = (f32[2048,384]{1,0:T(8,128)}, f32[2048,384]{1,0:T(8,128)}, bf16[2048,1536]{1,0:T(8,128)(2,1)}, f32[16,128,384]{2,1,0:T(8,128)}, f32[8,2048]{1,0:T(8,128)}, /*index=5*/bf16[2048,384]{1,0:T(8,128)(2,1)}) custom-call(bf16[2048,1024]{1,0:T(8,128)(2,1)} %get-tuple-element.33.proj_ref.rim_ref, f32[8,2048]{1,0:T(8,128)} %pad.26.raw_ref, ...), custom_call_target="tpu_custom_call" | custom-call | tf_op jit(solution)/shard_map/mix_forward/pallas_call | solution.py:1046
  143.2 0.9 slice.112
  144.1 0.6 reshape.142.x_in
  144.7 9.0 %plane_sum.1 = f32[8,512]{1,0:T(8,128)} custom-call(f32[8,512]{1,0:T(8,128)} %reshape.142.x_in), custom_call_target="tpu_custom_call" | custom-call | tf_op jit(solution)/shard_map/plane_sum/pallas_call | solution.py:429
  153.8 0.7 rsqrt_bitcast_fusion
  154.5 0.7 reshape.143
  155.3 7.0 %convolution_convert_fusion = bf16[384,1536]{1,0:T(8,128)(2,1)} fusion(bf16[2048,1536]{1,0:T(8,128)(2,1)} %bitcast.54, bf16[2048,384]{1,0:T(8,128)(2,1)} %get-tuple-element.43, f32[2048]{0:T(1024)S(1)} %bitcast.68), kind=kOutput, calls=%fused_computation.1 | convolution fusion | flops 2418868224 | bytes 9052160 | tf_op jit(solution)/shard_map/dot_general | solution.py:775
  162.3 0.6 dynamic-slice.3
  162.9 0.7 reshape.144.sum_ref
  163.6 58.1 %mix_backward.1 = (bf16[2048,1152]{1,0:T(8,128)(2,1)}, f32[8,640]{1,0:T(8,128)}, f32[8,384]{1,0:T(8,128)}, f32[2,8,128]{2,1,0:T(8,128)}, f32[2,128,1536]{2,1,0:T(8,128)}, /*index=5*/f32[96,1536]{1,0:T(8,128)}) custom-call(bf16[2048,1024]{1,0:T(8,128)(2,1)} %get-tuple-element.33.proj_ref.rim_ref, bf16[2048,1024]{1,0:T(8,128)(2,1)} %get-tuple-element.33.proj_ref.rim_ref, ...), custom_call_target="tpu_custom_call" | custom-call | tf_op jit(solution)/shard_map/mix_backward/pallas_call | solution.py:1145
  221.7 2.8 fusion.1
  225.3 0.8 slice_reduce_fusion
  227.0 0.5 copy.38
  227.5 0.5 reshape.148
  228.2 0.7 copy.48
  228.8 75.4 %reduce_all.1 = (f32[2,128,1536]{2,1,0:T(8,128)}, f32[48,6448]{1,0:T(8,128)}, f32[8,128]{1,0:T(8,128)}) custom-call(f32[8,2,2,8,128]{4,3,2,1,0:T(8,128)} %bitcast.64, bf16[2,128,1536]{2,1,0:T(8,128)(2,1)} %bitcast.52, bf16[2,128,1536]{2,1,0:T(8,128)(2,1)} %bitcast.57, f32[1,1536]{1,0:T(1,128)} %broadcast_in_dim_reshape.10.gain_in, ...), custom_call_target="tpu_custom_call" | custom-call | tf_op jit(solution)/shard_map/reduce_all/pallas_call | solution.py:742
  304.2 1.8 multiply_reduce_fusion
  306.0 0.5 convert_divide_fusion
  306.6 0.6 slice.127
  307.2 0.6 slice.126
  307.7 0.6 fusion.15
  308.5 0.7 copy.40
  309.1 1.1 copy.62
  310.3 0.7 copy-done
  311.0 1.0 copy.63
  312.5 0.8 copy.64
  (69 shorter events, 3.6 us)
Async XLA Ops:
  109.6 1.2 copy-start.6
  111.7 1.0 copy-start.7
  221.7 2.8 copy-start.3
  221.7 3.1 copy-start.4
  304.2 1.8 copy-start.8
  304.2 2.4 copy-start.5
  304.2 4.9 %copy-start.1 = (f32[2,128,1536]{2,1,0:T(8,128)S(1)}, f32[2,128,1536]{2,1,0:T(8,128)}, u32[]{:S(2)}) copy-start(f32[2,128,1536]{2,1,0:T(8,128)} %get-tuple-element.51) | copy-start | bytes 4718596
  309.1 1.9 copy-start
  311.0 1.5 copy-start.2
